TPU v7x, 32 devices: a whole 2x2x4 slice. The times are simulated.
32 devices in a mesh: intv: 1, node: 4 (over y, x), row: 8 (over z, core).
Axes of the slice: x: 2, y: 2, z: 4, core: 2. Of those that a mesh axis runs over, the one named last changes fastest.
Arguments:
- inv_factors: float32 [4, 8, 2, 512, 512], P(('intv', 'node'), 'row'), may hold values from -0.48535534 to 0.48535534, as said below
- coupling: float32 [8, 512, 512], P('row'), may hold values from -0.5 to 0.5
- vectors: float32 [8, 512, 64], P('row'), may hold values from -6 to 6
Outputs:
- moments: float32 [8, 512, 256], P(('intv', 'row'), 'node')
- gram: float32 [256, 256], P('intv')
Inputs may be any that keep to these rules, and one draw needn't show every extreme that they name: `inv_factors`: each [j, k] entry holds the real part then the imaginary part of a full 512 x 512 inverse factor.
All inputs are finite; a program needn't handle non-finite values.
Results may differ from a plain program's by a relative error of at most 0.0003.
Values sent between devices are 32-bit elements; how exact they have to be, the bound alone decides.
No kernel may reach another device: no remote copies, remote signals or barrier semaphores. Data moves between devices by JAX's collectives and lax.ppermute only.
A program may use at most 64 MiB of HBM per device.

v0:
```python
import math

import jax
import jax.numpy as jnp
from jax import lax
from jax.sharding import PartitionSpec as P

MOM = 2
PREC = lax.Precision.HIGH


def dot_nt(rows, matrix):
    return lax.dot_general(rows, matrix, (((1,), (1,)), ((), ())), precision=PREC)


def apply_t(matrix, rows):
    n = matrix.shape[1]
    w = rows.shape[0] // 2
    q = dot_nt(rows, matrix)
    return jnp.concatenate([q[:w, :n] - q[w:, n:], q[:w, n:] + q[w:, :n]], axis=0)


def product(left, right):
    n = left.shape[1]
    q_re = jnp.dot(left, right[:n], precision=PREC)
    q_im = jnp.dot(left, right[n:], precision=PREC)
    return jnp.concatenate([q_re[:n] - q_im[n:], q_re[n:] + q_im[:n]], axis=0)


def tree_sum(values):
    while len(values) > 1:
        values = [values[i] + values[i + 1] for i in range(0, len(values), 2)]
    return values[0]


def shards(inv_factors, coupling, vectors):
    n = inv_factors.shape[3]
    width = vectors.shape[2]
    half = width // 2
    rows = lax.axis_size("row")
    nodes = lax.axis_size("node")
    layers = rows // 2
    core = lax.axis_index("row") % 2
    layer = lax.axis_index("row") // 2
    node = lax.axis_index("node")
    first = core == 0

    def swap_core(value):
        return lax.ppermute(value, "row", [(r, r ^ 1) for r in range(rows)])

    def hop(value, source, target):
        return lax.ppermute(value, "row", [(2 * source + c, 2 * target + c) for c in range(2)])

    def exchange_node(value, d):
        return lax.ppermute(value, "node", [(j, j ^ d) for j in range(nodes)])

    def exchange_layer(value, d):
        return lax.ppermute(value, "row", [(r, r ^ (2 * d)) for r in range(rows)])

    factor = inv_factors[0, 0].reshape(2 * n, n)
    couple = coupling[0]
    v_t = vectors[0].T

    q = dot_nt(v_t, factor)
    own_u = jnp.concatenate([q[:, :n], q[:, n:]], axis=0)
    own_c = jnp.dot(own_u, couple, precision=PREC)
    from_a = swap_core(own_c)
    y = jnp.concatenate([v_t + from_a[:width], from_a[width:]], axis=0)
    w_full = jnp.dot(apply_t(factor, y), couple, precision=PREC)
    w_lo = jnp.concatenate([w_full[:half], w_full[width : width + half]], axis=0)
    w_hi = jnp.concatenate([w_full[half:width], w_full[width + half :]], axis=0)
    w_loc = jnp.where(first, swap_core(w_lo), w_hi)

    a_own = jnp.concatenate(
        [
            lax.dot_general(couple, factor[:n], (((0,), (0,)), ((), ())), precision=PREC),
            lax.dot_general(couple, factor[n:], (((0,), (0,)), ((), ())), precision=PREC),
        ],
        axis=0,
    )
    a_other = swap_core(a_own)
    a_a = jnp.where(first, a_own, a_other)
    a_b = jnp.where(first, a_other, a_own)
    p_mat = product(a_b, a_a)
    b_own = jnp.dot(factor, couple, precision=PREC)
    b_other = swap_core(b_own)
    b_a = jnp.where(first, b_own, b_other)
    b_b = jnp.where(first, b_other, b_own)
    q_mat = product(b_a, b_b)
    f_other = swap_core(factor)
    f_a = jnp.where(first, factor, f_other)
    f_b = jnp.where(first, f_other, factor)
    v_other = swap_core(v_t)
    v_a = jnp.where(first, v_t, v_other)
    v_b = jnp.where(first, v_other, v_t)
    zero = jnp.zeros((half, n), jnp.float32)
    va_half = jnp.concatenate([jnp.where(first, v_a[:half], v_a[half:]), zero], axis=0)
    vb_half = jnp.concatenate([jnp.where(first, v_b[:half], v_b[half:]), zero], axis=0)

    carry = jnp.zeros((2 * half, n), jnp.float32)
    leaving = w_loc
    for t in range(layers - 1):
        got = hop(leaving, t, t + 1)
        carry = carry + got
        if t < layers - 2:
            leaving = w_loc + apply_t(p_mat, got)
    y_a = va_half + carry
    u_a = apply_t(f_a, y_a)
    u_b = apply_t(f_b, vb_half + apply_t(a_a, y_a))
    s_loc = u_a + apply_t(b_a, u_b)

    following = jnp.zeros((2 * half, n), jnp.float32)
    leaving = s_loc
    for t in range(layers - 1, 0, -1):
        got = hop(leaving, t, t - 1)
        following = following + got
        if t > 1:
            leaving = s_loc + apply_t(q_mat, got)
    x_a = s_loc + apply_t(q_mat, following)
    x_b = u_b + apply_t(b_b, following)

    keep = jnp.where(first, x_a, x_b)
    recv = swap_core(jnp.where(first, x_b, x_a))
    lo = jnp.where(first, keep, recv)
    hi = jnp.where(first, recv, keep)
    x_own = jnp.concatenate([lo[:half], hi[:half], lo[half:], hi[half:]], axis=0).T

    share = n // nodes
    pieces = [lax.dynamic_slice_in_dim(x_own, (node ^ d) * share, share, 0) for d in range(nodes)]
    blocks = [pieces[0]] + [exchange_node(pieces[d], d) for d in range(1, nodes)]
    parts = []
    for order in range(MOM):
        re_terms, im_terms = [], []
        for d in range(nodes):
            theta = 2.0 * math.pi * ((node ^ d).astype(jnp.float32) + 0.5) / nodes
            w_re = jnp.cos((order + 1) * theta) / nodes
            w_im = jnp.sin((order + 1) * theta) / nodes
            re, im = blocks[d][:, :width], blocks[d][:, width:]
            re_terms.append(w_re * re - w_im * im)
            im_terms.append(w_re * im + w_im * re)
        parts += [tree_sum(re_terms), tree_sum(im_terms)]
    moments = jnp.concatenate(parts, axis=1)
    cols = moments.shape[1]

    gram = lax.dot_general(moments, moments, (((0,), (0,)), ((), ())), precision=PREC)
    hc = cols // 2
    top, bottom = gram[:hc], gram[hc:]
    mine = jnp.where(first, top, bottom) + swap_core(jnp.where(first, bottom, top))
    gs = hc // nodes
    own = [lax.dynamic_slice_in_dim(mine, (node ^ d) * gs, gs, 0) for d in range(nodes)]
    piece = tree_sum([own[0]] + [exchange_node(own[d], d) for d in range(1, nodes)])
    piece = tree_sum([piece] + [exchange_layer(piece, d) for d in range(1, layers)])
    piece = piece * (nodes / (rows * n))
    got = [piece] + [exchange_node(piece, d) for d in range(1, nodes)]
    mine = jnp.zeros((hc, cols), jnp.float32)
    for d in range(nodes):
        mine = lax.dynamic_update_slice_in_dim(mine, got[d], (node ^ d) * gs, 0)
    other = swap_core(mine)
    gram = jnp.concatenate([jnp.where(first, mine, other), jnp.where(first, other, mine)], axis=0)
    return moments[None], gram


def solution(mesh):
    return jax.shard_map(
        shards,
        mesh=mesh,
        in_specs=(
            P(("intv", "node"), "row", None, None, None),
            P("row", None, None),
            P("row", None, None),
        ),
        out_specs=(P(("intv", "row"), "node", None), P("intv", None)),
        check_vma=False,
    )
```

profile of v0, /device:TPU:0, one launch (start us, length us, event | category | flops | bytes accessed | tf_op | source)
XLA Modules:
  0.0 103.6 jit_solution(4573746422861630655)
XLA Ops:
  0.6 0.6 collective-permute-start
  1.3 2.9 %fusion.45 = f32[64,1024]{1,0:T(8,128)S(1)} fusion(f32[1024,512]{1,0:T(8,128)} %bitcast.51, f32[1,512,64]{1,2,0:T(8,128)} %param.5), kind=kOutput, calls=%fused_computation.73 | convolution fusion | flops 201326592 | bytes 2490368 | tf_op jit(solution)/shard_map/dot_general | solution.py:13
  4.2 1.1 %fusion.27 = f32[128,512]{1,0:T(8,128)} fusion(f32[1,512,512]{2,1,0:T(8,128)S(1)} %copy-done, f32[64,512]{1,0:T(8,128)S(1)} %get-tuple-element.51, f32[64,512]{1,0:T(8,128)S(1)} %get-tuple-element.50), kind=kOutput, calls=%fused_computation.34 | convolution fusion | flops 201392128 | bytes 1572864 | tf_op jit(solution)/shard_map/dot_general | solution.py:66
  5.3 0.6 collective-permute-start.1
  5.9 1.0 fusion.17
  7.0 1.0 fusion.19
  8.0 1.6 %pad_maximum_fusion = f32[1024,512]{1,0:T(8,128)} fusion(f32[512,512]{1,0:T(8,128)S(1)} %fusion.17, f32[512,512]{1,0:T(8,128)S(1)} %fusion.19), kind=kLoop, calls=%fused_computation | loop fusion | flops 524288 | bytes 4194304 | tf_op jit(solution)/shard_map/concatenate | solution.py:74
  9.6 3.2 %fusion.21 = f32[1024,512]{1,0:T(8,128)} fusion(f32[1024,512]{1,0:T(8,128)S(1)} %bitcast.52, f32[1,512,512]{2,1,0:T(8,128)S(1)} %copy-done), kind=kOutput, calls=%fused_computation.28 | convolution fusion | flops 1610612736 | bytes 5242880 | tf_op jit(solution)/shard_map/dot_general | solution.py:85
  12.8 0.5 collective-permute-start.8
  13.3 0.9 broadcast_select_fusion.12
  14.3 1.2 %fusion.36 = f32[128,1024]{1,0:T(8,128)S(1)} fusion(f32[1024,512]{1,0:T(8,128)S(1)} %bitcast.53, f32[64,512]{1,0:T(8,128)S(1)} %get-tuple-element.59, f32[64,512]{1,0:T(8,128)S(1)} %get-tuple-element.60), kind=kOutput, calls=%fused_computation.47 | convolution fusion | flops 402718720 | bytes 2883584 | tf_op jit(solution)/shard_map/dot_general | solution.py:13
  15.5 0.4 fusion.25
  16.1 1.4 %collective-permute-done.2 = f32[64,512]{1,0:T(8,128)S(1)} collective-permute-done((f32[64,512]{1,0:T(8,128)S(1)}, f32[64,512]{1,0:T(8,128)S(1)}, u32[]{:S(2)}, u32[]{:S(2)}) %collective-permute-start.2) | collective-permute-done | bytes 131104 | tf_op jit(solution)/shard_map/ppermute | solution.py:49
  17.5 5.0 %collective-permute-start.3 = (f32[64,512]{1,0:T(8,128)S(1)}, f32[64,512]{1,0:T(8,128)S(1)}, u32[]{:S(2)}, u32[]{:S(2)}) collective-permute-start(f32[64,512]{1,0:T(8,128)S(1)} %maximum_select_fusion), channel_id=1, source_target_pairs={{0,2},{1,3},{8,10},{9,11},{16,18},{17,19},{24,26},{25,27}} | collective-permute-start | bytes 393224 | tf_op jit(solution)/shard_map/ppermute | solution.py:52
  22.6 0.5 broadcast_select_fusion.2
  23.1 3.5 %fusion.13 = f32[1024,512]{1,0:T(8,128)S(1)} fusion(f32[1024,512]{1,0:T(8,128)S(1)} %broadcast_select_fusion.2, f32[1024,512]{1,0:T(8,128)} %collective-permute-done.4, pred[]{:T(512)S(6)} %eq.5, f32[512,512]{1,0:T(8,128)S(1)} %copy-done.3, f32[512,512]{1,0:T(8,128)S(1)} %copy-done.5), kind=kOutput, calls=%fused_computation.20 | convolution fusion | flops 1611661312 | bytes 7340033 | tf_op jit(solution)/shard_map/dot_general | solution.py:26
  26.5 3.5 %fusion.15 = f32[1024,512]{1,0:T(8,128)S(1)} fusion(f32[1024,512]{1,0:T(8,128)S(1)} %broadcast_select_fusion.2, f32[1024,512]{1,0:T(8,128)} %collective-permute-done.4, pred[]{:T(512)S(6)} %eq.5, f32[512,512]{1,0:T(8,128)S(1)} %copy-done.3, f32[512,512]{1,0:T(8,128)S(1)} %copy-done.5), kind=kOutput, calls=%fused_computation.22 | convolution fusion | flops 1611661312 | bytes 7340033 | tf_op jit(solution)/shard_map/dot_general | solution.py:25
  30.0 0.5 slice_subtract_fusion.1
  30.5 1.1 %fusion.5 = f32[64,1024]{1,0:T(8,128)S(1)} fusion(f32[64,512]{1,0:T(8,128)S(1)} %collective-permute-done.3, f32[512,512]{1,0:T(8,128)S(1)} %get-tuple-element.11, f32[512,512]{1,0:T(8,128)S(1)} %get-tuple-element.10), kind=kOutput, calls=%fused_computation.8 | convolution fusion | flops 201850880 | bytes 2490368 | tf_op jit(solution)/shard_map/dot_general | solution.py:13
  31.6 0.7 collective-permute-start.5
  32.3 2.8 %broadcast_select_fusion = (f32[1024,512]{1,0:T(8,128)S(1)}, f32[1024,512]{1,0:T(8,128)S(1)}) fusion(f32[1024,512]{1,0:T(8,128)} %collective-permute-done.8, f32[1024,512]{1,0:T(8,128)} %fusion.21, pred[]{:T(512)S(6)} %eq.5), kind=kLoop, calls=%fused_computation.38 | loop fusion | flops 1048576 | bytes 8388609 | tf_op jit(solution)/shard_map/jit(_where)/select_n | solution.py:88
  35.1 1.8 %fusion.9 = f32[1024,512]{1,0:T(8,128)S(1)} fusion(f32[1024,512]{1,0:T(8,128)S(1)} %get-tuple-element.9, f32[1024,512]{1,0:T(8,128)S(1)} %get-tuple-element.8), kind=kOutput, calls=%fused_computation.14 | convolution fusion | flops 1610612736 | bytes 5242880 | tf_op jit(solution)/shard_map/dot_general | solution.py:26
  37.0 1.1 %fusion.4 = f32[64,1024]{1,0:T(8,128)S(1)} fusion(f32[64,512]{1,0:T(8,128)S(1)} %collective-permute-done.5, f32[512,512]{1,0:T(8,128)S(1)} %get-tuple-element.11, f32[512,512]{1,0:T(8,128)S(1)} %get-tuple-element.10), kind=kOutput, calls=%fused_computation.7 | convolution fusion | flops 201850880 | bytes 2490368 | tf_op jit(solution)/shard_map/dot_general | solution.py:13
  38.1 0.9 collective-permute-start.6
  39.0 1.8 %fusion.11 = f32[1024,512]{1,0:T(8,128)S(1)} fusion(f32[1024,512]{1,0:T(8,128)S(1)} %get-tuple-element.9, f32[1024,512]{1,0:T(8,128)S(1)} %get-tuple-element.8), kind=kOutput, calls=%fused_computation.16 | convolution fusion | flops 1610612736 | bytes 5242880 | tf_op jit(solution)/shard_map/dot_general | solution.py:25
  40.9 1.1 %fusion.68 = f32[64,1024]{1,0:T(8,128)S(1)} fusion(f32[64,512]{1,0:T(8,128)S(1)} %add_add_fusion.1, f32[1024,512]{1,0:T(8,128)S(1)} %broadcast_select_fusion.2), kind=kOutput, calls=%fused_computation.147 | convolution fusion | flops 201326592 | bytes 2490368 | tf_op jit(solution)/shard_map/dot_general | solution.py:13
  42.0 1.1 %fusion.2 = f32[64,1024]{1,0:T(8,128)S(1)} fusion(f32[64,512]{1,0:T(8,128)S(1)} %add_add_fusion.1, f32[1024,512]{1,0:T(8,128)S(1)} %bitcast.54, f32[1024,512]{1,0:T(8,128)} %collective-permute-done.7, pred[]{:T(512)S(6)} %eq.5), kind=kOutput, calls=%fused_computation.5 | convolution fusion | flops 201850880 | bytes 4587521 | tf_op jit(solution)/shard_map/dot_general | solution.py:13
  43.1 2.7 %fusion = f32[64,1024]{1,0:T(8,128)S(1)} fusion(f32[1024,512]{1,0:T(8,128)} %collective-permute-done.7, f32[1024,512]{1,0:T(8,128)S(1)} %bitcast.55, pred[]{:T(512)S(6)} %eq.5, f32[32,512]{1,0:T(8,128)S(1)} %get-tuple-element.37, f32[32,512]{1,0:T(8,128)S(1)} %get-tuple-element.36, f32[32,512]{1,0:T(8,128)S(1)} %slice_select_fusion.1), kind=kOutput, calls=%fused_computation.3 | convolution fusion | flops 201916416 | bytes 4653057 | tf_op jit(solution)/shard_map/dot_general | solution.py:13
  45.9 1.1 %fusion.48 = f32[64,1024]{1,0:T(8,128)S(1)} fusion(f32[1024,512]{1,0:T(8,128)S(1)} %get-tuple-element.9, f32[32,512]{1,0:T(8,128)S(1)} %get-tuple-element.33, f32[32,512]{1,0:T(8,128)S(1)} %get-tuple-element.32), kind=kOutput, calls=%fused_computation.80 | convolution fusion | flops 201359360 | bytes 2490368 | tf_op jit(solution)/shard_map/dot_general | solution.py:13
  47.0 0.7 collective-permute-start.9
  47.7 0.5 slice_subtract_fusion
  48.2 1.1 %fusion.8 = f32[64,1024]{1,0:T(8,128)S(1)} fusion(f32[64,512]{1,0:T(8,128)S(1)} %collective-permute-done.9, f32[512,512]{1,0:T(8,128)S(1)} %get-tuple-element.7, f32[512,512]{1,0:T(8,128)S(1)} %get-tuple-element.6), kind=kOutput, calls=%fused_computation.11 | convolution fusion | flops 201850880 | bytes 2490368 | tf_op jit(solution)/shard_map/dot_general | solution.py:13
  49.4 0.7 collective-permute-start.10
  50.1 1.1 %fusion.7 = f32[64,1024]{1,0:T(8,128)S(1)} fusion(f32[64,512]{1,0:T(8,128)S(1)} %collective-permute-done.10, f32[512,512]{1,0:T(8,128)S(1)} %get-tuple-element.7, f32[512,512]{1,0:T(8,128)S(1)} %get-tuple-element.6), kind=kOutput, calls=%fused_computation.10 | convolution fusion | flops 201850880 | bytes 2490368 | tf_op jit(solution)/shard_map/dot_general | solution.py:13
  51.2 1.3 %collective-permute-start.11 = (f32[64,512]{1,0:T(8,128)S(1)}, f32[64,512]{1,0:T(8,128)S(1)}, u32[]{:S(2)}, u32[]{:S(2)}) collective-permute-start(f32[64,512]{1,0:T(8,128)S(1)} %maximum_add_fusion.6), channel_id=1, source_target_pairs={{2,0},{3,1},{10,8},{11,9},{18,16},{19,17},{26,24},{27,25}} | collective-permute-start | bytes 393224 | tf_op jit(solution)/shard_map/ppermute | solution.py:52
  52.5 15.7 %collective-permute-done.11 = f32[64,512]{1,0:T(8,128)S(1)} collective-permute-done((f32[64,512]{1,0:T(8,128)S(1)}, f32[64,512]{1,0:T(8,128)S(1)}, u32[]{:S(2)}, u32[]{:S(2)}) %collective-permute-start.11) | collective-permute-done | bytes 131104 | tf_op jit(solution)/shard_map/ppermute | solution.py:52
  68.3 1.1 %fusion.63 = f32[64,1024]{1,0:T(8,128)S(1)} fusion(f32[1024,512]{1,0:T(8,128)S(1)} %get-tuple-element.8, f32[64,512]{1,0:T(8,128)S(1)} %collective-permute-done.11, f32[64,512]{1,0:T(8,128)S(1)} %collective-permute-done.9, f32[64,512]{1,0:T(8,128)S(1)} %collective-permute-done.10), kind=kOutput, calls=%fused_computation.142 | convolution fusion | flops 201392128 | bytes 2752512 | tf_op jit(solution)/shard_map/dot_general | solution.py:13
  69.4 1.1 %fusion.6 = f32[64,1024]{1,0:T(8,128)S(1)} fusion(f32[512,512]{1,0:T(8,128)S(1)} %get-tuple-element.7, f32[512,512]{1,0:T(8,128)S(1)} %get-tuple-element.6, f32[64,512]{1,0:T(8,128)S(1)} %collective-permute-done.11, f32[64,512]{1,0:T(8,128)S(1)} %collective-permute-done.9, f32[64,512]{1,0:T(8,128)S(1)} %collective-permute-done.10), kind=kOutput, calls=%fused_computation.9 | convolution fusion | flops 201916416 | bytes 2752512 | tf_op jit(solution)/shard_map/dot_general | solution.py:13
  70.7 1.3 %collective-permute-done.12 = f32[64,512]{1,0:T(8,128)S(1)} collective-permute-done((f32[64,512]{1,0:T(8,128)S(1)}, f32[64,512]{1,0:T(8,128)S(1)}, u32[]{:S(2)}, u32[]{:S(2)}) %collective-permute-start.12) | collective-permute-done | bytes 131104 | tf_op jit(solution)/shard_map/ppermute | solution.py:49
  72.2 2.5 %collective-permute-start.15 = (f32[128,128]{0,1:T(8,128)S(1)}, f32[128,128]{0,1:T(8,128)S(1)}, u32[]{:S(2)}, u32[]{:S(2)}) collective-permute-start(f32[128,128]{0,1:T(8,128)S(1)} %get-tuple-element.19), channel_id=1, source_target_pairs={{0,24},{8,16},{16,8},{24,0},{1,25},{9,17},{17,9},{25,1},{2,26},{10... | collective-permute-start | bytes 196616 | tf_op jit(solution)/shard_map/ppermute | solution.py:55
  74.7 0.5 collective-permute-start.14
  75.2 0.5 collective-permute-start.13
  77.0 0.4 collective-permute-done.15
  77.4 1.5 %collective-permute-done.14 = f32[128,128]{0,1:T(8,128)S(1)} collective-permute-done((f32[128,128]{0,1:T(8,128)S(1)}, f32[128,128]{0,1:T(8,128)S(1)}, u32[]{:S(2)}, u32[]{:S(2)}) %collective-permute-start.14) | collective-permute-done | bytes 65568 | tf_op jit(solution)/shard_map/ppermute | solution.py:55
  79.0 0.5 collective-permute-done.13
  80.0 1.3 %collective-permute-done.16 = f32[128,256]{1,0:T(8,128)S(1)} collective-permute-done((f32[128,256]{1,0:T(8,128)S(1)}, f32[128,256]{1,0:T(8,128)S(1)}, u32[]{:S(2)}, u32[]{:S(2)}) %collective-permute-start.16) | collective-permute-done | bytes 131104 | tf_op jit(solution)/shard_map/ppermute | solution.py:49
  81.4 1.6 %collective-permute-start.18 = (f32[32,256]{1,0:T(8,128)S(1)}, f32[32,256]{1,0:T(8,128)S(1)}, u32[]{:S(2)}, u32[]{:S(2)}) collective-permute-start(f32[32,256]{1,0:T(8,128)S(1)} %get-tuple-element.54), channel_id=1, source_target_pairs={{0,16},{8,24},{16,0},{24,8},{1,17},{9,25},{17,1},{25,9},{2,18},{10... | collective-permute-start | bytes 98312 | tf_op jit(solution)/shard_map/ppermute | solution.py:55
  83.0 0.7 collective-permute-start.19
  83.7 1.3 %collective-permute-start.17 = (f32[32,256]{1,0:T(8,128)S(1)}, f32[32,256]{1,0:T(8,128)S(1)}, u32[]{:S(2)}, u32[]{:S(2)}) collective-permute-start(f32[32,256]{1,0:T(8,128)S(1)} %get-tuple-element.52), channel_id=1, source_target_pairs={{0,8},{8,0},{16,24},{24,16},{1,9},{9,1},{17,25},{25,17},{2,10},{10... | collective-permute-start | bytes 98312 | tf_op jit(solution)/shard_map/ppermute | solution.py:55
  85.0 0.4 collective-permute-done.18
  85.4 2.4 %collective-permute-done.19 = f32[32,256]{1,0:T(8,128)S(1)} collective-permute-done((f32[32,256]{1,0:T(8,128)S(1)}, f32[32,256]{1,0:T(8,128)S(1)}, u32[]{:S(2)}, u32[]{:S(2)}) %collective-permute-start.19) | collective-permute-done | bytes 32800 | tf_op jit(solution)/shard_map/ppermute | solution.py:55
  87.9 1.9 %collective-permute-start.22 = (f32[32,256]{1,0:T(8,128)S(1)}, f32[32,256]{1,0:T(8,128)S(1)}, u32[]{:S(2)}, u32[]{:S(2)}) collective-permute-start(f32[32,256]{1,0:T(8,128)S(1)} %add_add_fusion.2), channel_id=1, source_target_pairs={{0,6},{1,7},{2,4},{3,5},{4,2},{5,3},{6,0},{7,1},{8,14},{9,15},{10,... | collective-permute-start | bytes 98312 | tf_op jit(solution)/shard_map/ppermute | solution.py:58
  89.8 1.6 %collective-permute-start.20 = (f32[32,256]{1,0:T(8,128)S(1)}, f32[32,256]{1,0:T(8,128)S(1)}, u32[]{:S(2)}, u32[]{:S(2)}) collective-permute-start(f32[32,256]{1,0:T(8,128)S(1)} %add_add_fusion.2), channel_id=1, source_target_pairs={{0,2},{1,3},{2,0},{3,1},{4,6},{5,7},{6,4},{7,5},{8,10},{9,11},{10,... | collective-permute-start | bytes 98312 | tf_op jit(solution)/shard_map/ppermute | solution.py:58
  91.4 1.3 %collective-permute-done.21 = f32[32,256]{1,0:T(8,128)S(1)} collective-permute-done((f32[32,256]{1,0:T(8,128)S(1)}, f32[32,256]{1,0:T(8,128)S(1)}, u32[]{:S(2)}, u32[]{:S(2)}) %collective-permute-start.21) | collective-permute-done | bytes 32800 | tf_op jit(solution)/shard_map/ppermute | solution.py:58
  92.7 1.0 collective-permute-done.22
  94.1 1.1 %collective-permute-start.23 = (f32[32,256]{1,0:T(8,128)S(1)}, f32[32,256]{1,0:T(8,128)S(1)}, u32[]{:S(2)}, u32[]{:S(2)}) collective-permute-start(f32[32,256]{1,0:T(8,128)S(1)} %get-tuple-element.5), channel_id=1, source_target_pairs={{0,8},{8,0},{16,24},{24,16},{1,9},{9,1},{17,25},{25,17},{2,10},{10... | collective-permute-start | bytes 98312 | tf_op jit(solution)/shard_map/ppermute | solution.py:55
  95.2 1.5 %collective-permute-start.24 = (f32[32,256]{1,0:T(8,128)S(1)}, f32[32,256]{1,0:T(8,128)S(1)}, u32[]{:S(2)}, u32[]{:S(2)}) collective-permute-start(f32[32,256]{1,0:T(8,128)S(1)} %get-tuple-element.5), channel_id=1, source_target_pairs={{0,16},{8,24},{16,0},{24,8},{1,17},{9,25},{17,1},{25,9},{2,18},{10... | collective-permute-start | bytes 98312 | tf_op jit(solution)/shard_map/ppermute | solution.py:55
  96.7 0.9 collective-permute-start.25
  97.6 0.4 collective-permute-done.23
  98.0 1.1 %collective-permute-done.24 = f32[32,256]{1,0:T(8,128)S(1)} collective-permute-done((f32[32,256]{1,0:T(8,128)S(1)}, f32[32,256]{1,0:T(8,128)S(1)}, u32[]{:S(2)}, u32[]{:S(2)}) %collective-permute-start.24) | collective-permute-done | bytes 32800 | tf_op jit(solution)/shard_map/ppermute | solution.py:55
  99.1 2.4 %collective-permute-done.25 = f32[32,256]{1,0:T(8,128)S(1)} collective-permute-done((f32[32,256]{1,0:T(8,128)S(1)}, f32[32,256]{1,0:T(8,128)S(1)}, u32[]{:S(2)}, u32[]{:S(2)}) %collective-permute-start.25) | collective-permute-done | bytes 32800 | tf_op jit(solution)/shard_map/ppermute | solution.py:55
  101.6 0.8 copy.5
  102.3 0.6 collective-permute-done.26
  102.9 0.7 pad_maximum_fusion.9
  (77 shorter events, 1.9 us)
Async XLA Ops:
  0.6 3.6 %copy-start = (f32[1,512,512]{2,1,0:T(8,128)S(1)}, f32[1,512,512]{2,1,0:T(8,128)}, u32[]{:S(2)}) copy-start(f32[1,512,512]{2,1,0:T(8,128)} %param.4) | copy-start | bytes 3145732
  0.6 12.7 %collective-permute-start = (f32[64,512]{1,0:T(8,128)}, f32[64,512]{1,0:T(8,128)}, u32[]{:S(2)}, u32[]{:S(2)}) collective-permute-start(f32[64,512]{1,0:T(8,128)} %bitcast.56), channel_id=1, source_target_pairs={{0,1},{1,0},{2,3},{3,2},{4,5},{5,4},{6,7},{7,6},{8,9},{9,8},{10,11... | collective-permute-start | bytes 393224 | tf_op jit(solution)/shard_map/ppermute | solution.py:49
  1.2 4.7 %copy-start.1 = (f32[1,1,2,512,512]{4,3,2,1,0:T(8,128)S(1)}, f32[1,1,2,512,512]{4,3,2,1,0:T(8,128)}, u32[]{:S(2)}) copy-start(f32[1,1,2,512,512]{4,3,2,1,0:T(8,128)} %param.3) | copy-start | bytes 6291460
  1.2 40.8 %collective-permute-start.7 = (f32[1024,512]{1,0:T(8,128)}, f32[1024,512]{1,0:T(8,128)}, u32[]{:S(2)}, u32[]{:S(2)}) collective-permute-start(f32[1024,512]{1,0:T(8,128)} %bitcast.50), channel_id=1, source_target_pairs={{0,1},{1,0},{2,3},{3,2},{4,5},{5,4},{6,7},{7,6},{8,9},{9,8},{10,11... | collective-permute-start | bytes 6291464 | tf_op jit(solution)/shard_map/ppermute | solution.py:49
  5.3 8.0 %collective-permute-start.1 = (f32[128,512]{1,0:T(8,128)}, f32[128,512]{1,0:T(8,128)S(1)}, u32[]{:S(2)}, u32[]{:S(2)}) collective-permute-start(f32[128,512]{1,0:T(8,128)} %fusion.27), channel_id=1, source_target_pairs={{0,1},{1,0},{2,3},{3,2},{4,5},{5,4},{6,7},{7,6},{8,9},{9,8},{10,11... | collective-permute-start | bytes 786440 | tf_op jit(solution)/shard_map/ppermute | solution.py:49
  6.9 2.7 %copy-start.2 = (f32[512,512]{1,0:T(8,128)}, f32[512,512]{1,0:T(8,128)S(1)}, u32[]{:S(2)}) copy-start(f32[512,512]{1,0:T(8,128)S(1)} %fusion.17) | copy-start | bytes 3145732
  8.0 4.8 %copy-start.4 = (f32[512,512]{1,0:T(8,128)}, f32[512,512]{1,0:T(8,128)S(1)}, u32[]{:S(2)}) copy-start(f32[512,512]{1,0:T(8,128)S(1)} %fusion.19) | copy-start | bytes 3145732
  9.6 3.7 %copy-start.6 = (f32[1,512,64]{1,2,0:T(8,128)S(1)}, f32[1,512,64]{1,2,0:T(8,128)}, u32[]{:S(2)}) copy-start(f32[1,512,64]{1,2,0:T(8,128)} %param.5) | copy-start | bytes 393220
  9.6 12.9 %collective-permute-start.4 = (f32[1024,512]{1,0:T(8,128)}, f32[1024,512]{1,0:T(8,128)}, u32[]{:S(2)}, u32[]{:S(2)}) collective-permute-start(f32[1024,512]{1,0:T(8,128)} %pad_maximum_fusion), channel_id=1, source_target_pairs={{0,1},{1,0},{2,3},{3,2},{4,5},{5,4},{6,7},{7,6},{8,9},{9,8},{10,11... | collective-permute-start | bytes 6291464 | tf_op jit(solution)/shard_map/ppermute | solution.py:49
  12.8 19.5 %collective-permute-start.8 = (f32[1024,512]{1,0:T(8,128)}, f32[1024,512]{1,0:T(8,128)}, u32[]{:S(2)}, u32[]{:S(2)}) collective-permute-start(f32[1024,512]{1,0:T(8,128)} %fusion.21), channel_id=1, source_target_pairs={{0,1},{1,0},{2,3},{3,2},{4,5},{5,4},{6,7},{7,6},{8,9},{9,8},{10,11... | collective-permute-start | bytes 6291464 | tf_op jit(solution)/shard_map/ppermute | solution.py:49
  15.5 7.1 %copy-start.3 = (f32[512,512]{1,0:T(8,128)S(1)}, f32[512,512]{1,0:T(8,128)}, u32[]{:S(2)}) copy-start(f32[512,512]{1,0:T(8,128)} %copy-done.2) | copy-start | bytes 3145732
  15.5 7.1 %copy-start.5 = (f32[512,512]{1,0:T(8,128)S(1)}, f32[512,512]{1,0:T(8,128)}, u32[]{:S(2)}) copy-start(f32[512,512]{1,0:T(8,128)} %copy-done.4) | copy-start | bytes 3145732
  16.0 1.5 %collective-permute-start.2 = (f32[64,512]{1,0:T(8,128)S(1)}, f32[64,512]{1,0:T(8,128)S(1)}, u32[]{:S(2)}, u32[]{:S(2)}) collective-permute-start(f32[64,512]{1,0:T(8,128)S(1)} %pad_maximum_fusion.10), channel_id=1, source_target_pairs={{0,1},{1,0},{2,3},{3,2},{4,5},{5,4},{6,7},{7,6},{8,9},{9,8},{10,11... | collective-permute-start | bytes 393224 | tf_op jit(solution)/shard_map/ppermute | solution.py:49
  17.5 13.0 %collective-permute-start.3 = (f32[64,512]{1,0:T(8,128)S(1)}, f32[64,512]{1,0:T(8,128)S(1)}, u32[]{:S(2)}, u32[]{:S(2)}) collective-permute-start(f32[64,512]{1,0:T(8,128)S(1)} %maximum_select_fusion), channel_id=1, source_target_pairs={{0,2},{1,3},{8,10},{9,11},{16,18},{17,19},{24,26},{25,27}} | collective-permute-start | bytes 393224 | tf_op jit(solution)/shard_map/ppermute | solution.py:52
  31.6 5.3 %collective-permute-start.5 = (f32[64,512]{1,0:T(8,128)S(1)}, f32[64,512]{1,0:T(8,128)S(1)}, u32[]{:S(2)}, u32[]{:S(2)}) collective-permute-start(f32[64,512]{1,0:T(8,128)S(1)} %maximum_add_fusion), channel_id=1, source_target_pairs={{2,4},{3,5},{10,12},{11,13},{18,20},{19,21},{26,28},{27,29}} | collective-permute-start | bytes 393224 | tf_op jit(solution)/shard_map/ppermute | solution.py:52
  38.1 2.7 %collective-permute-start.6 = (f32[64,512]{1,0:T(8,128)S(1)}, f32[64,512]{1,0:T(8,128)S(1)}, u32[]{:S(2)}, u32[]{:S(2)}) collective-permute-start(f32[64,512]{1,0:T(8,128)S(1)} %maximum_add_fusion.1), channel_id=1, source_target_pairs={{4,6},{5,7},{12,14},{13,15},{20,22},{21,23},{28,30},{29,31}} | collective-permute-start | bytes 393224 | tf_op jit(solution)/shard_map/ppermute | solution.py:52
  47.0 1.2 %collective-permute-start.9 = (f32[64,512]{1,0:T(8,128)S(1)}, f32[64,512]{1,0:T(8,128)S(1)}, u32[]{:S(2)}, u32[]{:S(2)}) collective-permute-start(f32[64,512]{1,0:T(8,128)S(1)} %maximum_add_fusion.2), channel_id=1, source_target_pairs={{6,4},{7,5},{14,12},{15,13},{22,20},{23,21},{30,28},{31,29}} | collective-permute-start | bytes 393224 | tf_op jit(solution)/shard_map/ppermute | solution.py:52
  49.4 0.7 collective-permute-start.10
  51.2 17.0 %collective-permute-start.11 = (f32[64,512]{1,0:T(8,128)S(1)}, f32[64,512]{1,0:T(8,128)S(1)}, u32[]{:S(2)}, u32[]{:S(2)}) collective-permute-start(f32[64,512]{1,0:T(8,128)S(1)} %maximum_add_fusion.6), channel_id=1, source_target_pairs={{2,0},{3,1},{10,8},{11,9},{18,16},{19,17},{26,24},{27,25}} | collective-permute-start | bytes 393224 | tf_op jit(solution)/shard_map/ppermute | solution.py:52
  70.6 1.4 %collective-permute-start.12 = (f32[64,512]{1,0:T(8,128)S(1)}, f32[64,512]{1,0:T(8,128)S(1)}, u32[]{:S(2)}, u32[]{:S(2)}) collective-permute-start(f32[64,512]{1,0:T(8,128)S(1)} %broadcast_select_fusion.10), channel_id=1, source_target_pairs={{0,1},{1,0},{2,3},{3,2},{4,5},{5,4},{6,7},{7,6},{8,9},{9,8},{10,11... | collective-permute-start | bytes 393224 | tf_op jit(solution)/shard_map/ppermute | solution.py:49
  72.2 5.3 %collective-permute-start.15 = (f32[128,128]{0,1:T(8,128)S(1)}, f32[128,128]{0,1:T(8,128)S(1)}, u32[]{:S(2)}, u32[]{:S(2)}) collective-permute-start(f32[128,128]{0,1:T(8,128)S(1)} %get-tuple-element.19), channel_id=1, source_target_pairs={{0,24},{8,16},{16,8},{24,0},{1,25},{9,17},{17,9},{25,1},{2,26},{10... | collective-permute-start | bytes 196616 | tf_op jit(solution)/shard_map/ppermute | solution.py:55
  74.7 4.3 %collective-permute-start.14 = (f32[128,128]{0,1:T(8,128)S(1)}, f32[128,128]{0,1:T(8,128)S(1)}, u32[]{:S(2)}, u32[]{:S(2)}) collective-permute-start(f32[128,128]{0,1:T(8,128)S(1)} %get-tuple-element.20), channel_id=1, source_target_pairs={{0,16},{8,24},{16,0},{24,8},{1,17},{9,25},{17,1},{25,9},{2,18},{10... | collective-permute-start | bytes 196616 | tf_op jit(solution)/shard_map/ppermute | solution.py:55
  75.2 4.3 %collective-permute-start.13 = (f32[128,128]{0,1:T(8,128)S(1)}, f32[128,128]{0,1:T(8,128)S(1)}, u32[]{:S(2)}, u32[]{:S(2)}) collective-permute-start(f32[128,128]{0,1:T(8,128)S(1)} %get-tuple-element.21), channel_id=1, source_target_pairs={{0,8},{8,0},{16,24},{24,16},{1,9},{9,1},{17,25},{25,17},{2,10},{10... | collective-permute-start | bytes 196616 | tf_op jit(solution)/shard_map/ppermute | solution.py:55
  79.9 1.4 %collective-permute-start.16 = (f32[128,256]{1,0:T(8,128)S(1)}, f32[128,256]{1,0:T(8,128)S(1)}, u32[]{:S(2)}, u32[]{:S(2)}) collective-permute-start(f32[128,256]{1,0:T(8,128)S(1)} %slice_select_fusion), channel_id=1, source_target_pairs={{0,1},{1,0},{2,3},{3,2},{4,5},{5,4},{6,7},{7,6},{8,9},{9,8},{10,11... | collective-permute-start | bytes 393224 | tf_op jit(solution)/shard_map/ppermute | solution.py:49
  81.4 4.0 %collective-permute-start.18 = (f32[32,256]{1,0:T(8,128)S(1)}, f32[32,256]{1,0:T(8,128)S(1)}, u32[]{:S(2)}, u32[]{:S(2)}) collective-permute-start(f32[32,256]{1,0:T(8,128)S(1)} %get-tuple-element.54), channel_id=1, source_target_pairs={{0,16},{8,24},{16,0},{24,8},{1,17},{9,25},{17,1},{25,9},{2,18},{10... | collective-permute-start | bytes 98312 | tf_op jit(solution)/shard_map/ppermute | solution.py:55
  83.0 4.8 %collective-permute-start.19 = (f32[32,256]{1,0:T(8,128)S(1)}, f32[32,256]{1,0:T(8,128)S(1)}, u32[]{:S(2)}, u32[]{:S(2)}) collective-permute-start(f32[32,256]{1,0:T(8,128)S(1)} %get-tuple-element.53), channel_id=1, source_target_pairs={{0,24},{8,16},{16,8},{24,0},{1,25},{9,17},{17,9},{25,1},{2,26},{10... | collective-permute-start | bytes 98312 | tf_op jit(solution)/shard_map/ppermute | solution.py:55
  83.7 4.1 %collective-permute-start.17 = (f32[32,256]{1,0:T(8,128)S(1)}, f32[32,256]{1,0:T(8,128)S(1)}, u32[]{:S(2)}, u32[]{:S(2)}) collective-permute-start(f32[32,256]{1,0:T(8,128)S(1)} %get-tuple-element.52), channel_id=1, source_target_pairs={{0,8},{8,0},{16,24},{24,16},{1,9},{9,1},{17,25},{25,17},{2,10},{10... | collective-permute-start | bytes 98312 | tf_op jit(solution)/shard_map/ppermute | solution.py:55
  87.8 4.9 %collective-permute-start.21 = (f32[32,256]{1,0:T(8,128)S(1)}, f32[32,256]{1,0:T(8,128)S(1)}, u32[]{:S(2)}, u32[]{:S(2)}) collective-permute-start(f32[32,256]{1,0:T(8,128)S(1)} %add_add_fusion.2), channel_id=1, source_target_pairs={{0,4},{1,5},{2,6},{3,7},{4,0},{5,1},{6,2},{7,3},{8,12},{9,13},{10,... | collective-permute-start | bytes 98312 | tf_op jit(solution)/shard_map/ppermute | solution.py:58
  87.9 5.8 %collective-permute-start.22 = (f32[32,256]{1,0:T(8,128)S(1)}, f32[32,256]{1,0:T(8,128)S(1)}, u32[]{:S(2)}, u32[]{:S(2)}) collective-permute-start(f32[32,256]{1,0:T(8,128)S(1)} %add_add_fusion.2), channel_id=1, source_target_pairs={{0,6},{1,7},{2,4},{3,5},{4,2},{5,3},{6,0},{7,1},{8,14},{9,15},{10,... | collective-permute-start | bytes 98312 | tf_op jit(solution)/shard_map/ppermute | solution.py:58
  89.8 4.2 %collective-permute-start.20 = (f32[32,256]{1,0:T(8,128)S(1)}, f32[32,256]{1,0:T(8,128)S(1)}, u32[]{:S(2)}, u32[]{:S(2)}) collective-permute-start(f32[32,256]{1,0:T(8,128)S(1)} %add_add_fusion.2), channel_id=1, source_target_pairs={{0,2},{1,3},{2,0},{3,1},{4,6},{5,7},{6,4},{7,5},{8,10},{9,11},{10,... | collective-permute-start | bytes 98312 | tf_op jit(solution)/shard_map/ppermute | solution.py:58
  94.1 4.0 %collective-permute-start.23 = (f32[32,256]{1,0:T(8,128)S(1)}, f32[32,256]{1,0:T(8,128)S(1)}, u32[]{:S(2)}, u32[]{:S(2)}) collective-permute-start(f32[32,256]{1,0:T(8,128)S(1)} %get-tuple-element.5), channel_id=1, source_target_pairs={{0,8},{8,0},{16,24},{24,16},{1,9},{9,1},{17,25},{25,17},{2,10},{10... | collective-permute-start | bytes 98312 | tf_op jit(solution)/shard_map/ppermute | solution.py:55
  95.2 3.9 %collective-permute-start.24 = (f32[32,256]{1,0:T(8,128)S(1)}, f32[32,256]{1,0:T(8,128)S(1)}, u32[]{:S(2)}, u32[]{:S(2)}) collective-permute-start(f32[32,256]{1,0:T(8,128)S(1)} %get-tuple-element.5), channel_id=1, source_target_pairs={{0,16},{8,24},{16,0},{24,8},{1,17},{9,25},{17,1},{25,9},{2,18},{10... | collective-permute-start | bytes 98312 | tf_op jit(solution)/shard_map/ppermute | solution.py:55
  96.7 4.8 %collective-permute-start.25 = (f32[32,256]{1,0:T(8,128)S(1)}, f32[32,256]{1,0:T(8,128)S(1)}, u32[]{:S(2)}, u32[]{:S(2)}) collective-permute-start(f32[32,256]{1,0:T(8,128)S(1)} %get-tuple-element.5), channel_id=1, source_target_pairs={{0,24},{8,16},{16,8},{24,0},{1,25},{9,17},{17,9},{25,1},{2,26},{10... | collective-permute-start | bytes 98312 | tf_op jit(solution)/shard_map/ppermute | solution.py:55
  101.5 1.3 %collective-permute-start.26 = (f32[128,256]{1,0:T(8,128)S(1)}, f32[128,256]{1,0:T(8,128)S(1)}, u32[]{:S(2)}, u32[]{:S(2)}) collective-permute-start(f32[128,256]{1,0:T(8,128)S(1)} %constant_dynamic-update-slice_fusion), channel_id=1, source_target_pairs={{0,1},{1,0},{2,3},{3,2},{4,5},{5,4},{6,7},{7,6},{8,9},{9,8},{10,11... | collective-permute-start | bytes 393224 | tf_op jit(solution)/shard_map/ppermute | solution.py:49
where the time goes:
time: 104 us
  matrix products  34.3 us (33%)
  waiting for transfers between devices  32.2 us (31%)
  starting transfers between devices  25.4 us (24%)
  other arithmetic  8.26 us (8%)
  between operations  2.53 us (2%)
    dot_general x12, matrix products, dot_nt(): lax.dot_general(rows, matrix, (((1,), (1,)), ((), ())), precision=PREC)  16.7 us
    ppermute x6, waiting for transfers between devices, hop(): lax.ppermute(value, 'row', [(2 * source + c, 2 * target + c) for c in ran...  15.7 us
    ppermute x9, starting transfers between devices, exchange_node(): return lax.ppermute(value, 'node', [(j, j ^ d) for j in range(nodes)])  10.7 us
    ppermute x9, waiting for transfers between devices, exchange_node(): return lax.ppermute(value, 'node', [(j, j ^ d) for j in range(nodes)])  9.23 us
    ppermute x6, starting transfers between devices, hop(): lax.ppermute(value, 'row', [(2 * source + c, 2 * target + c) for c in ran...  9.22 us
    dot_general x2, matrix products, product(): q_im = jnp.dot(left, right[n:], precision=PREC)  5.27 us
    dot_general x2, matrix products, product(): q_re = jnp.dot(left, right[:n], precision=PREC)  5.27 us
    ppermute x9, waiting for transfers between devices, swap_core(): return lax.ppermute(value, 'row', [(r, r ^ 1) for r in range(rows)])  4.56 us
  transfers between devices with their start and end apart: 27, of which 16 were waited for; matrix products, arithmetic and copies ran while one was open for 31% of the time, Pallas kernels for 0%

commit v1 on v0

v1 whole, which is shorter than its diff:
```python
import functools
import functools
import math

import jax
import jax.numpy as jnp
from jax import lax
from jax.experimental import pallas as pl
from jax.experimental.pallas import tpu as pltpu
from jax.sharding import PartitionSpec as P


MOM = 2
PREC = lax.Precision.HIGH
F32, BF16 = jnp.float32, jnp.bfloat16
NN = (((1,), (0,)), ((), ()))
NT = (((1,), (1,)), ((), ()))
VMEM = pl.BlockSpec(memory_space=pltpu.VMEM)
HBM = pl.BlockSpec(memory_space=pltpu.HBM)
CHUNKS = 4


def parts_of(x):
    high = x.astype(BF16)
    return high, (x - high.astype(F32)).astype(BF16)


def times(rows, matrix, dims):
    w = rows.shape[0]
    high, low = parts_of(rows)
    both = lax.dot_general(
        jnp.concatenate([high, low], axis=0), matrix[0], dims, preferred_element_type=F32
    )
    rest = lax.dot_general(high, matrix[1], dims, preferred_element_type=F32)
    return both[:w] + (both[w:] + rest)


def apply_to(rows, matrix):
    w, n = rows.shape[0] // 2, rows.shape[1]
    q = times(rows, matrix, NT)
    return jnp.concatenate([q[:w, :n] - q[w:, n:], q[:w, n:] + q[w:, :n]], axis=0)


def add_real(block, real):
    w = real.shape[0]
    return jnp.concatenate([block[:w] + real, block[w:]], axis=0)


def read(pair):
    return pair[0][...], pair[1][...]


def block_of(pair, role):
    return pair[0][role], pair[1][role]


def write(pair, value):
    high, low = parts_of(value)
    pair[0][...] = high
    pair[1][...] = low


def call(kernel, outs, *operands):
    return pl.pallas_call(
        kernel,
        out_shape=tuple(pltpu.VMEM(shape, dtype) for shape, dtype in outs),
        in_specs=[VMEM] * len(operands),
        out_specs=tuple([VMEM] * len(outs)),
        compiler_params=pltpu.CompilerParams(vmem_limit_bytes=20 << 20),
    )(*[pltpu.with_memory_space_constraint(x, pltpu.VMEM) for x in operands])


def enter_kernel(f_any, c_any, v_any, fh, fl, ch, cl, vt, g, f_buf, c_buf, v_buf, sems):
    n = c_buf.shape[0]
    rows = f_buf.shape[0] // CHUNKS
    v_copy = pltpu.make_async_copy(v_any, v_buf, sems.at[CHUNKS])
    v_copy.start()
    copies = []
    for i in range(CHUNKS):
        part = pl.ds(i * rows, rows)
        copies.append(pltpu.make_async_copy(f_any.at[part], f_buf.at[part], sems.at[i]))
        copies[-1].start()
    c_copy = pltpu.make_async_copy(c_any, c_buf, sems.at[CHUNKS + 1])
    c_copy.start()
    v_copy.wait()
    real = v_buf[...]
    vt[...] = real
    pieces = []
    for i in range(CHUNKS):
        part = pl.ds(i * rows, rows)
        copies[i].wait()
        high, low = parts_of(f_buf[part, :])
        fh[part, :] = high
        fl[part, :] = low
        pieces.append(times(real, (high, low), NT))
    q = jnp.concatenate(pieces, axis=1)
    u = jnp.concatenate([q[:, :n], q[:, n:]], axis=0)
    c_copy.wait()
    write((ch, cl), c_buf[...])
    g[...] = times(u, read((ch, cl)), NN)


def leave_kernel(vt, g, fh, fl, ch, cl, lo, hi):
    y = add_real(g[...], vt[...])
    w = times(apply_to(y, read((fh, fl))), read((ch, cl)), NN)
    half = lo.shape[0] // 2
    width = 2 * half
    lo[...] = jnp.concatenate([w[:half], w[width : width + half]], axis=0)
    hi[...] = jnp.concatenate([w[half:width], w[width + half :]], axis=0)


def pair_product(left, right, dims):
    return lax.dot_general(left[0], right[0], dims, preferred_element_type=F32) + (
        lax.dot_general(left[0], right[1], dims, preferred_element_type=F32)
        + lax.dot_general(left[1], right[0], dims, preferred_element_type=F32)
    )


def product_kernel(compute, *refs):
    operands, (whole, buf, sem) = refs[:-3], refs[-3:]
    buf[...] = compute(*operands)
    copy = pltpu.make_async_copy(buf, whole, sem)
    copy.start()
    copy.wait()


def product_in_place(compute, *refs):
    refs[-1][...] = compute(*refs[:-1])


def product(compute, shape, *operands):
    return pl.pallas_call(
        functools.partial(product_kernel, compute),
        out_shape=pltpu.HBM(shape, F32),
        in_specs=[VMEM] * len(operands),
        out_specs=HBM,
        scratch_shapes=[pltpu.VMEM(shape, F32), pltpu.SemaphoreType.DMA(())],
        compiler_params=pltpu.CompilerParams(vmem_limit_bytes=20 << 20),
    )(*[pltpu.with_memory_space_constraint(x, pltpu.VMEM) for x in operands])


def a_part(index, fh, fl, ch, cl):
    n = ch.shape[0]
    part = pl.ds(index * n, n)
    return pair_product((ch[...].T, cl[...].T), (fh[part, :], fl[part, :]), NN)


def b_part(fh, fl, ch, cl):
    return pair_product(read((fh, fl)), read((ch, cl)), NN)


def roles_kernel(count, *refs):
    sources = (refs[:count], refs[count : 2 * count])
    high, low, buf, sems = refs[-4:]
    mine = lax.axis_index("row") % 2
    slots = (mine, 1 - mine)
    rows = buf.shape[1] // CHUNKS
    copies = []
    for side in range(2):
        start = 0
        for source in sources[side]:
            for i in range(source.shape[0] // rows):
                copy = pltpu.make_async_copy(
                    source.at[pl.ds(i * rows, rows)],
                    buf.at[side, pl.ds(start, rows)],
                    sems.at[side, start // rows],
                )
                copy.start()
                copies.append((side, start, copy))
                start += rows
    for side, start, copy in copies:
        copy.wait()
        part = pl.ds(start, rows)
        h, l = parts_of(buf[side, part, :])
        high[slots[side], part, :] = h
        low[slots[side], part, :] = l


def roles_and_vectors_kernel(count, *refs):
    v_own, v_other, va, vb = refs[2 * count : 2 * count + 4]
    roles_kernel(count, *refs[: 2 * count], *refs[-4:])
    mine = lax.axis_index("row") % 2
    half = va.shape[0]
    own = v_own[pl.ds(pl.multiple_of(mine * half, half), half), :]
    other = v_other[pl.ds(pl.multiple_of(mine * half, half), half), :]
    va[...] = jnp.where(mine == 0, own, other)
    vb[...] = jnp.where(mine == 0, other, own)


def roles(owns, others, vectors=()):
    n = others[0].shape[1]
    shape = (2, 2 * n, n)
    halves = [(v.shape[0] // 2, n) for v in vectors]
    body = roles_and_vectors_kernel if vectors else roles_kernel
    return pl.pallas_call(
        functools.partial(body, len(others)),
        out_shape=tuple(pltpu.VMEM(half, F32) for half in halves)
        + (pltpu.VMEM(shape, BF16), pltpu.VMEM(shape, BF16)),
        in_specs=[HBM] * (2 * len(others)) + [VMEM] * len(vectors),
        out_specs=(VMEM,) * (2 + len(halves)),
        scratch_shapes=[pltpu.VMEM(shape, F32), pltpu.SemaphoreType.DMA((2, CHUNKS))],
        compiler_params=pltpu.CompilerParams(vmem_limit_bytes=20 << 20),
    )(
        *[pltpu.with_memory_space_constraint(x, pltpu.HBM) for x in owns],
        *others,
        *[pltpu.with_memory_space_constraint(x, pltpu.VMEM) for x in vectors],
    )


def forward_kernel(*refs):
    *cs, va, vb, ah, al, out = refs
    c = cs[0][...]
    for other in cs[1:]:
        c = c + other[...]
    y = apply_to(add_real(c, va[...]), block_of((ah, al), 0))
    out[...] = apply_to(add_real(y, vb[...]), block_of((ah, al), 1))


def turn_kernel(c, va, vb, fh, fl, ah, al, bh, bl, ua, ub, s):
    y = add_real(c[...], va[...])
    y_b = add_real(apply_to(y, block_of((ah, al), 0)), vb[...])
    u_b = apply_to(y_b, block_of((fh, fl), 1))
    u_a = apply_to(y, block_of((fh, fl), 0))
    ub[...] = u_b
    ua[...] = u_a
    s[...] = u_a + apply_to(u_b, block_of((bh, bl), 0))


def backward_kernel(r, ua, ub, bh, bl, xa, *xb):
    x_b = ub[...] + apply_to(r[...], block_of((bh, bl), 1))
    for out in xb:
        out[...] = x_b
    xa[...] = ua[...] + apply_to(x_b, block_of((bh, bl), 0))


def after(*values, every=False):
    held = lax.optimization_barrier(values)
    return held if every else held[0]


def tree_sum(values):
    while len(values) > 1:
        values = [values[i] + values[i + 1] for i in range(0, len(values), 2)]
    return values[0]


def shards(inv_factors, coupling, vectors):
    n = inv_factors.shape[3]
    width = vectors.shape[2]
    half = width // 2
    rows = lax.axis_size("row")
    nodes = lax.axis_size("node")
    layers = rows // 2
    core = lax.axis_index("row") % 2
    node = lax.axis_index("node")
    first = core == 0

    def swap_core(value):
        return lax.ppermute(value, "row", [(r, r ^ 1) for r in range(rows)])

    def hop(value, source, target):
        return lax.ppermute(value, "row", [(2 * source + c, 2 * target + c) for c in range(2)])

    def exchange_node(value, d):
        return lax.ppermute(value, "node", [(j, j ^ d) for j in range(nodes)])

    def exchange_layer(value, d):
        return lax.ppermute(value, "row", [(r, r ^ (2 * d)) for r in range(rows)])

    factor = inv_factors[0, 0].reshape(2 * n, n)
    couple = coupling[0]
    block = ((2 * half, n), F32)

    fh, fl, ch, cl, v_t, g = pl.pallas_call(
        enter_kernel,
        out_shape=(
            pltpu.VMEM((2 * n, n), BF16),
            pltpu.VMEM((2 * n, n), BF16),
            pltpu.VMEM((n, n), BF16),
            pltpu.VMEM((n, n), BF16),
            pltpu.VMEM((width, n), F32),
            pltpu.VMEM((2 * width, n), F32),
        ),
        in_specs=[HBM] * 3,
        out_specs=(VMEM,) * 6,
        scratch_shapes=[
            pltpu.VMEM((2 * n, n), F32),
            pltpu.VMEM((n, n), F32),
            pltpu.VMEM((width, n), F32),
            pltpu.SemaphoreType.DMA((CHUNKS + 2,)),
        ],
        compiler_params=pltpu.CompilerParams(vmem_limit_bytes=20 << 20),
        name="enter",
    )(*[pltpu.with_memory_space_constraint(x, pltpu.HBM) for x in (factor, couple, vectors[0].T)])
    from_a = swap_core(g)
    (a_re,) = call(
        functools.partial(product_in_place, functools.partial(a_part, 0)),
        [((n, n), F32)], after(fh, g), fl, ch, cl,
    )
    lo, hi = call(leave_kernel, [block, block], v_t, from_a, after(fh, from_a), fl, ch, cl)

    got_lo = lax.ppermute(lo, "row", [(1, 2)])
    got_hi = lax.ppermute(hi, "row", [(1, 3)])
    got = [got_lo, got_hi]
    a_im = product(functools.partial(a_part, 1), (n, n), after(fh, lo), fl, ch, cl)
    a_re_other = swap_core(after(a_re, lo))
    a_im_other = swap_core(a_im)
    v_other = swap_core(after(v_t, lo))
    va, vb, *a_mats = roles([a_re, a_im], [a_re_other, a_im_other], [v_t, v_other])
    f_other = swap_core(after(factor, a_re_other, a_im_other))
    carry = jnp.zeros((2 * half, n), F32)
    for t in range(layers - 1):
        if t > 0:
            got = [hop(leaving, t, t + 1)]
        carry = sum(got, carry)
        if t < layers - 2:
            (leaving,) = call(forward_kernel, [block], *got, va, vb, *a_mats)
        if t == 0:
            f_mats = roles([after(factor, leaving)], [f_other])
            b_own = product(b_part, (2 * n, n), after(fh, leaving), fl, ch, cl)
            b_other = swap_core(b_own)
        if t == 1:
            b_mats = roles([after(b_own, leaving)], [b_other])
    u_a, u_b, leaving = call(turn_kernel, [block] * 3, carry, va, vb, *f_mats, *a_mats, *b_mats)

    following = jnp.zeros((2 * half, n), F32)
    for t in range(layers - 1, 0, -1):
        got = hop(leaving, t, t - 1)
        following = following + got
        if t > 1:
            (leaving,) = call(backward_kernel, [block], got, u_a, u_b, *b_mats)
    x_a, x_b = call(backward_kernel, [block] * 2, following, u_a, u_b, *b_mats)

    share = n // nodes
    x_both = jnp.concatenate([x_a, x_b], axis=0)
    pieces = [lax.dynamic_slice_in_dim(x_both, (node ^ d) * share, share, 1) for d in range(nodes)]
    pieces = [pieces[0]] + [exchange_node(pieces[d], d) for d in range(1, nodes)]
    pieces = [p.reshape(2, 2, half, share) for p in pieces]
    terms = []
    for order in range(MOM):
        re_terms, im_terms = [], []
        for d in range(nodes):
            theta = 2.0 * math.pi * ((node ^ d).astype(F32) + 0.5) / nodes
            w_re = jnp.cos((order + 1) * theta) / nodes
            w_im = jnp.sin((order + 1) * theta) / nodes
            re, im = pieces[d][:, 0], pieces[d][:, 1]
            re_terms.append(w_re * re - w_im * im)
            im_terms.append(w_re * im + w_im * re)
        terms += [tree_sum(re_terms), tree_sum(im_terms)]
    mine = jnp.stack(terms, axis=1)
    groups = 2 * MOM
    cols = groups * width
    other = swap_core(mine.reshape(2 * groups * half, share)).reshape(mine.shape)
    both = jnp.stack([jnp.where(first, mine, other), jnp.where(first, other, mine)], axis=2)
    both = both.reshape(2, cols, share)
    moments = jnp.where(first, both[0], both[1])

    mine = mine.reshape(2, groups * half, share)
    gram = lax.dot_general(mine[0], both[0], NT, precision=PREC) + lax.dot_general(
        mine[1], both[1], NT, precision=PREC
    )
    hc = groups * half
    layer = lax.axis_index("row") // 2
    gs = hc // layers
    own = [lax.dynamic_slice_in_dim(gram, (layer ^ d) * gs, gs, 0) for d in range(layers)]
    piece = tree_sum([own[0]] + [exchange_layer(own[d], d) for d in range(1, layers)])
    piece = tree_sum([piece] + [exchange_node(piece, d) for d in range(1, nodes)])
    piece = piece * (nodes / (rows * n))
    got = [piece] + [exchange_layer(piece, d) for d in range(1, layers)]
    gram = jnp.zeros((hc, cols), F32)
    for d in range(layers):
        gram = lax.dynamic_update_slice_in_dim(gram, got[d], (layer ^ d) * gs, 0)
    other = swap_core(gram)
    gram = gram.reshape(groups, half, cols)
    other = other.reshape(groups, half, cols)
    gram = jnp.stack([jnp.where(first, gram, other), jnp.where(first, other, gram)], axis=1)
    return moments.T[None], gram.reshape(cols, cols)


def solution(mesh):
    return jax.shard_map(
        shards,
        mesh=mesh,
        in_specs=(
            P(("intv", "node"), "row", None, None, None),
            P("row", None, None),
            P("row", None, None),
        ),
        out_specs=(P(("intv", "row"), "node", None), P("intv", None)),
        check_vma=False,
    )
```

time: 104 us -> 99.8 us (0.960)
  matrix products: 34.3 us -> 0.46 us
  Pallas kernels: 0 us -> 26.7 us
  waiting for transfers between devices: 32.2 us -> 41.6 us
  other arithmetic: 8.26 us -> 1.02 us
  local copies, waits for them, and re-layouts: 0.94 us -> 2.48 us
    dot_general x22 -> x2, matrix products: 34.3 us -> 0.46 us  [the longest x1 0.23 us: shards(): lax.dot_general(mine[1], both[1], NT, precision=PREC)]
    pallas_call x0 -> x14, Pallas kernels: none -> 26.7 us  [the longest x8 12.2 us: call(): pl.pallas_call(kernel, out_shape=tuple((pltpu.VMEM(shape, dtype) for shap...]
    ppermute x6 -> x5, waiting for transfers between devices: 15.7 us -> 23.5 us  [hop(): lax.ppermute(value, 'row', [(2 * source + c, 2 * target + c) for c in ran...]
    ppermute x6 -> x5, starting transfers between devices: 9.22 us -> 4.13 us  [hop(): lax.ppermute(value, 'row', [(2 * source + c, 2 * target + c) for c in ran...]
    ppermute x3 -> x6, waiting for transfers between devices: 2.65 us -> 7.1 us  [exchange_layer(): return lax.ppermute(value, 'row', [(r, r ^ 2 * d) for r in range(rows)])]
    ppermute x3 -> x6, starting transfers between devices: 3.55 us -> 7.99 us  [exchange_layer(): return lax.ppermute(value, 'row', [(r, r ^ 2 * d) for r in range(rows)])]
    ppermute x9 -> x6, waiting for transfers between devices: 9.23 us -> 4.87 us  [exchange_node(): return lax.ppermute(value, 'node', [(j, j ^ d) for j in range(nodes)])]
    select_n x9 -> x1, other arithmetic: 4.37 us -> 0.02 us  [shards(): jnp.where(first, gram, other)]
  transfers between devices with their start and end apart: 27 -> 27, of which waited for: 16 -> 18; matrix products, arithmetic and copies ran while one was open for 31% -> 1% of each run, Pallas kernels for 0% -> 7%
where the time goes in v1:
time: 99.8 us; the launch traced here: 99.5 us
  waiting for transfers between devices  41.6 us (42%)
  Pallas kernels  26.7 us (27%)
  starting transfers between devices  24.9 us (25%)
  local copies, waits for them, and re-layouts  2.48 us (2%)
  between operations  2.33 us (2%)
  other arithmetic  1.02 us (1%)
    ppermute x5, waiting for transfers between devices, hop(): lax.ppermute(value, 'row', [(2 * source + c, 2 * target + c) for c in ran...  23.5 us
    pallas_call x8, Pallas kernels, call(): pl.pallas_call(kernel, out_shape=tuple((pltpu.VMEM(shape, dtype) for shap...  12.2 us
    ppermute x6, starting transfers between devices, exchange_layer(): return lax.ppermute(value, 'row', [(r, r ^ 2 * d) for r in range(rows)])  7.99 us
    ppermute x6, starting transfers between devices, exchange_node(): return lax.ppermute(value, 'node', [(j, j ^ d) for j in range(nodes)])  7.11 us
    ppermute x6, waiting for transfers between devices, exchange_layer(): return lax.ppermute(value, 'row', [(r, r ^ 2 * d) for r in range(rows)])  7.1 us
    ppermute x8, waiting for transfers between devices, swap_core(): return lax.ppermute(value, 'row', [(r, r ^ 1) for r in range(rows)])  6.13 us
    pallas_call x3, Pallas kernels, roles(): pl.pallas_call(functools.partial(body, len(others)), out_shape=tuple((plt...  6.12 us
    pallas_call x2, Pallas kernels, product(): pl.pallas_call(functools.partial(product_kernel, compute), out_shape=pltp...  5.15 us
  transfers between devices with their start and end apart: 27, of which 18 were waited for; matrix products, arithmetic and copies ran while one was open for 1% of the time, Pallas kernels for 7%

profile of v1, /device:TPU:0, one launch (start us, length us, event | category | flops | bytes accessed | tf_op | source)
XLA Modules:
  0.0 99.5 jit_solution(18280665981935633037)
XLA Ops:
  0.6 3.3 %enter.1 = (bf16[1024,512]{1,0:T(8,128)(2,1)S(1)}, bf16[1024,512]{1,0:T(8,128)(2,1)S(1)}, bf16[512,512]{1,0:T(8,128)(2,1)S(1)}, bf16[512,512]{1,0:T(8,128)(2,1)S...) custom-call(f32[1024,512]{1,0:T(8,128)} %bitcast.146, f32[512,512]{1,0:T(8,128)} %bitcast.155, f32[64,512]{1,0:T(8,128)} %bitcast.180), custom_call_target="tpu_custom_call" | custom-call | tf_op jit(solution)/shard_map/enter/pallas_call | solution.py:274
  3.9 0.5 collective-permute-start
  4.5 1.0 %shard_map.51.refs_0_ = f32[512,512]{1,0:T(8,128)S(1)} custom-call(bf16[1024,512]{1,0:T(8,128)(2,1)S(1)} %get-tuple-element.53.fh.refs_0_, bf16[1024,512]{1,0:T(8,128)(2,1)S(1)} %get-tuple-element.36.fl.refs_1_, bf16[512,512]{1,0:T(8,128)(2,1)S(1)} %get-tuple-element.37.ch.refs_2_, bf16[512,512]{1,0:T(8,128)(2,1)S(1)} %get-tuple-element.38.cl.refs_3_), custom_call_target="tpu_custom_call" | custom-call | tf_op jit(solution)/shard_map/pallas_call | solution.py:64
  5.5 0.1 collective-permute-done.g
  5.6 1.1 %shard_map.50 = (f32[64,512]{1,0:T(8,128)S(1)}, f32[64,512]{1,0:T(8,128)S(1)}) custom-call(f32[64,512]{1,0:T(8,128)S(1)} %get-tuple-element.44.vt.refs_4_, f32[128,512]{1,0:T(8,128)S(1)} %collective-permute-done.g, bf16[1024,512]{1,0:T(8,128)(2,1)S(1)} %get-tuple-element.53.fh.refs_0_, bf16[1024,512]{1,0:T(8,128)(2,1)S(1)} %get-tuple-element.36.fl.refs_1_, ...), custom_call_target="tpu_custom_call" | custom-call | tf_op jit(solution)/shard_map/pallas_call | solution.py:64
  6.7 2.0 %shard_map.52.refs_1_ = f32[512,512]{1,0:T(8,128)} custom-call(bf16[1024,512]{1,0:T(8,128)(2,1)S(1)} %get-tuple-element.53.fh.refs_0_, bf16[1024,512]{1,0:T(8,128)(2,1)S(1)} %get-tuple-element.36.fl.refs_1_, bf16[512,512]{1,0:T(8,128)(2,1)S(1)} %get-tuple-element.37.ch.refs_2_, bf16[512,512]{1,0:T(8,128)(2,1)S(1)} %get-tuple-element.38.cl.refs_3_), custom_call_target="tpu_custom_call" | custom-call | tf_op jit(solution)/shard_map/pallas_call | solution.py:132
  8.7 0.4 collective-permute-start.3
  9.2 0.1 collective-permute-start.4
  9.3 0.4 collective-permute-start.5
  9.7 0.7 collective-permute-start.2
  10.3 0.7 collective-permute-start.1
  11.0 2.1 %collective-permute-done.5.refs_5_ = f32[64,512]{1,0:T(8,128)S(1)} collective-permute-done((f32[64,512]{1,0:T(8,128)S(1)}, f32[64,512]{1,0:T(8,128)S(1)}, u32[]{:S(2)}, u32[]{:S(2)}) %collective-permute-start.5) | collective-permute-done | bytes 131104 | tf_op jit(solution)/shard_map/ppermute | solution.py:259
  13.1 2.0 %shard_map.53 = (f32[32,512]{1,0:T(8,128)S(1)}, f32[32,512]{1,0:T(8,128)S(1)}, bf16[2,1024,512]{2,1,0:T(8,128)(2,1)S(1)}, bf16[2,1024,512]{2,1,0:T(8,128)(2,1)S(1)}) custom-call(f32[512,512]{1,0:T(8,128)} %copy-done.2, f32[512,512]{1,0:T(8,128)} %shard_map.52.refs_1_, f32[512,512]{1,0:T(8,128)S(1)} %collective-permute-done.3.refs_2_, ...), custom_call_target="tpu_custom_call" | custom-call | tf_op jit(solution)/shard_map/pallas_call | solution.py:195
  15.2 1.5 %shard_map.54 = f32[64,512]{1,0:T(8,128)S(1)} custom-call(f32[64,512]{1,0:T(8,128)S(1)} %collective-permute-done.1.refs_0_, f32[64,512]{1,0:T(8,128)S(1)} %collective-permute-done.2.refs_1_, f32[32,512]{1,0:T(8,128)S(1)} %get-tuple-element.45.refs_2_.refs_1_.va, f32[32,512]{1,0:T(8,128)S(1)} %get-tuple-element.46.refs_3_.refs_2_.vb, ...), custom_call_target="tpu_custom_call" | custom-call | tf_op jit(solution)/shard_map/pallas_call | solution.py:64
  16.7 0.0 copy-start.3
  16.7 3.1 %shard_map.57.refs_0_ = f32[1024,512]{1,0:T(8,128)} custom-call(bf16[1024,512]{1,0:T(8,128)(2,1)S(1)} %get-tuple-element.53.fh.refs_0_, bf16[1024,512]{1,0:T(8,128)(2,1)S(1)} %get-tuple-element.36.fl.refs_1_, bf16[512,512]{1,0:T(8,128)(2,1)S(1)} %get-tuple-element.37.ch.refs_2_, bf16[512,512]{1,0:T(8,128)(2,1)S(1)} %get-tuple-element.38.cl.refs_3_), custom_call_target="tpu_custom_call" | custom-call | tf_op jit(solution)/shard_map/pallas_call | solution.py:132
  19.8 2.6 %collective-permute-start.9 = (f32[1024,512]{1,0:T(8,128)}, f32[1024,512]{1,0:T(8,128)S(1)}, u32[]{:S(2)}, u32[]{:S(2)}) collective-permute-start(f32[1024,512]{1,0:T(8,128)} %shard_map.57.refs_0_), channel_id=1, source_target_pairs={{0,1},{1,0},{2,3},{3,2},{4,5},{5,4},{6,7},{7,6},{8,9},{9,8},{10,11... | collective-permute-start | bytes 6291464 | tf_op jit(solution)/shard_map/ppermute | solution.py:259
  22.5 0.1 collective-permute-start.8
  22.6 0.7 collective-permute-start.6
  23.3 1.5 %shard_map.55 = f32[64,512]{1,0:T(8,128)S(1)} custom-call(f32[64,512]{1,0:T(8,128)S(1)} %collective-permute-done.6.refs_0_, f32[32,512]{1,0:T(8,128)S(1)} %get-tuple-element.45.refs_2_.refs_1_.va, f32[32,512]{1,0:T(8,128)S(1)} %get-tuple-element.46.refs_3_.refs_2_.vb, bf16[2,1024,512]{2,1,0:T(8,128)(2,1)S(1)} %get-tuple-element.47.refs_4_.refs_3_.ah, ...), custom_call_target="tpu_custom_call" | custom-call | tf_op jit(solution)/shard_map/pallas_call | solution.py:64
  24.7 0.7 collective-permute-start.7
  25.5 1.0 %collective-permute-done.9.refs_1_ = f32[1024,512]{1,0:T(8,128)S(1)} collective-permute-done((f32[1024,512]{1,0:T(8,128)}, f32[1024,512]{1,0:T(8,128)S(1)}, u32[]{:S(2)}, u32[]{:S(2)}) %collective-permute-start.9) | collective-permute-done | bytes 2097184 | tf_op jit(solution)/shard_map/ppermute | solution.py:259
  26.5 2.0 %shard_map.58 = (bf16[2,1024,512]{2,1,0:T(8,128)(2,1)S(1)}, bf16[2,1024,512]{2,1,0:T(8,128)(2,1)S(1)}) custom-call(f32[1024,512]{1,0:T(8,128)} %shard_map.57.refs_0_, f32[1024,512]{1,0:T(8,128)S(1)} %collective-permute-done.9.refs_1_), custom_call_target="tpu_custom_call" | custom-call | tf_op jit(solution)/shard_map/pallas_call | solution.py:195
  28.5 0.9 collective-permute-done.8.refs_1_
  29.5 2.0 %shard_map.56 = (bf16[2,1024,512]{2,1,0:T(8,128)(2,1)S(1)}, bf16[2,1024,512]{2,1,0:T(8,128)(2,1)S(1)}) custom-call(f32[1024,512]{1,0:T(8,128)} %bitcast.147, f32[1024,512]{1,0:T(8,128)S(1)} %collective-permute-done.8.refs_1_), custom_call_target="tpu_custom_call" | custom-call | tf_op jit(solution)/shard_map/pallas_call | solution.py:195
  31.5 2.8 %shard_map.59 = (f32[64,512]{1,0:T(8,128)S(1)}, f32[64,512]{1,0:T(8,128)S(1)}, f32[64,512]{1,0:T(8,128)S(1)}) custom-call(f32[64,512]{1,0:T(8,128)S(1)} %add_add_fusion.1.c, f32[32,512]{1,0:T(8,128)S(1)} %get-tuple-element.45.refs_2_.refs_1_.va, f32[32,512]{1,0:T(8,128)S(1)} %get-tuple-element.46.refs_3_.refs_2_.vb, ...), custom_call_target="tpu_custom_call" | custom-call | tf_op jit(solution)/shard_map/pallas_call | solution.py:64
  34.3 0.7 collective-permute-start.10
  35.0 1.5 %shard_map.60 = f32[64,512]{1,0:T(8,128)S(1)} custom-call(f32[64,512]{1,0:T(8,128)S(1)} %collective-permute-done.10.r, f32[64,512]{1,0:T(8,128)S(1)} %get-tuple-element.58.ua, f32[64,512]{1,0:T(8,128)S(1)} %get-tuple-element.59.ub, bf16[2,1024,512]{2,1,0:T(8,128)(2,1)S(1)} %get-tuple-element.55.bh, bf16[2,1024,512]{2,1,0:T(8,128)(2,1)S(1)} %get-tuple-element.56.bl), custom_call_target="tpu_custom_call" | custom-call | tf_op jit(solution)/shard_map/pallas_call | solution.py:64
  36.5 0.7 collective-permute-start.11
  37.2 1.5 %shard_map.61 = f32[64,512]{1,0:T(8,128)S(1)} custom-call(f32[64,512]{1,0:T(8,128)S(1)} %collective-permute-done.11.r, f32[64,512]{1,0:T(8,128)S(1)} %get-tuple-element.58.ua, f32[64,512]{1,0:T(8,128)S(1)} %get-tuple-element.59.ub, bf16[2,1024,512]{2,1,0:T(8,128)(2,1)S(1)} %get-tuple-element.55.bh, bf16[2,1024,512]{2,1,0:T(8,128)(2,1)S(1)} %get-tuple-element.56.bl), custom_call_target="tpu_custom_call" | custom-call | tf_op jit(solution)/shard_map/pallas_call | solution.py:64
  38.6 1.5 %collective-permute-start.12 = (f32[64,512]{1,0:T(8,128)S(1)}, f32[64,512]{1,0:T(8,128)S(1)}, u32[]{:S(2)}, u32[]{:S(2)}) collective-permute-start(f32[64,512]{1,0:T(8,128)S(1)} %shard_map.61), channel_id=1, source_target_pairs={{2,0},{3,1},{10,8},{11,9},{18,16},{19,17},{26,24},{27,25}} | collective-permute-start | bytes 393224 | tf_op jit(solution)/shard_map/ppermute | solution.py:262
  40.1 23.4 %collective-permute-done.12 = f32[64,512]{1,0:T(8,128)S(1)} collective-permute-done((f32[64,512]{1,0:T(8,128)S(1)}, f32[64,512]{1,0:T(8,128)S(1)}, u32[]{:S(2)}, u32[]{:S(2)}) %collective-permute-start.12) | collective-permute-done | bytes 131104 | tf_op jit(solution)/shard_map/ppermute | solution.py:262
  63.6 1.6 %copy-done.1 = bf16[2,1024,512]{2,1,0:T(8,128)(2,1)S(1)} copy-done((bf16[2,1024,512]{2,1,0:T(8,128)(2,1)S(1)}, bf16[2,1024,512]{2,1,0:T(8,128)(2,1)}, u32[]{:S(2)}) %copy-start.1) | copy-done | bytes 2097176
  65.2 1.5 %shard_map.62 = (f32[64,512]{1,0:T(8,128)S(1)}, f32[64,512]{1,0:T(8,128)S(1)}) custom-call(f32[64,512]{1,0:T(8,128)S(1)} %add_add_fusion.r, f32[64,512]{1,0:T(8,128)S(1)} %get-tuple-element.58.ua, f32[64,512]{1,0:T(8,128)S(1)} %get-tuple-element.59.ub, bf16[2,1024,512]{2,1,0:T(8,128)(2,1)S(1)} %get-tuple-element.55.bh, bf16[2,1024,512]{2,1,0:T(8,128)(2,1)S(1)} %copy-done.1), custom_call_target="tpu_custom_call" | custom-call | tf_op jit(solution)/shard_map/pallas_call | solution.py:64
  66.8 2.5 %collective-permute-start.15 = (f32[128,128]{1,0:T(8,128)S(1)}, f32[128,128]{1,0:T(8,128)S(1)}, u32[]{:S(2)}, u32[]{:S(2)}) collective-permute-start(f32[128,128]{1,0:T(8,128)S(1)} %get-tuple-element.72), channel_id=1, source_target_pairs={{0,24},{8,16},{16,8},{24,0},{1,25},{9,17},{17,9},{25,1},{2,26},{10... | collective-permute-start | bytes 196616 | tf_op jit(solution)/shard_map/ppermute | solution.py:265
  69.3 0.5 collective-permute-start.14
  69.8 0.5 collective-permute-start.13
  71.6 0.4 collective-permute-done.15
  72.0 1.5 %collective-permute-done.14 = f32[128,128]{1,0:T(8,128)S(1)} collective-permute-done((f32[128,128]{1,0:T(8,128)S(1)}, f32[128,128]{1,0:T(8,128)S(1)}, u32[]{:S(2)}, u32[]{:S(2)}) %collective-permute-start.14) | collective-permute-done | bytes 65568 | tf_op jit(solution)/shard_map/ppermute | solution.py:265
  73.6 0.5 collective-permute-done.13
  74.2 0.1 collective-permute-start.16
  74.3 1.3 %collective-permute-done.16 = f32[256,128]{1,0:T(8,128)S(1)} collective-permute-done((f32[256,128]{1,0:T(8,128)S(1)}, f32[256,128]{1,0:T(8,128)S(1)}, u32[]{:S(2)}, u32[]{:S(2)}) %collective-permute-start.16) | collective-permute-done | bytes 131104 | tf_op jit(solution)/shard_map/ppermute | solution.py:259
  75.7 0.2 fusion.10
  75.9 0.2 convolution_add_fusion
  76.2 0.1 collective-permute-start.17
  76.3 0.1 collective-permute-start.19
  76.4 3.4 %collective-permute-start.18 = (f32[32,256]{1,0:T(8,128)S(1)}, f32[32,256]{1,0:T(8,128)S(1)}, u32[]{:S(2)}, u32[]{:S(2)}) collective-permute-start(f32[32,256]{1,0:T(8,128)S(1)} %get-tuple-element.78), channel_id=1, source_target_pairs={{0,4},{1,5},{2,6},{3,7},{4,0},{5,1},{6,2},{7,3},{8,12},{9,13},{10,... | collective-permute-start | bytes 98312 | tf_op jit(solution)/shard_map/ppermute | solution.py:268
  79.8 0.4 collective-permute-done.17
  80.2 1.9 %collective-permute-done.19 = f32[32,256]{1,0:T(8,128)S(1)} collective-permute-done((f32[32,256]{1,0:T(8,128)S(1)}, f32[32,256]{1,0:T(8,128)S(1)}, u32[]{:S(2)}, u32[]{:S(2)}) %collective-permute-start.19) | collective-permute-done | bytes 32800 | tf_op jit(solution)/shard_map/ppermute | solution.py:268
  82.1 0.9 collective-permute-done.18
  83.0 1.6 %collective-permute-start.22 = (f32[32,256]{1,0:T(8,128)S(1)}, f32[32,256]{1,0:T(8,128)S(1)}, u32[]{:S(2)}, u32[]{:S(2)}) collective-permute-start(f32[32,256]{1,0:T(8,128)S(1)} %add_add_fusion.2), channel_id=1, source_target_pairs={{0,24},{8,16},{16,8},{24,0},{1,25},{9,17},{17,9},{25,1},{2,26},{10... | collective-permute-start | bytes 98312 | tf_op jit(solution)/shard_map/ppermute | solution.py:265
  84.6 0.5 collective-permute-start.21
  85.1 1.5 %collective-permute-start.20 = (f32[32,256]{1,0:T(8,128)S(1)}, f32[32,256]{1,0:T(8,128)S(1)}, u32[]{:S(2)}, u32[]{:S(2)}) collective-permute-start(f32[32,256]{1,0:T(8,128)S(1)} %add_add_fusion.2), channel_id=1, source_target_pairs={{0,8},{8,0},{16,24},{24,16},{1,9},{9,1},{17,25},{25,17},{2,10},{10... | collective-permute-start | bytes 98312 | tf_op jit(solution)/shard_map/ppermute | solution.py:265
  86.6 1.3 %collective-permute-done.22 = f32[32,256]{1,0:T(8,128)S(1)} collective-permute-done((f32[32,256]{1,0:T(8,128)S(1)}, f32[32,256]{1,0:T(8,128)S(1)}, u32[]{:S(2)}, u32[]{:S(2)}) %collective-permute-start.22) | collective-permute-done | bytes 32800 | tf_op jit(solution)/shard_map/ppermute | solution.py:265
  87.9 0.6 collective-permute-done.21
  88.5 0.5 collective-permute-done.20
  89.0 0.3 collective-permute-start.23
  89.3 2.3 %collective-permute-start.24 = (f32[32,256]{1,0:T(8,128)S(1)}, f32[32,256]{1,0:T(8,128)S(1)}, u32[]{:S(2)}, u32[]{:S(2)}) collective-permute-start(f32[32,256]{1,0:T(8,128)S(1)} %get-tuple-element.65), channel_id=1, source_target_pairs={{0,4},{1,5},{2,6},{3,7},{4,0},{5,1},{6,2},{7,3},{8,12},{9,13},{10,... | collective-permute-start | bytes 98312 | tf_op jit(solution)/shard_map/ppermute | solution.py:268
  91.6 1.8 %collective-permute-start.25 = (f32[32,256]{1,0:T(8,128)S(1)}, f32[32,256]{1,0:T(8,128)S(1)}, u32[]{:S(2)}, u32[]{:S(2)}) collective-permute-start(f32[32,256]{1,0:T(8,128)S(1)} %get-tuple-element.65), channel_id=1, source_target_pairs={{0,6},{1,7},{2,4},{3,5},{4,2},{5,3},{6,0},{7,1},{8,14},{9,15},{10,... | collective-permute-start | bytes 98312 | tf_op jit(solution)/shard_map/ppermute | solution.py:268
  93.5 0.6 collective-permute-done.24
  94.1 3.2 %collective-permute-done.25 = f32[32,256]{1,0:T(8,128)S(1)} collective-permute-done((f32[32,256]{1,0:T(8,128)S(1)}, f32[32,256]{1,0:T(8,128)S(1)}, u32[]{:S(2)}, u32[]{:S(2)}) %collective-permute-start.25) | collective-permute-done | bytes 32800 | tf_op jit(solution)/shard_map/ppermute | solution.py:268
  97.4 0.8 copy.43
  98.1 0.6 collective-permute-done.26
  98.7 0.7 pad_maximum_fusion
  (38 shorter events, 0.5 us)
Async XLA Ops:
  3.9 1.7 %collective-permute-start = (f32[128,512]{1,0:T(8,128)S(1)}, f32[128,512]{1,0:T(8,128)S(1)}, u32[]{:S(2)}, u32[]{:S(2)}) collective-permute-start(f32[128,512]{1,0:T(8,128)S(1)} %get-tuple-element.33), channel_id=1, source_target_pairs={{0,1},{1,0},{2,3},{3,2},{4,5},{5,4},{6,7},{7,6},{8,9},{9,8},{10,11... | collective-permute-start | bytes 786440 | tf_op jit(solution)/shard_map/ppermute | solution.py:259
  5.5 3.2 %copy-start.2 = (f32[512,512]{1,0:T(8,128)}, f32[512,512]{1,0:T(8,128)S(1)}, u32[]{:S(2)}) copy-start(f32[512,512]{1,0:T(8,128)S(1)} %shard_map.51.refs_0_) | copy-start | bytes 3145732
  8.7 4.4 %collective-permute-start.3 = (f32[512,512]{1,0:T(8,128)S(1)}, f32[512,512]{1,0:T(8,128)S(1)}, u32[]{:S(2)}, u32[]{:S(2)}) collective-permute-start(f32[512,512]{1,0:T(8,128)S(1)} %shard_map.51.refs_0_), channel_id=1, source_target_pairs={{0,1},{1,0},{2,3},{3,2},{4,5},{5,4},{6,7},{7,6},{8,9},{9,8},{10,11... | collective-permute-start | bytes 3145736 | tf_op jit(solution)/shard_map/ppermute | solution.py:259
  9.2 4.0 %collective-permute-start.4 = (f32[512,512]{1,0:T(8,128)}, f32[512,512]{1,0:T(8,128)S(1)}, u32[]{:S(2)}, u32[]{:S(2)}) collective-permute-start(f32[512,512]{1,0:T(8,128)} %shard_map.52.refs_1_), channel_id=1, source_target_pairs={{0,1},{1,0},{2,3},{3,2},{4,5},{5,4},{6,7},{7,6},{8,9},{9,8},{10,11... | collective-permute-start | bytes 3145736 | tf_op jit(solution)/shard_map/ppermute | solution.py:259
  9.3 3.8 %collective-permute-start.5 = (f32[64,512]{1,0:T(8,128)S(1)}, f32[64,512]{1,0:T(8,128)S(1)}, u32[]{:S(2)}, u32[]{:S(2)}) collective-permute-start(f32[64,512]{1,0:T(8,128)S(1)} %get-tuple-element.44.vt.refs_4_), channel_id=1, source_target_pairs={{0,1},{1,0},{2,3},{3,2},{4,5},{5,4},{6,7},{7,6},{8,9},{9,8},{10,11... | collective-permute-start | bytes 393224 | tf_op jit(solution)/shard_map/ppermute | solution.py:259
  9.7 5.5 %collective-permute-start.2 = (f32[64,512]{1,0:T(8,128)S(1)}, f32[64,512]{1,0:T(8,128)S(1)}, u32[]{:S(2)}, u32[]{:S(2)}) collective-permute-start(f32[64,512]{1,0:T(8,128)S(1)} %get-tuple-element.40), channel_id=1, source_target_pairs={{1,3},{9,11},{17,19},{25,27}} | collective-permute-start | bytes 393224 | tf_op jit(solution)/shard_map/ppermute | solution.py:303
  10.3 4.9 %collective-permute-start.1 = (f32[64,512]{1,0:T(8,128)S(1)}, f32[64,512]{1,0:T(8,128)S(1)}, u32[]{:S(2)}, u32[]{:S(2)}) collective-permute-start(f32[64,512]{1,0:T(8,128)S(1)} %get-tuple-element.39), channel_id=1, source_target_pairs={{1,2},{9,10},{17,18},{25,26}} | collective-permute-start | bytes 393224 | tf_op jit(solution)/shard_map/ppermute | solution.py:302
  16.7 5.8 %copy-start.3 = (f32[1,1,2,512,512]{4,3,2,1,0:T(8,128)S(1)}, f32[1,1,2,512,512]{4,3,2,1,0:T(8,128)}, u32[]{:S(2)}) copy-start(f32[1,1,2,512,512]{4,3,2,1,0:T(8,128)} %param.3) | copy-start | bytes 6291460
  19.8 6.6 %collective-permute-start.9 = (f32[1024,512]{1,0:T(8,128)}, f32[1024,512]{1,0:T(8,128)S(1)}, u32[]{:S(2)}, u32[]{:S(2)}) collective-permute-start(f32[1024,512]{1,0:T(8,128)} %shard_map.57.refs_0_), channel_id=1, source_target_pairs={{0,1},{1,0},{2,3},{3,2},{4,5},{5,4},{6,7},{7,6},{8,9},{9,8},{10,11... | collective-permute-start | bytes 6291464 | tf_op jit(solution)/shard_map/ppermute | solution.py:259
  22.5 7.0 %collective-permute-start.8 = (f32[1024,512]{1,0:T(8,128)S(1)}, f32[1024,512]{1,0:T(8,128)S(1)}, u32[]{:S(2)}, u32[]{:S(2)}) collective-permute-start(f32[1024,512]{1,0:T(8,128)S(1)} %bitcast.148), channel_id=1, source_target_pairs={{0,1},{1,0},{2,3},{3,2},{4,5},{5,4},{6,7},{7,6},{8,9},{9,8},{10,11... | collective-permute-start | bytes 6291464 | tf_op jit(solution)/shard_map/ppermute | solution.py:259
  22.6 0.7 collective-permute-start.6
  24.7 0.7 collective-permute-start.7
  28.5 8.6 %copy-start = (bf16[2,1024,512]{2,1,0:T(8,128)(2,1)}, bf16[2,1024,512]{2,1,0:T(8,128)(2,1)S(1)}, u32[]{:S(2)}) copy-start(bf16[2,1024,512]{2,1,0:T(8,128)(2,1)S(1)} %get-tuple-element.56.bl) | copy-start | bytes 6291460
  34.3 0.7 collective-permute-start.10
  36.5 0.7 collective-permute-start.11
  38.6 24.9 %collective-permute-start.12 = (f32[64,512]{1,0:T(8,128)S(1)}, f32[64,512]{1,0:T(8,128)S(1)}, u32[]{:S(2)}, u32[]{:S(2)}) collective-permute-start(f32[64,512]{1,0:T(8,128)S(1)} %shard_map.61), channel_id=1, source_target_pairs={{2,0},{3,1},{10,8},{11,9},{18,16},{19,17},{26,24},{27,25}} | collective-permute-start | bytes 393224 | tf_op jit(solution)/shard_map/ppermute | solution.py:262
  63.6 1.6 %copy-start.1 = (bf16[2,1024,512]{2,1,0:T(8,128)(2,1)S(1)}, bf16[2,1024,512]{2,1,0:T(8,128)(2,1)}, u32[]{:S(2)}) copy-start(bf16[2,1024,512]{2,1,0:T(8,128)(2,1)} %copy-done) | copy-start | bytes 6291460
  66.8 5.2 %collective-permute-start.15 = (f32[128,128]{1,0:T(8,128)S(1)}, f32[128,128]{1,0:T(8,128)S(1)}, u32[]{:S(2)}, u32[]{:S(2)}) collective-permute-start(f32[128,128]{1,0:T(8,128)S(1)} %get-tuple-element.72), channel_id=1, source_target_pairs={{0,24},{8,16},{16,8},{24,0},{1,25},{9,17},{17,9},{25,1},{2,26},{10... | collective-permute-start | bytes 196616 | tf_op jit(solution)/shard_map/ppermute | solution.py:265
  69.3 4.3 %collective-permute-start.14 = (f32[128,128]{1,0:T(8,128)S(1)}, f32[128,128]{1,0:T(8,128)S(1)}, u32[]{:S(2)}, u32[]{:S(2)}) collective-permute-start(f32[128,128]{1,0:T(8,128)S(1)} %get-tuple-element.73), channel_id=1, source_target_pairs={{0,16},{8,24},{16,0},{24,8},{1,17},{9,25},{17,1},{25,9},{2,18},{10... | collective-permute-start | bytes 196616 | tf_op jit(solution)/shard_map/ppermute | solution.py:265
  69.8 4.3 %collective-permute-start.13 = (f32[128,128]{1,0:T(8,128)S(1)}, f32[128,128]{1,0:T(8,128)S(1)}, u32[]{:S(2)}, u32[]{:S(2)}) collective-permute-start(f32[128,128]{1,0:T(8,128)S(1)} %get-tuple-element.74), channel_id=1, source_target_pairs={{0,8},{8,0},{16,24},{24,16},{1,9},{9,1},{17,25},{25,17},{2,10},{10... | collective-permute-start | bytes 196616 | tf_op jit(solution)/shard_map/ppermute | solution.py:265
  74.2 1.4 %collective-permute-start.16 = (f32[256,128]{1,0:T(8,128)S(1)}, f32[256,128]{1,0:T(8,128)S(1)}, u32[]{:S(2)}, u32[]{:S(2)}) collective-permute-start(f32[256,128]{1,0:T(8,128)S(1)} %bitcast.168), channel_id=1, source_target_pairs={{0,1},{1,0},{2,3},{3,2},{4,5},{5,4},{6,7},{7,6},{8,9},{9,8},{10,11... | collective-permute-start | bytes 393224 | tf_op jit(solution)/shard_map/ppermute | solution.py:259
  76.2 4.0 %collective-permute-start.17 = (f32[32,256]{1,0:T(8,128)S(1)}, f32[32,256]{1,0:T(8,128)S(1)}, u32[]{:S(2)}, u32[]{:S(2)}) collective-permute-start(f32[32,256]{1,0:T(8,128)S(1)} %get-tuple-element.76), channel_id=1, source_target_pairs={{0,2},{1,3},{2,0},{3,1},{4,6},{5,7},{6,4},{7,5},{8,10},{9,11},{10,... | collective-permute-start | bytes 98312 | tf_op jit(solution)/shard_map/ppermute | solution.py:268
  76.3 5.8 %collective-permute-start.19 = (f32[32,256]{1,0:T(8,128)S(1)}, f32[32,256]{1,0:T(8,128)S(1)}, u32[]{:S(2)}, u32[]{:S(2)}) collective-permute-start(f32[32,256]{1,0:T(8,128)S(1)} %get-tuple-element.77), channel_id=1, source_target_pairs={{0,6},{1,7},{2,4},{3,5},{4,2},{5,3},{6,0},{7,1},{8,14},{9,15},{10,... | collective-permute-start | bytes 98312 | tf_op jit(solution)/shard_map/ppermute | solution.py:268
  76.4 6.6 %collective-permute-start.18 = (f32[32,256]{1,0:T(8,128)S(1)}, f32[32,256]{1,0:T(8,128)S(1)}, u32[]{:S(2)}, u32[]{:S(2)}) collective-permute-start(f32[32,256]{1,0:T(8,128)S(1)} %get-tuple-element.78), channel_id=1, source_target_pairs={{0,4},{1,5},{2,6},{3,7},{4,0},{5,1},{6,2},{7,3},{8,12},{9,13},{10,... | collective-permute-start | bytes 98312 | tf_op jit(solution)/shard_map/ppermute | solution.py:268
  83.0 4.9 %collective-permute-start.22 = (f32[32,256]{1,0:T(8,128)S(1)}, f32[32,256]{1,0:T(8,128)S(1)}, u32[]{:S(2)}, u32[]{:S(2)}) collective-permute-start(f32[32,256]{1,0:T(8,128)S(1)} %add_add_fusion.2), channel_id=1, source_target_pairs={{0,24},{8,16},{16,8},{24,0},{1,25},{9,17},{17,9},{25,1},{2,26},{10... | collective-permute-start | bytes 98312 | tf_op jit(solution)/shard_map/ppermute | solution.py:265
  84.6 3.9 %collective-permute-start.21 = (f32[32,256]{1,0:T(8,128)S(1)}, f32[32,256]{1,0:T(8,128)S(1)}, u32[]{:S(2)}, u32[]{:S(2)}) collective-permute-start(f32[32,256]{1,0:T(8,128)S(1)} %add_add_fusion.2), channel_id=1, source_target_pairs={{0,16},{8,24},{16,0},{24,8},{1,17},{9,25},{17,1},{25,9},{2,18},{10... | collective-permute-start | bytes 98312 | tf_op jit(solution)/shard_map/ppermute | solution.py:265
  85.1 3.9 %collective-permute-start.20 = (f32[32,256]{1,0:T(8,128)S(1)}, f32[32,256]{1,0:T(8,128)S(1)}, u32[]{:S(2)}, u32[]{:S(2)}) collective-permute-start(f32[32,256]{1,0:T(8,128)S(1)} %add_add_fusion.2), channel_id=1, source_target_pairs={{0,8},{8,0},{16,24},{24,16},{1,9},{9,1},{17,25},{25,17},{2,10},{10... | collective-permute-start | bytes 98312 | tf_op jit(solution)/shard_map/ppermute | solution.py:265
  89.0 4.5 %collective-permute-start.23 = (f32[32,256]{1,0:T(8,128)S(1)}, f32[32,256]{1,0:T(8,128)S(1)}, u32[]{:S(2)}, u32[]{:S(2)}) collective-permute-start(f32[32,256]{1,0:T(8,128)S(1)} %get-tuple-element.65), channel_id=1, source_target_pairs={{0,2},{1,3},{2,0},{3,1},{4,6},{5,7},{6,4},{7,5},{8,10},{9,11},{10,... | collective-permute-start | bytes 98312 | tf_op jit(solution)/shard_map/ppermute | solution.py:268
  89.3 4.8 %collective-permute-start.24 = (f32[32,256]{1,0:T(8,128)S(1)}, f32[32,256]{1,0:T(8,128)S(1)}, u32[]{:S(2)}, u32[]{:S(2)}) collective-permute-start(f32[32,256]{1,0:T(8,128)S(1)} %get-tuple-element.65), channel_id=1, source_target_pairs={{0,4},{1,5},{2,6},{3,7},{4,0},{5,1},{6,2},{7,3},{8,12},{9,13},{10,... | collective-permute-start | bytes 98312 | tf_op jit(solution)/shard_map/ppermute | solution.py:268
  91.6 5.7 %collective-permute-start.25 = (f32[32,256]{1,0:T(8,128)S(1)}, f32[32,256]{1,0:T(8,128)S(1)}, u32[]{:S(2)}, u32[]{:S(2)}) collective-permute-start(f32[32,256]{1,0:T(8,128)S(1)} %get-tuple-element.65), channel_id=1, source_target_pairs={{0,6},{1,7},{2,4},{3,5},{4,2},{5,3},{6,0},{7,1},{8,14},{9,15},{10,... | collective-permute-start | bytes 98312 | tf_op jit(solution)/shard_map/ppermute | solution.py:268
  97.4 1.3 %collective-permute-start.26 = (f32[128,256]{1,0:T(8,128)S(1)}, f32[128,256]{1,0:T(8,128)S(1)}, u32[]{:S(2)}, u32[]{:S(2)}) collective-permute-start(f32[128,256]{1,0:T(8,128)S(1)} %constant_dynamic-update-slice_fusion.2), channel_id=1, source_target_pairs={{0,1},{1,0},{2,3},{3,2},{4,5},{5,4},{6,7},{7,6},{8,9},{9,8},{10,11... | collective-permute-start | bytes 393224 | tf_op jit(solution)/shard_map/ppermute | solution.py:259

commit v2 on v1

--- a/solution.py
+++ b/solution.py
@@ -35,10 +35,10 @@
     return both[:w] + (both[w:] + rest)
 
 
-def apply_to(rows, matrix):
-    w, n = rows.shape[0] // 2, rows.shape[1]
-    q = times(rows, matrix, NT)
-    return jnp.concatenate([q[:w, :n] - q[w:, n:], q[:w, n:] + q[w:, :n]], axis=0)
+def apply_to(rows, matrix, dims):
+    w = rows.shape[0] // 2
+    re, im = (times(rows, part, dims) for part in matrix)
+    return jnp.concatenate([re[:w] - im[w:], im[:w] + re[w:]], axis=0)
 
 
 def add_real(block, real):
@@ -50,8 +50,8 @@
     return pair[0][...], pair[1][...]
 
 
-def block_of(pair, role):
-    return pair[0][role], pair[1][role]
+def block_of(pair, *role):
+    return tuple((pair[0][(*role, part)], pair[1][(*role, part)]) for part in range(2))
 
 
 def write(pair, value):
@@ -72,13 +72,14 @@
 
 def enter_kernel(f_any, c_any, v_any, fh, fl, ch, cl, vt, g, f_buf, c_buf, v_buf, sems):
     n = c_buf.shape[0]
-    rows = f_buf.shape[0] // CHUNKS
+    per_part = CHUNKS // 2
+    rows = n // per_part
     v_copy = pltpu.make_async_copy(v_any, v_buf, sems.at[CHUNKS])
     v_copy.start()
     copies = []
-    for i in range(CHUNKS):
-        part = pl.ds(i * rows, rows)
-        copies.append(pltpu.make_async_copy(f_any.at[part], f_buf.at[part], sems.at[i]))
+    places = [(i // per_part, pl.ds(i % per_part * rows, rows)) for i in range(CHUNKS)]
+    for i, place in enumerate(places):
+        copies.append(pltpu.make_async_copy(f_any.at[place], f_buf.at[place], sems.at[i]))
         copies[-1].start()
     c_copy = pltpu.make_async_copy(c_any, c_buf, sems.at[CHUNKS + 1])
     c_copy.start()
@@ -86,12 +87,11 @@
     real = v_buf[...]
     vt[...] = real
     pieces = []
-    for i in range(CHUNKS):
-        part = pl.ds(i * rows, rows)
-        copies[i].wait()
-        high, low = parts_of(f_buf[part, :])
-        fh[part, :] = high
-        fl[part, :] = low
+    for copy, place in zip(copies, places):
+        copy.wait()
+        high, low = parts_of(f_buf[place])
+        fh[place] = high
+        fl[place] = low
         pieces.append(times(real, (high, low), NT))
     q = jnp.concatenate(pieces, axis=1)
     u = jnp.concatenate([q[:, :n], q[:, n:]], axis=0)
@@ -102,7 +102,7 @@
 
 def leave_kernel(vt, g, fh, fl, ch, cl, lo, hi):
     y = add_real(g[...], vt[...])
-    w = times(apply_to(y, read((fh, fl))), read((ch, cl)), NN)
+    w = times(apply_to(y, block_of((fh, fl)), NT), read((ch, cl)), NN)
     half = lo.shape[0] // 2
     width = 2 * half
     lo[...] = jnp.concatenate([w[:half], w[width : width + half]], axis=0)
@@ -116,37 +116,15 @@
     )
 
 
-def product_kernel(compute, *refs):
-    operands, (whole, buf, sem) = refs[:-3], refs[-3:]
-    buf[...] = compute(*operands)
-    copy = pltpu.make_async_copy(buf, whole, sem)
-    copy.start()
-    copy.wait()
-
-
-def product_in_place(compute, *refs):
-    refs[-1][...] = compute(*refs[:-1])
-
-
-def product(compute, shape, *operands):
-    return pl.pallas_call(
-        functools.partial(product_kernel, compute),
-        out_shape=pltpu.HBM(shape, F32),
-        in_specs=[VMEM] * len(operands),
-        out_specs=HBM,
-        scratch_shapes=[pltpu.VMEM(shape, F32), pltpu.SemaphoreType.DMA(())],
-        compiler_params=pltpu.CompilerParams(vmem_limit_bytes=20 << 20),
-    )(*[pltpu.with_memory_space_constraint(x, pltpu.VMEM) for x in operands])
-
-
-def a_part(index, fh, fl, ch, cl):
-    n = ch.shape[0]
-    part = pl.ds(index * n, n)
-    return pair_product((ch[...].T, cl[...].T), (fh[part, :], fl[part, :]), NN)
-
-
-def b_part(fh, fl, ch, cl):
-    return pair_product(read((fh, fl)), read((ch, cl)), NN)
+def a_kernel(index, fh, fl, ch, cl, out):
+    factor = (fh[index].T, fl[index].T)
+    out[...] = pair_product(factor, read((ch, cl)), NN)
+
+
+def b_kernel(fh, fl, ch, cl, out):
+    couple = (ch[...].T, cl[...].T)
+    for index in range(2):
+        out[index] = pair_product(couple, (fh[index], fl[index]), NT)
 
 
 def roles_kernel(count, *refs):
@@ -154,26 +132,24 @@
     high, low, buf, sems = refs[-4:]
     mine = lax.axis_index("row") % 2
     slots = (mine, 1 - mine)
-    rows = buf.shape[1] // CHUNKS
+    n = buf.shape[2]
+    rows = n // (CHUNKS // 2)
     copies = []
     for side in range(2):
-        start = 0
-        for source in sources[side]:
-            for i in range(source.shape[0] // rows):
+        halves = sources[side] if count == 2 else [sources[side][0].at[i] for i in range(2)]
+        for index, half in enumerate(halves):
+            for start in range(0, n, rows):
+                part = pl.ds(start, rows)
                 copy = pltpu.make_async_copy(
-                    source.at[pl.ds(i * rows, rows)],
-                    buf.at[side, pl.ds(start, rows)],
-                    sems.at[side, start // rows],
+                    half.at[part], buf.at[side, index, part], sems.at[side, len(copies) % CHUNKS]
                 )
                 copy.start()
-                copies.append((side, start, copy))
-                start += rows
-    for side, start, copy in copies:
+                copies.append((side, index, part, copy))
+    for side, index, part, copy in copies:
         copy.wait()
-        part = pl.ds(start, rows)
-        h, l = parts_of(buf[side, part, :])
-        high[slots[side], part, :] = h
-        low[slots[side], part, :] = l
+        h, l = parts_of(buf[side, index, part, :])
+        high[slots[side], index, part, :] = h
+        low[slots[side], index, part, :] = l
 
 
 def roles_and_vectors_kernel(count, *refs):
@@ -188,8 +164,8 @@
 
 
 def roles(owns, others, vectors=()):
-    n = others[0].shape[1]
-    shape = (2, 2 * n, n)
+    n = others[0].shape[-1]
+    shape = (2, 2, n, n)
     halves = [(v.shape[0] // 2, n) for v in vectors]
     body = roles_and_vectors_kernel if vectors else roles_kernel
     return pl.pallas_call(
@@ -212,25 +188,25 @@
     c = cs[0][...]
     for other in cs[1:]:
         c = c + other[...]
-    y = apply_to(add_real(c, va[...]), block_of((ah, al), 0))
-    out[...] = apply_to(add_real(y, vb[...]), block_of((ah, al), 1))
+    y = apply_to(add_real(c, va[...]), block_of((ah, al), 0), NN)
+    out[...] = apply_to(add_real(y, vb[...]), block_of((ah, al), 1), NN)
 
 
 def turn_kernel(c, va, vb, fh, fl, ah, al, bh, bl, ua, ub, s):
     y = add_real(c[...], va[...])
-    y_b = add_real(apply_to(y, block_of((ah, al), 0)), vb[...])
-    u_b = apply_to(y_b, block_of((fh, fl), 1))
-    u_a = apply_to(y, block_of((fh, fl), 0))
+    y_b = add_real(apply_to(y, block_of((ah, al), 0), NN), vb[...])
+    u_b = apply_to(y_b, block_of((fh, fl), 1), NT)
+    u_a = apply_to(y, block_of((fh, fl), 0), NT)
     ub[...] = u_b
     ua[...] = u_a
-    s[...] = u_a + apply_to(u_b, block_of((bh, bl), 0))
+    s[...] = u_a + apply_to(u_b, block_of((bh, bl), 0), NN)
 
 
 def backward_kernel(r, ua, ub, bh, bl, xa, *xb):
-    x_b = ub[...] + apply_to(r[...], block_of((bh, bl), 1))
+    x_b = ub[...] + apply_to(r[...], block_of((bh, bl), 1), NN)
     for out in xb:
         out[...] = x_b
-    xa[...] = ua[...] + apply_to(x_b, block_of((bh, bl), 0))
+    xa[...] = ua[...] + apply_to(x_b, block_of((bh, bl), 0), NN)
 
 
 def after(*values, every=False):
@@ -267,15 +243,15 @@
     def exchange_layer(value, d):
         return lax.ppermute(value, "row", [(r, r ^ (2 * d)) for r in range(rows)])
 
-    factor = inv_factors[0, 0].reshape(2 * n, n)
+    factor = inv_factors[0, 0]
     couple = coupling[0]
     block = ((2 * half, n), F32)
 
     fh, fl, ch, cl, v_t, g = pl.pallas_call(
         enter_kernel,
         out_shape=(
-            pltpu.VMEM((2 * n, n), BF16),
-            pltpu.VMEM((2 * n, n), BF16),
+            pltpu.VMEM((2, n, n), BF16),
+            pltpu.VMEM((2, n, n), BF16),
             pltpu.VMEM((n, n), BF16),
             pltpu.VMEM((n, n), BF16),
             pltpu.VMEM((width, n), F32),
@@ -284,7 +260,7 @@
         in_specs=[HBM] * 3,
         out_specs=(VMEM,) * 6,
         scratch_shapes=[
-            pltpu.VMEM((2 * n, n), F32),
+            pltpu.VMEM((2, n, n), F32),
             pltpu.VMEM((n, n), F32),
             pltpu.VMEM((width, n), F32),
             pltpu.SemaphoreType.DMA((CHUNKS + 2,)),
@@ -293,17 +269,14 @@
         name="enter",
     )(*[pltpu.with_memory_space_constraint(x, pltpu.HBM) for x in (factor, couple, vectors[0].T)])
     from_a = swap_core(g)
-    (a_re,) = call(
-        functools.partial(product_in_place, functools.partial(a_part, 0)),
-        [((n, n), F32)], after(fh, g), fl, ch, cl,
-    )
+    (a_re,) = call(functools.partial(a_kernel, 0), [((n, n), F32)], after(fh, g), fl, ch, cl)
     lo, hi = call(leave_kernel, [block, block], v_t, from_a, after(fh, from_a), fl, ch, cl)
 
     got_lo = lax.ppermute(lo, "row", [(1, 2)])
     got_hi = lax.ppermute(hi, "row", [(1, 3)])
     got = [got_lo, got_hi]
-    a_im = product(functools.partial(a_part, 1), (n, n), after(fh, lo), fl, ch, cl)
-    a_re_other = swap_core(after(a_re, lo))
+    (a_im,) = call(functools.partial(a_kernel, 1), [((n, n), F32)], after(fh, lo), fl, ch, cl)
+    a_re_other = swap_core(after(a_re, from_a))
     a_im_other = swap_core(a_im)
     v_other = swap_core(after(v_t, lo))
     va, vb, *a_mats = roles([a_re, a_im], [a_re_other, a_im_other], [v_t, v_other])
@@ -317,7 +290,7 @@
             (leaving,) = call(forward_kernel, [block], *got, va, vb, *a_mats)
         if t == 0:
             f_mats = roles([after(factor, leaving)], [f_other])
-            b_own = product(b_part, (2 * n, n), after(fh, leaving), fl, ch, cl)
+            (b_own,) = call(b_kernel, [((2, n, n), F32)], after(fh, leaving), fl, ch, cl)
             b_other = swap_core(b_own)
         if t == 1:
             b_mats = roles([after(b_own, leaving)], [b_other])
@@ -360,16 +333,15 @@
         mine[1], both[1], NT, precision=PREC
     )
     hc = groups * half
-    layer = lax.axis_index("row") // 2
-    gs = hc // layers
-    own = [lax.dynamic_slice_in_dim(gram, (layer ^ d) * gs, gs, 0) for d in range(layers)]
-    piece = tree_sum([own[0]] + [exchange_layer(own[d], d) for d in range(1, layers)])
-    piece = tree_sum([piece] + [exchange_node(piece, d) for d in range(1, nodes)])
+    gs = hc // nodes
+    own = [lax.dynamic_slice_in_dim(gram, (node ^ d) * gs, gs, 0) for d in range(nodes)]
+    piece = tree_sum([own[0]] + [exchange_node(own[d], d) for d in range(1, nodes)])
+    piece = tree_sum([piece] + [exchange_layer(piece, d) for d in range(1, layers)])
     piece = piece * (nodes / (rows * n))
-    got = [piece] + [exchange_layer(piece, d) for d in range(1, layers)]
+    got = [piece] + [exchange_node(piece, d) for d in range(1, nodes)]
     gram = jnp.zeros((hc, cols), F32)
-    for d in range(layers):
-        gram = lax.dynamic_update_slice_in_dim(gram, got[d], (layer ^ d) * gs, 0)
+    for d in range(nodes):
+        gram = lax.dynamic_update_slice_in_dim(gram, got[d], (node ^ d) * gs, 0)
     other = swap_core(gram)
     gram = gram.reshape(groups, half, cols)
     other = other.reshape(groups, half, cols)

time: 99.8 us -> 92.6 us (0.928)
  Pallas kernels: 26.7 us -> 20.9 us
  waiting for transfers between devices: 41.6 us -> 40.1 us
    ppermute x6 -> x3, waiting for transfers between devices: 7.1 us -> 1.89 us  [exchange_layer(): return lax.ppermute(value, 'row', [(r, r ^ 2 * d) for r in range(rows)])]
    pallas_call x3 -> x1, Pallas kernels: 8.42 us -> 3.27 us  [shards(): pl.pallas_call(enter_kernel, out_shape=(pltpu.VMEM((2, n, n), BF16), pltp...]
    ppermute x6 -> x9, waiting for transfers between devices: 4.87 us -> 8.64 us  [exchange_node(): return lax.ppermute(value, 'node', [(j, j ^ d) for j in range(nodes)])]
    ppermute x6 -> x9, starting transfers between devices: 7.11 us -> 10.7 us  [exchange_node(): return lax.ppermute(value, 'node', [(j, j ^ d) for j in range(nodes)])]
    ppermute x6 -> x3, starting transfers between devices: 7.99 us -> 4.45 us  [exchange_layer(): return lax.ppermute(value, 'row', [(r, r ^ 2 * d) for r in range(rows)])]
    pallas_call x8 -> x10, Pallas kernels: 12.2 us -> 11.5 us  [call(): pl.pallas_call(kernel, out_shape=tuple((pltpu.VMEM(shape, dtype) for shap...]
    unnamed x10 -> x14, local copies, waits for them, and re-layouts: 2.37 us -> 2.37 us
  transfers between devices with their start and end apart: 27 -> 27, of which waited for: 18 -> 18; matrix products, arithmetic and copies ran while one was open for 1% -> 1% of each run, Pallas kernels for 7% -> 6%
where the time goes in v2:
time: 92.6 us; the launch traced here: 92.3 us
  waiting for transfers between devices  40.1 us (43%)
  starting transfers between devices  24.9 us (27%)
  Pallas kernels  20.9 us (23%)
  local copies, waits for them, and re-layouts  2.48 us (3%)
  between operations  2.38 us (3%)
  other arithmetic  1.02 us (1%)
    ppermute x5, waiting for transfers between devices, hop(): lax.ppermute(value, 'row', [(2 * source + c, 2 * target + c) for c in ran...  23.1 us
    pallas_call x10, Pallas kernels, call(): pl.pallas_call(kernel, out_shape=tuple((pltpu.VMEM(shape, dtype) for shap...  11.5 us
    ppermute x9, starting transfers between devices, exchange_node(): return lax.ppermute(value, 'node', [(j, j ^ d) for j in range(nodes)])  10.7 us
    ppermute x9, waiting for transfers between devices, exchange_node(): return lax.ppermute(value, 'node', [(j, j ^ d) for j in range(nodes)])  8.64 us
    ppermute x8, waiting for transfers between devices, swap_core(): return lax.ppermute(value, 'row', [(r, r ^ 1) for r in range(rows)])  6.46 us
    pallas_call x3, Pallas kernels, roles(): pl.pallas_call(functools.partial(body, len(others)), out_shape=tuple((plt...  6.13 us
    ppermute x3, starting transfers between devices, exchange_layer(): return lax.ppermute(value, 'row', [(r, r ^ 2 * d) for r in range(rows)])  4.45 us
    ppermute x8, starting transfers between devices, swap_core(): return lax.ppermute(value, 'row', [(r, r ^ 1) for r in range(rows)])  4.3 us
  transfers between devices with their start and end apart: 27, of which 18 were waited for; matrix products, arithmetic and copies ran while one was open for 1% of the time, Pallas kernels for 6%

profile of v2, /device:TPU:0, one launch (start us, length us, event | category | flops | bytes accessed | tf_op | source)
XLA Modules:
  0.0 92.3 jit_solution(2193124548139649385)
XLA Ops:
  0.6 3.3 %enter.1 = (bf16[2,512,512]{2,1,0:T(8,128)(2,1)S(1)}, bf16[2,512,512]{2,1,0:T(8,128)(2,1)S(1)}, bf16[512,512]{1,0:T(8,128)(2,1)S(1)}, bf16[512,512]{1,0:T(8,128)...) custom-call(f32[2,512,512]{2,1,0:T(8,128)} %bitcast.146, f32[512,512]{1,0:T(8,128)} %bitcast.155, ...), custom_call_target="tpu_custom_call" | custom-call | tf_op jit(solution)/shard_map/enter/pallas_call | solution.py:250
  3.9 0.5 collective-permute-start
  4.5 1.0 %shard_map.51.refs_0_ = f32[512,512]{1,0:T(8,128)S(1)} custom-call(bf16[2,512,512]{2,1,0:T(8,128)(2,1)S(1)} %get-tuple-element.53.fh, bf16[2,512,512]{2,1,0:T(8,128)(2,1)S(1)} %get-tuple-element.36.fl, bf16[512,512]{1,0:T(8,128)(2,1)S(1)} %get-tuple-element.37.ch, bf16[512,512]{1,0:T(8,128)(2,1)S(1)} %get-tuple-element.38.cl), custom_call_target="tpu_custom_call" | custom-call | tf_op jit(solution)/shard_map/pallas_call | solution.py:64
  5.5 0.1 collective-permute-done.g
  5.6 1.1 %shard_map.50 = (f32[64,512]{1,0:T(8,128)S(1)}, f32[64,512]{1,0:T(8,128)S(1)}) custom-call(f32[64,512]{1,0:T(8,128)S(1)} %get-tuple-element.44.vt.refs_4_, f32[128,512]{1,0:T(8,128)S(1)} %collective-permute-done.g, bf16[2,512,512]{2,1,0:T(8,128)(2,1)S(1)} %get-tuple-element.53.fh, bf16[2,512,512]{2,1,0:T(8,128)(2,1)S(1)} %get-tuple-element.36.fl, ...), custom_call_target="tpu_custom_call" | custom-call | tf_op jit(solution)/shard_map/pallas_call | solution.py:64
  6.7 1.0 %shard_map.52.refs_1_ = f32[512,512]{1,0:T(8,128)S(1)} custom-call(bf16[2,512,512]{2,1,0:T(8,128)(2,1)S(1)} %get-tuple-element.53.fh, bf16[2,512,512]{2,1,0:T(8,128)(2,1)S(1)} %get-tuple-element.36.fl, bf16[512,512]{1,0:T(8,128)(2,1)S(1)} %get-tuple-element.37.ch, bf16[512,512]{1,0:T(8,128)(2,1)S(1)} %get-tuple-element.38.cl), custom_call_target="tpu_custom_call" | custom-call | tf_op jit(solution)/shard_map/pallas_call | solution.py:64
  7.7 0.4 collective-permute-start.3
  8.2 0.1 collective-permute-start.4
  8.3 0.4 collective-permute-start.5
  8.7 0.7 collective-permute-start.2
  9.3 0.7 collective-permute-start.1
  10.0 2.1 %collective-permute-done.5.refs_5_ = f32[64,512]{1,0:T(8,128)S(1)} collective-permute-done((f32[64,512]{1,0:T(8,128)S(1)}, f32[64,512]{1,0:T(8,128)S(1)}, u32[]{:S(2)}, u32[]{:S(2)}) %collective-permute-start.5) | collective-permute-done | bytes 131104 | tf_op jit(solution)/shard_map/ppermute | solution.py:235
  12.1 2.1 %shard_map.53 = (f32[32,512]{1,0:T(8,128)S(1)}, f32[32,512]{1,0:T(8,128)S(1)}, bf16[2,2,512,512]{3,2,1,0:T(8,128)(2,1)S(1)}, bf16[2,2,512,512]{3,2,1,0:T(8,128)(2,1)S(1)}) custom-call(f32[512,512]{1,0:T(8,128)} %copy-done.3, f32[512,512]{1,0:T(8,128)} %copy-done.4, f32[512,512]{1,0:T(8,128)S(1)} %collective-permute-done.3.refs_2_, ...), custom_call_target="tpu_custom_call" | custom-call | tf_op jit(solution)/shard_map/pallas_call | solution.py:171
  14.2 0.9 shard_map.54
  15.1 0.0 copy-start.5
  15.1 1.8 %shard_map.57.refs_0_ = f32[2,512,512]{2,1,0:T(8,128)S(1)} custom-call(bf16[2,512,512]{2,1,0:T(8,128)(2,1)S(1)} %get-tuple-element.53.fh, bf16[2,512,512]{2,1,0:T(8,128)(2,1)S(1)} %get-tuple-element.36.fl, bf16[512,512]{1,0:T(8,128)(2,1)S(1)} %get-tuple-element.37.ch, bf16[512,512]{1,0:T(8,128)(2,1)S(1)} %get-tuple-element.38.cl), custom_call_target="tpu_custom_call" | custom-call | tf_op jit(solution)/shard_map/pallas_call | solution.py:64
  17.0 2.6 %collective-permute-start.9 = (f32[2,512,512]{2,1,0:T(8,128)S(1)}, f32[2,512,512]{2,1,0:T(8,128)S(1)}, u32[]{:S(2)}, u32[]{:S(2)}) collective-permute-start(f32[2,512,512]{2,1,0:T(8,128)S(1)} %shard_map.57.refs_0_), channel_id=1, source_target_pairs={{0,1},{1,0},{2,3},{3,2},{4,5},{5,4},{6,7},{7,6},{8,9},{9,8},{10,11... | collective-permute-start | bytes 6291464 | tf_op jit(solution)/shard_map/ppermute | solution.py:235
  19.6 0.1 collective-permute-start.8
  19.7 0.7 collective-permute-start.6
  20.4 0.9 shard_map.55
  21.3 0.7 collective-permute-start.7
  22.0 1.4 %collective-permute-done.9.refs_1_ = f32[2,512,512]{2,1,0:T(8,128)S(1)} collective-permute-done((f32[2,512,512]{2,1,0:T(8,128)S(1)}, f32[2,512,512]{2,1,0:T(8,128)S(1)}, u32[]{:S(2)}, u32[]{:S(2)}) %collective-permute-start.9) | collective-permute-done | bytes 2097184 | tf_op jit(solution)/shard_map/ppermute | solution.py:235
  23.4 2.0 %shard_map.58 = (bf16[2,2,512,512]{3,2,1,0:T(8,128)(2,1)S(1)}, bf16[2,2,512,512]{3,2,1,0:T(8,128)(2,1)S(1)}) custom-call(f32[2,512,512]{2,1,0:T(8,128)} %copy-done.2, f32[2,512,512]{2,1,0:T(8,128)S(1)} %collective-permute-done.9.refs_1_), custom_call_target="tpu_custom_call" | custom-call | tf_op jit(solution)/shard_map/pallas_call | solution.py:171
  25.5 0.9 %collective-permute-done.8.refs_1_ = f32[2,512,512]{2,1,0:T(8,128)S(1)} collective-permute-done((f32[2,512,512]{2,1,0:T(8,128)S(1)}, f32[2,512,512]{2,1,0:T(8,128)S(1)}, u32[]{:S(2)}, u32[]{:S(2)}) %collective-permute-start.8) | collective-permute-done | bytes 2097184 | tf_op jit(solution)/shard_map/ppermute | solution.py:235
  26.4 2.0 %shard_map.56 = (bf16[2,2,512,512]{3,2,1,0:T(8,128)(2,1)S(1)}, bf16[2,2,512,512]{3,2,1,0:T(8,128)(2,1)S(1)}) custom-call(f32[2,512,512]{2,1,0:T(8,128)} %bitcast.147, f32[2,512,512]{2,1,0:T(8,128)S(1)} %collective-permute-done.8.refs_1_), custom_call_target="tpu_custom_call" | custom-call | tf_op jit(solution)/shard_map/pallas_call | solution.py:171
  28.5 2.1 %shard_map.59 = (f32[64,512]{1,0:T(8,128)S(1)}, f32[64,512]{1,0:T(8,128)S(1)}, f32[64,512]{1,0:T(8,128)S(1)}) custom-call(f32[64,512]{1,0:T(8,128)S(1)} %add_add_fusion.1.c, f32[32,512]{1,0:T(8,128)S(1)} %get-tuple-element.45.refs_2_.refs_1_.va, f32[32,512]{1,0:T(8,128)S(1)} %get-tuple-element.46.refs_3_.refs_2_.vb, ...), custom_call_target="tpu_custom_call" | custom-call | tf_op jit(solution)/shard_map/pallas_call | solution.py:64
  30.6 0.7 collective-permute-start.10
  31.3 0.9 shard_map.60
  32.2 0.7 collective-permute-start.11
  32.9 0.9 shard_map.61
  33.8 1.5 %collective-permute-start.12 = (f32[64,512]{1,0:T(8,128)S(1)}, f32[64,512]{1,0:T(8,128)S(1)}, u32[]{:S(2)}, u32[]{:S(2)}) collective-permute-start(f32[64,512]{1,0:T(8,128)S(1)} %shard_map.61), channel_id=1, source_target_pairs={{2,0},{3,1},{10,8},{11,9},{18,16},{19,17},{26,24},{27,25}} | collective-permute-start | bytes 393224 | tf_op jit(solution)/shard_map/ppermute | solution.py:238
  35.3 23.1 %collective-permute-done.12 = f32[64,512]{1,0:T(8,128)S(1)} collective-permute-done((f32[64,512]{1,0:T(8,128)S(1)}, f32[64,512]{1,0:T(8,128)S(1)}, u32[]{:S(2)}, u32[]{:S(2)}) %collective-permute-start.12) | collective-permute-done | bytes 131104 | tf_op jit(solution)/shard_map/ppermute | solution.py:238
  58.5 1.6 %copy-done.1 = bf16[2,2,512,512]{3,2,1,0:T(8,128)(2,1)S(1)} copy-done((bf16[2,2,512,512]{3,2,1,0:T(8,128)(2,1)S(1)}, bf16[2,2,512,512]{3,2,1,0:T(8,128)(2,1)}, u32[]{:S(2)}) %copy-start.1) | copy-done | bytes 2097176
  60.1 0.9 shard_map.62
  61.1 2.5 %collective-permute-start.15 = (f32[128,128]{1,0:T(8,128)S(1)}, f32[128,128]{1,0:T(8,128)S(1)}, u32[]{:S(2)}, u32[]{:S(2)}) collective-permute-start(f32[128,128]{1,0:T(8,128)S(1)} %get-tuple-element.72), channel_id=1, source_target_pairs={{0,24},{8,16},{16,8},{24,0},{1,25},{9,17},{17,9},{25,1},{2,26},{10... | collective-permute-start | bytes 196616 | tf_op jit(solution)/shard_map/ppermute | solution.py:241
  63.6 0.5 collective-permute-start.14
  64.1 0.5 collective-permute-start.13
  65.9 0.4 collective-permute-done.15
  66.3 1.5 %collective-permute-done.14 = f32[128,128]{1,0:T(8,128)S(1)} collective-permute-done((f32[128,128]{1,0:T(8,128)S(1)}, f32[128,128]{1,0:T(8,128)S(1)}, u32[]{:S(2)}, u32[]{:S(2)}) %collective-permute-start.14) | collective-permute-done | bytes 65568 | tf_op jit(solution)/shard_map/ppermute | solution.py:241
  67.8 0.5 collective-permute-done.13
  68.5 0.1 collective-permute-start.16
  68.6 1.3 %collective-permute-done.16 = f32[256,128]{1,0:T(8,128)S(1)} collective-permute-done((f32[256,128]{1,0:T(8,128)S(1)}, f32[256,128]{1,0:T(8,128)S(1)}, u32[]{:S(2)}, u32[]{:S(2)}) %collective-permute-start.16) | collective-permute-done | bytes 131104 | tf_op jit(solution)/shard_map/ppermute | solution.py:235
  70.0 0.2 fusion.10
  70.2 0.2 convolution_add_fusion
  70.5 0.6 collective-permute-start.17
  71.1 2.4 %collective-permute-start.19 = (f32[32,256]{1,0:T(8,128)S(1)}, f32[32,256]{1,0:T(8,128)S(1)}, u32[]{:S(2)}, u32[]{:S(2)}) collective-permute-start(f32[32,256]{1,0:T(8,128)S(1)} %get-tuple-element.77), channel_id=1, source_target_pairs={{0,24},{8,16},{16,8},{24,0},{1,25},{9,17},{17,9},{25,1},{2,26},{10... | collective-permute-start | bytes 98312 | tf_op jit(solution)/shard_map/ppermute | solution.py:241
  73.5 0.5 collective-permute-start.18
  74.0 0.4 collective-permute-done.17
  74.5 1.5 %collective-permute-done.19 = f32[32,256]{1,0:T(8,128)S(1)} collective-permute-done((f32[32,256]{1,0:T(8,128)S(1)}, f32[32,256]{1,0:T(8,128)S(1)}, u32[]{:S(2)}, u32[]{:S(2)}) %collective-permute-start.19) | collective-permute-done | bytes 32800 | tf_op jit(solution)/shard_map/ppermute | solution.py:241
  75.9 1.5 %collective-permute-done.18 = f32[32,256]{1,0:T(8,128)S(1)} collective-permute-done((f32[32,256]{1,0:T(8,128)S(1)}, f32[32,256]{1,0:T(8,128)S(1)}, u32[]{:S(2)}, u32[]{:S(2)}) %collective-permute-start.18) | collective-permute-done | bytes 32800 | tf_op jit(solution)/shard_map/ppermute | solution.py:241
  77.4 0.1 collective-permute-start.22
  77.5 1.0 %collective-permute-start.21 = (f32[32,256]{1,0:T(8,128)S(1)}, f32[32,256]{1,0:T(8,128)S(1)}, u32[]{:S(2)}, u32[]{:S(2)}) collective-permute-start(f32[32,256]{1,0:T(8,128)S(1)} %add_add_fusion.2), channel_id=1, source_target_pairs={{0,4},{1,5},{2,6},{3,7},{4,0},{5,1},{6,2},{7,3},{8,12},{9,13},{10,... | collective-permute-start | bytes 98312 | tf_op jit(solution)/shard_map/ppermute | solution.py:244
  78.6 3.3 %collective-permute-start.20 = (f32[32,256]{1,0:T(8,128)S(1)}, f32[32,256]{1,0:T(8,128)S(1)}, u32[]{:S(2)}, u32[]{:S(2)}) collective-permute-start(f32[32,256]{1,0:T(8,128)S(1)} %add_add_fusion.2), channel_id=1, source_target_pairs={{0,2},{1,3},{2,0},{3,1},{4,6},{5,7},{6,4},{7,5},{8,10},{9,11},{10,... | collective-permute-start | bytes 98312 | tf_op jit(solution)/shard_map/ppermute | solution.py:244
  81.9 1.3 %collective-permute-done.22 = f32[32,256]{1,0:T(8,128)S(1)} collective-permute-done((f32[32,256]{1,0:T(8,128)S(1)}, f32[32,256]{1,0:T(8,128)S(1)}, u32[]{:S(2)}, u32[]{:S(2)}) %collective-permute-start.22) | collective-permute-done | bytes 32800 | tf_op jit(solution)/shard_map/ppermute | solution.py:244
  83.2 0.6 collective-permute-done.20
  83.8 0.6 collective-permute-start.23
  84.4 0.9 %collective-permute-start.24 = (f32[32,256]{1,0:T(8,128)S(1)}, f32[32,256]{1,0:T(8,128)S(1)}, u32[]{:S(2)}, u32[]{:S(2)}) collective-permute-start(f32[32,256]{1,0:T(8,128)S(1)} %get-tuple-element.65), channel_id=1, source_target_pairs={{0,16},{8,24},{16,0},{24,8},{1,17},{9,25},{17,1},{25,9},{2,18},{10... | collective-permute-start | bytes 98312 | tf_op jit(solution)/shard_map/ppermute | solution.py:241
  85.4 2.0 %collective-permute-start.25 = (f32[32,256]{1,0:T(8,128)S(1)}, f32[32,256]{1,0:T(8,128)S(1)}, u32[]{:S(2)}, u32[]{:S(2)}) collective-permute-start(f32[32,256]{1,0:T(8,128)S(1)} %get-tuple-element.65), channel_id=1, source_target_pairs={{0,24},{8,16},{16,8},{24,0},{1,25},{9,17},{17,9},{25,1},{2,26},{10... | collective-permute-start | bytes 98312 | tf_op jit(solution)/shard_map/ppermute | solution.py:241
  87.4 0.4 collective-permute-done.23
  87.8 0.5 collective-permute-done.24
  88.4 1.8 %collective-permute-done.25 = f32[32,256]{1,0:T(8,128)S(1)} collective-permute-done((f32[32,256]{1,0:T(8,128)S(1)}, f32[32,256]{1,0:T(8,128)S(1)}, u32[]{:S(2)}, u32[]{:S(2)}) %collective-permute-start.25) | collective-permute-done | bytes 32800 | tf_op jit(solution)/shard_map/ppermute | solution.py:241
  90.2 0.8 copy.43
  91.0 0.6 collective-permute-done.26
  91.6 0.7 pad_maximum_fusion
  (42 shorter events, 0.5 us)
Async XLA Ops:
  3.9 1.7 %collective-permute-start = (f32[128,512]{1,0:T(8,128)S(1)}, f32[128,512]{1,0:T(8,128)S(1)}, u32[]{:S(2)}, u32[]{:S(2)}) collective-permute-start(f32[128,512]{1,0:T(8,128)S(1)} %get-tuple-element.33), channel_id=1, source_target_pairs={{0,1},{1,0},{2,3},{3,2},{4,5},{5,4},{6,7},{7,6},{8,9},{9,8},{10,11... | collective-permute-start | bytes 786440 | tf_op jit(solution)/shard_map/ppermute | solution.py:235
  5.5 2.2 %copy-start.3 = (f32[512,512]{1,0:T(8,128)}, f32[512,512]{1,0:T(8,128)S(1)}, u32[]{:S(2)}) copy-start(f32[512,512]{1,0:T(8,128)S(1)} %shard_map.51.refs_0_) | copy-start | bytes 3145732
  7.7 4.4 %copy-start.4 = (f32[512,512]{1,0:T(8,128)}, f32[512,512]{1,0:T(8,128)S(1)}, u32[]{:S(2)}) copy-start(f32[512,512]{1,0:T(8,128)S(1)} %shard_map.52.refs_1_) | copy-start | bytes 3145732
  7.7 4.4 %collective-permute-start.3 = (f32[512,512]{1,0:T(8,128)S(1)}, f32[512,512]{1,0:T(8,128)S(1)}, u32[]{:S(2)}, u32[]{:S(2)}) collective-permute-start(f32[512,512]{1,0:T(8,128)S(1)} %shard_map.51.refs_0_), channel_id=1, source_target_pairs={{0,1},{1,0},{2,3},{3,2},{4,5},{5,4},{6,7},{7,6},{8,9},{9,8},{10,11... | collective-permute-start | bytes 3145736 | tf_op jit(solution)/shard_map/ppermute | solution.py:235
  8.2 4.0 %collective-permute-start.4 = (f32[512,512]{1,0:T(8,128)S(1)}, f32[512,512]{1,0:T(8,128)S(1)}, u32[]{:S(2)}, u32[]{:S(2)}) collective-permute-start(f32[512,512]{1,0:T(8,128)S(1)} %shard_map.52.refs_1_), channel_id=1, source_target_pairs={{0,1},{1,0},{2,3},{3,2},{4,5},{5,4},{6,7},{7,6},{8,9},{9,8},{10,11... | collective-permute-start | bytes 3145736 | tf_op jit(solution)/shard_map/ppermute | solution.py:235
  8.3 3.8 %collective-permute-start.5 = (f32[64,512]{1,0:T(8,128)S(1)}, f32[64,512]{1,0:T(8,128)S(1)}, u32[]{:S(2)}, u32[]{:S(2)}) collective-permute-start(f32[64,512]{1,0:T(8,128)S(1)} %get-tuple-element.44.vt.refs_4_), channel_id=1, source_target_pairs={{0,1},{1,0},{2,3},{3,2},{4,5},{5,4},{6,7},{7,6},{8,9},{9,8},{10,11... | collective-permute-start | bytes 393224 | tf_op jit(solution)/shard_map/ppermute | solution.py:235
  8.7 5.5 %collective-permute-start.2 = (f32[64,512]{1,0:T(8,128)S(1)}, f32[64,512]{1,0:T(8,128)S(1)}, u32[]{:S(2)}, u32[]{:S(2)}) collective-permute-start(f32[64,512]{1,0:T(8,128)S(1)} %get-tuple-element.40), channel_id=1, source_target_pairs={{1,3},{9,11},{17,19},{25,27}} | collective-permute-start | bytes 393224 | tf_op jit(solution)/shard_map/ppermute | solution.py:276
  9.3 4.9 %collective-permute-start.1 = (f32[64,512]{1,0:T(8,128)S(1)}, f32[64,512]{1,0:T(8,128)S(1)}, u32[]{:S(2)}, u32[]{:S(2)}) collective-permute-start(f32[64,512]{1,0:T(8,128)S(1)} %get-tuple-element.39), channel_id=1, source_target_pairs={{1,2},{9,10},{17,18},{25,26}} | collective-permute-start | bytes 393224 | tf_op jit(solution)/shard_map/ppermute | solution.py:275
  15.1 4.5 %copy-start.5 = (f32[1,1,2,512,512]{4,3,2,1,0:T(8,128)S(1)}, f32[1,1,2,512,512]{4,3,2,1,0:T(8,128)}, u32[]{:S(2)}) copy-start(f32[1,1,2,512,512]{4,3,2,1,0:T(8,128)} %param.3) | copy-start | bytes 6291460
  17.0 4.3 %copy-start.2 = (f32[2,512,512]{2,1,0:T(8,128)}, f32[2,512,512]{2,1,0:T(8,128)S(1)}, u32[]{:S(2)}) copy-start(f32[2,512,512]{2,1,0:T(8,128)S(1)} %shard_map.57.refs_0_) | copy-start | bytes 6291460
  17.0 6.4 %collective-permute-start.9 = (f32[2,512,512]{2,1,0:T(8,128)S(1)}, f32[2,512,512]{2,1,0:T(8,128)S(1)}, u32[]{:S(2)}, u32[]{:S(2)}) collective-permute-start(f32[2,512,512]{2,1,0:T(8,128)S(1)} %shard_map.57.refs_0_), channel_id=1, source_target_pairs={{0,1},{1,0},{2,3},{3,2},{4,5},{5,4},{6,7},{7,6},{8,9},{9,8},{10,11... | collective-permute-start | bytes 6291464 | tf_op jit(solution)/shard_map/ppermute | solution.py:235
  19.6 6.8 %collective-permute-start.8 = (f32[2,512,512]{2,1,0:T(8,128)S(1)}, f32[2,512,512]{2,1,0:T(8,128)S(1)}, u32[]{:S(2)}, u32[]{:S(2)}) collective-permute-start(f32[2,512,512]{2,1,0:T(8,128)S(1)} %bitcast.148), channel_id=1, source_target_pairs={{0,1},{1,0},{2,3},{3,2},{4,5},{5,4},{6,7},{7,6},{8,9},{9,8},{10,11... | collective-permute-start | bytes 6291464 | tf_op jit(solution)/shard_map/ppermute | solution.py:235
  19.7 0.7 collective-permute-start.6
  21.3 0.7 collective-permute-start.7
  25.5 7.4 %copy-start = (bf16[2,2,512,512]{3,2,1,0:T(8,128)(2,1)}, bf16[2,2,512,512]{3,2,1,0:T(8,128)(2,1)S(1)}, u32[]{:S(2)}) copy-start(bf16[2,2,512,512]{3,2,1,0:T(8,128)(2,1)S(1)} %get-tuple-element.56.bl) | copy-start | bytes 6291460
  30.6 0.7 collective-permute-start.10
  32.2 0.7 collective-permute-start.11
  33.8 24.6 %collective-permute-start.12 = (f32[64,512]{1,0:T(8,128)S(1)}, f32[64,512]{1,0:T(8,128)S(1)}, u32[]{:S(2)}, u32[]{:S(2)}) collective-permute-start(f32[64,512]{1,0:T(8,128)S(1)} %shard_map.61), channel_id=1, source_target_pairs={{2,0},{3,1},{10,8},{11,9},{18,16},{19,17},{26,24},{27,25}} | collective-permute-start | bytes 393224 | tf_op jit(solution)/shard_map/ppermute | solution.py:238
  58.5 1.6 %copy-start.1 = (bf16[2,2,512,512]{3,2,1,0:T(8,128)(2,1)S(1)}, bf16[2,2,512,512]{3,2,1,0:T(8,128)(2,1)}, u32[]{:S(2)}) copy-start(bf16[2,2,512,512]{3,2,1,0:T(8,128)(2,1)} %copy-done) | copy-start | bytes 6291460
  61.1 5.2 %collective-permute-start.15 = (f32[128,128]{1,0:T(8,128)S(1)}, f32[128,128]{1,0:T(8,128)S(1)}, u32[]{:S(2)}, u32[]{:S(2)}) collective-permute-start(f32[128,128]{1,0:T(8,128)S(1)} %get-tuple-element.72), channel_id=1, source_target_pairs={{0,24},{8,16},{16,8},{24,0},{1,25},{9,17},{17,9},{25,1},{2,26},{10... | collective-permute-start | bytes 196616 | tf_op jit(solution)/shard_map/ppermute | solution.py:241
  63.6 4.3 %collective-permute-start.14 = (f32[128,128]{1,0:T(8,128)S(1)}, f32[128,128]{1,0:T(8,128)S(1)}, u32[]{:S(2)}, u32[]{:S(2)}) collective-permute-start(f32[128,128]{1,0:T(8,128)S(1)} %get-tuple-element.73), channel_id=1, source_target_pairs={{0,16},{8,24},{16,0},{24,8},{1,17},{9,25},{17,1},{25,9},{2,18},{10... | collective-permute-start | bytes 196616 | tf_op jit(solution)/shard_map/ppermute | solution.py:241
  64.1 4.3 %collective-permute-start.13 = (f32[128,128]{1,0:T(8,128)S(1)}, f32[128,128]{1,0:T(8,128)S(1)}, u32[]{:S(2)}, u32[]{:S(2)}) collective-permute-start(f32[128,128]{1,0:T(8,128)S(1)} %get-tuple-element.74), channel_id=1, source_target_pairs={{0,8},{8,0},{16,24},{24,16},{1,9},{9,1},{17,25},{25,17},{2,10},{10... | collective-permute-start | bytes 196616 | tf_op jit(solution)/shard_map/ppermute | solution.py:241
  68.5 1.4 %collective-permute-start.16 = (f32[256,128]{1,0:T(8,128)S(1)}, f32[256,128]{1,0:T(8,128)S(1)}, u32[]{:S(2)}, u32[]{:S(2)}) collective-permute-start(f32[256,128]{1,0:T(8,128)S(1)} %bitcast.168), channel_id=1, source_target_pairs={{0,1},{1,0},{2,3},{3,2},{4,5},{5,4},{6,7},{7,6},{8,9},{9,8},{10,11... | collective-permute-start | bytes 393224 | tf_op jit(solution)/shard_map/ppermute | solution.py:235
  70.5 4.0 %collective-permute-start.17 = (f32[32,256]{1,0:T(8,128)S(1)}, f32[32,256]{1,0:T(8,128)S(1)}, u32[]{:S(2)}, u32[]{:S(2)}) collective-permute-start(f32[32,256]{1,0:T(8,128)S(1)} %get-tuple-element.76), channel_id=1, source_target_pairs={{0,8},{8,0},{16,24},{24,16},{1,9},{9,1},{17,25},{25,17},{2,10},{10... | collective-permute-start | bytes 98312 | tf_op jit(solution)/shard_map/ppermute | solution.py:241
  71.1 4.8 %collective-permute-start.19 = (f32[32,256]{1,0:T(8,128)S(1)}, f32[32,256]{1,0:T(8,128)S(1)}, u32[]{:S(2)}, u32[]{:S(2)}) collective-permute-start(f32[32,256]{1,0:T(8,128)S(1)} %get-tuple-element.77), channel_id=1, source_target_pairs={{0,24},{8,16},{16,8},{24,0},{1,25},{9,17},{17,9},{25,1},{2,26},{10... | collective-permute-start | bytes 98312 | tf_op jit(solution)/shard_map/ppermute | solution.py:241
  73.5 3.9 %collective-permute-start.18 = (f32[32,256]{1,0:T(8,128)S(1)}, f32[32,256]{1,0:T(8,128)S(1)}, u32[]{:S(2)}, u32[]{:S(2)}) collective-permute-start(f32[32,256]{1,0:T(8,128)S(1)} %get-tuple-element.78), channel_id=1, source_target_pairs={{0,16},{8,24},{16,0},{24,8},{1,17},{9,25},{17,1},{25,9},{2,18},{10... | collective-permute-start | bytes 98312 | tf_op jit(solution)/shard_map/ppermute | solution.py:241
  77.4 5.8 %collective-permute-start.22 = (f32[32,256]{1,0:T(8,128)S(1)}, f32[32,256]{1,0:T(8,128)S(1)}, u32[]{:S(2)}, u32[]{:S(2)}) collective-permute-start(f32[32,256]{1,0:T(8,128)S(1)} %add_add_fusion.2), channel_id=1, source_target_pairs={{0,6},{1,7},{2,4},{3,5},{4,2},{5,3},{6,0},{7,1},{8,14},{9,15},{10,... | collective-permute-start | bytes 98312 | tf_op jit(solution)/shard_map/ppermute | solution.py:244
  77.5 5.7 %collective-permute-start.21 = (f32[32,256]{1,0:T(8,128)S(1)}, f32[32,256]{1,0:T(8,128)S(1)}, u32[]{:S(2)}, u32[]{:S(2)}) collective-permute-start(f32[32,256]{1,0:T(8,128)S(1)} %add_add_fusion.2), channel_id=1, source_target_pairs={{0,4},{1,5},{2,6},{3,7},{4,0},{5,1},{6,2},{7,3},{8,12},{9,13},{10,... | collective-permute-start | bytes 98312 | tf_op jit(solution)/shard_map/ppermute | solution.py:244
  78.6 5.2 %collective-permute-start.20 = (f32[32,256]{1,0:T(8,128)S(1)}, f32[32,256]{1,0:T(8,128)S(1)}, u32[]{:S(2)}, u32[]{:S(2)}) collective-permute-start(f32[32,256]{1,0:T(8,128)S(1)} %add_add_fusion.2), channel_id=1, source_target_pairs={{0,2},{1,3},{2,0},{3,1},{4,6},{5,7},{6,4},{7,5},{8,10},{9,11},{10,... | collective-permute-start | bytes 98312 | tf_op jit(solution)/shard_map/ppermute | solution.py:244
  83.8 4.0 %collective-permute-start.23 = (f32[32,256]{1,0:T(8,128)S(1)}, f32[32,256]{1,0:T(8,128)S(1)}, u32[]{:S(2)}, u32[]{:S(2)}) collective-permute-start(f32[32,256]{1,0:T(8,128)S(1)} %get-tuple-element.65), channel_id=1, source_target_pairs={{0,8},{8,0},{16,24},{24,16},{1,9},{9,1},{17,25},{25,17},{2,10},{10... | collective-permute-start | bytes 98312 | tf_op jit(solution)/shard_map/ppermute | solution.py:241
  84.4 3.9 %collective-permute-start.24 = (f32[32,256]{1,0:T(8,128)S(1)}, f32[32,256]{1,0:T(8,128)S(1)}, u32[]{:S(2)}, u32[]{:S(2)}) collective-permute-start(f32[32,256]{1,0:T(8,128)S(1)} %get-tuple-element.65), channel_id=1, source_target_pairs={{0,16},{8,24},{16,0},{24,8},{1,17},{9,25},{17,1},{25,9},{2,18},{10... | collective-permute-start | bytes 98312 | tf_op jit(solution)/shard_map/ppermute | solution.py:241
  85.4 4.8 %collective-permute-start.25 = (f32[32,256]{1,0:T(8,128)S(1)}, f32[32,256]{1,0:T(8,128)S(1)}, u32[]{:S(2)}, u32[]{:S(2)}) collective-permute-start(f32[32,256]{1,0:T(8,128)S(1)} %get-tuple-element.65), channel_id=1, source_target_pairs={{0,24},{8,16},{16,8},{24,0},{1,25},{9,17},{17,9},{25,1},{2,26},{10... | collective-permute-start | bytes 98312 | tf_op jit(solution)/shard_map/ppermute | solution.py:241
  90.2 1.3 %collective-permute-start.26 = (f32[128,256]{1,0:T(8,128)S(1)}, f32[128,256]{1,0:T(8,128)S(1)}, u32[]{:S(2)}, u32[]{:S(2)}) collective-permute-start(f32[128,256]{1,0:T(8,128)S(1)} %constant_dynamic-update-slice_fusion.2), channel_id=1, source_target_pairs={{0,1},{1,0},{2,3},{3,2},{4,5},{5,4},{6,7},{7,6},{8,9},{9,8},{10,11... | collective-permute-start | bytes 393224 | tf_op jit(solution)/shard_map/ppermute | solution.py:235

commit v3 on v2

--- a/solution.py
+++ b/solution.py
@@ -11,13 +11,13 @@
 
 
 MOM = 2
-PREC = lax.Precision.HIGH
 F32, BF16 = jnp.float32, jnp.bfloat16
 NN = (((1,), (0,)), ((), ()))
 NT = (((1,), (1,)), ((), ()))
 VMEM = pl.BlockSpec(memory_space=pltpu.VMEM)
 HBM = pl.BlockSpec(memory_space=pltpu.HBM)
 CHUNKS = 4
+ENTER_CHUNKS = 2
 
 
 def parts_of(x):
@@ -50,8 +50,8 @@
     return pair[0][...], pair[1][...]
 
 
-def block_of(pair, *role):
-    return tuple((pair[0][(*role, part)], pair[1][(*role, part)]) for part in range(2))
+def block_of(mats, role):
+    return tuple((mats[0, role, part], mats[1, role, part]) for part in range(2))
 
 
 def write(pair, value):
@@ -60,28 +60,29 @@
     pair[1][...] = low
 
 
-def call(kernel, outs, *operands):
+def call(kernel, outs, *operands, scratch=()):
     return pl.pallas_call(
         kernel,
         out_shape=tuple(pltpu.VMEM(shape, dtype) for shape, dtype in outs),
         in_specs=[VMEM] * len(operands),
         out_specs=tuple([VMEM] * len(outs)),
+        scratch_shapes=[pltpu.VMEM(shape, dtype) for shape, dtype in scratch],
         compiler_params=pltpu.CompilerParams(vmem_limit_bytes=20 << 20),
     )(*[pltpu.with_memory_space_constraint(x, pltpu.VMEM) for x in operands])
 
 
 def enter_kernel(f_any, c_any, v_any, fh, fl, ch, cl, vt, g, f_buf, c_buf, v_buf, sems):
     n = c_buf.shape[0]
-    per_part = CHUNKS // 2
+    per_part = ENTER_CHUNKS // 2
     rows = n // per_part
-    v_copy = pltpu.make_async_copy(v_any, v_buf, sems.at[CHUNKS])
+    v_copy = pltpu.make_async_copy(v_any, v_buf, sems.at[ENTER_CHUNKS])
     v_copy.start()
     copies = []
-    places = [(i // per_part, pl.ds(i % per_part * rows, rows)) for i in range(CHUNKS)]
+    places = [(i // per_part, pl.ds(i % per_part * rows, rows)) for i in range(ENTER_CHUNKS)]
     for i, place in enumerate(places):
         copies.append(pltpu.make_async_copy(f_any.at[place], f_buf.at[place], sems.at[i]))
         copies[-1].start()
-    c_copy = pltpu.make_async_copy(c_any, c_buf, sems.at[CHUNKS + 1])
+    c_copy = pltpu.make_async_copy(c_any, c_buf, sems.at[ENTER_CHUNKS + 1])
     c_copy.start()
     v_copy.wait()
     real = v_buf[...]
@@ -102,7 +103,7 @@
 
 def leave_kernel(vt, g, fh, fl, ch, cl, lo, hi):
     y = add_real(g[...], vt[...])
-    w = times(apply_to(y, block_of((fh, fl)), NT), read((ch, cl)), NN)
+    w = times(apply_to(y, tuple((fh[part], fl[part]) for part in range(2)), NT), read((ch, cl)), NN)
     half = lo.shape[0] // 2
     width = 2 * half
     lo[...] = jnp.concatenate([w[:half], w[width : width + half]], axis=0)
@@ -129,7 +130,7 @@
 
 def roles_kernel(count, *refs):
     sources = (refs[:count], refs[count : 2 * count])
-    high, low, buf, sems = refs[-4:]
+    mats, buf, sems = refs[-3:]
     mine = lax.axis_index("row") % 2
     slots = (mine, 1 - mine)
     n = buf.shape[2]
@@ -148,13 +149,13 @@
     for side, index, part, copy in copies:
         copy.wait()
         h, l = parts_of(buf[side, index, part, :])
-        high[slots[side], index, part, :] = h
-        low[slots[side], index, part, :] = l
+        mats[0, slots[side], index, part, :] = h
+        mats[1, slots[side], index, part, :] = l
 
 
 def roles_and_vectors_kernel(count, *refs):
     v_own, v_other, va, vb = refs[2 * count : 2 * count + 4]
-    roles_kernel(count, *refs[: 2 * count], *refs[-4:])
+    roles_kernel(count, *refs[: 2 * count], *refs[-3:])
     mine = lax.axis_index("row") % 2
     half = va.shape[0]
     own = v_own[pl.ds(pl.multiple_of(mine * half, half), half), :]
@@ -165,16 +166,16 @@
 
 def roles(owns, others, vectors=()):
     n = others[0].shape[-1]
-    shape = (2, 2, n, n)
+    shape = (2, 2, 2, n, n)
     halves = [(v.shape[0] // 2, n) for v in vectors]
     body = roles_and_vectors_kernel if vectors else roles_kernel
     return pl.pallas_call(
         functools.partial(body, len(others)),
         out_shape=tuple(pltpu.VMEM(half, F32) for half in halves)
-        + (pltpu.VMEM(shape, BF16), pltpu.VMEM(shape, BF16)),
+        + (pltpu.VMEM(shape, BF16),),
         in_specs=[HBM] * (2 * len(others)) + [VMEM] * len(vectors),
-        out_specs=(VMEM,) * (2 + len(halves)),
-        scratch_shapes=[pltpu.VMEM(shape, F32), pltpu.SemaphoreType.DMA((2, CHUNKS))],
+        out_specs=(VMEM,) * (1 + len(halves)),
+        scratch_shapes=[pltpu.VMEM(shape[1:], F32), pltpu.SemaphoreType.DMA((2, CHUNKS))],
         compiler_params=pltpu.CompilerParams(vmem_limit_bytes=20 << 20),
     )(
         *[pltpu.with_memory_space_constraint(x, pltpu.HBM) for x in owns],
@@ -183,30 +184,114 @@
     )
 
 
+def total(refs):
+    value = refs[0][...]
+    for other in refs[1:]:
+        value = value + other[...]
+    return value
+
+
 def forward_kernel(*refs):
-    *cs, va, vb, ah, al, out = refs
-    c = cs[0][...]
-    for other in cs[1:]:
-        c = c + other[...]
-    y = apply_to(add_real(c, va[...]), block_of((ah, al), 0), NN)
-    out[...] = apply_to(add_real(y, vb[...]), block_of((ah, al), 1), NN)
-
-
-def turn_kernel(c, va, vb, fh, fl, ah, al, bh, bl, ua, ub, s):
-    y = add_real(c[...], va[...])
-    y_b = add_real(apply_to(y, block_of((ah, al), 0), NN), vb[...])
-    u_b = apply_to(y_b, block_of((fh, fl), 1), NT)
-    u_a = apply_to(y, block_of((fh, fl), 0), NT)
+    *cs, va, vb, a_mats, out = refs
+    y = apply_to(add_real(total(cs), va[...]), block_of(a_mats, 0), NN)
+    out[...] = apply_to(add_real(y, vb[...]), block_of(a_mats, 1), NN)
+
+
+def turn_kernel(*refs):
+    *cs, va, vb, f_mats, a_mats, b_mats, ua, ub, s, weights = refs
+    nodes = lax.axis_size("node")
+    line = lax.broadcasted_iota(jnp.int32, weights.shape, 0)
+    other, kind = line % nodes, line // nodes
+    theta = 2.0 * math.pi * ((lax.axis_index("node") ^ other).astype(F32) + 0.5) / nodes
+    angle = (kind // 2 + 1).astype(F32) * theta
+    weights[...] = jnp.where(kind % 2 == 0, jnp.cos(angle), jnp.sin(angle)) / nodes
+    y = add_real(total(cs), va[...])
+    y_b = add_real(apply_to(y, block_of(a_mats, 0), NN), vb[...])
+    u_b = apply_to(y_b, block_of(f_mats, 1), NT)
+    u_a = apply_to(y, block_of(f_mats, 0), NT)
     ub[...] = u_b
     ua[...] = u_a
-    s[...] = u_a + apply_to(u_b, block_of((bh, bl), 0), NN)
-
-
-def backward_kernel(r, ua, ub, bh, bl, xa, *xb):
-    x_b = ub[...] + apply_to(r[...], block_of((bh, bl), 1), NN)
-    for out in xb:
-        out[...] = x_b
-    xa[...] = ua[...] + apply_to(x_b, block_of((bh, bl), 0), NN)
+    s[...] = u_a + apply_to(u_b, block_of(b_mats, 0), NN)
+
+
+def backward_kernel(r, ua, ub, b_mats, xa):
+    x_b = ub[...] + apply_to(r[...], block_of(b_mats, 1), NN)
+    xa[...] = ua[...] + apply_to(x_b, block_of(b_mats, 0), NN)
+
+
+def leave_backward_kernel(shares, *refs):
+    *rs, ua, ub, b_mats = refs[: -1 - shares]
+    *pieces, x = refs[-1 - shares :]
+    node = lax.axis_index("node")
+    x_b = ub[...] + apply_to(total(rs), block_of(b_mats, 1), NN)
+    rows = x_b.shape[0]
+    x[pl.ds(rows, rows), :] = x_b
+    x[pl.ds(0, rows), :] = ua[...] + apply_to(x_b, block_of(b_mats, 0), NN)
+    for d, piece in enumerate(pieces):
+        lanes = piece.shape[1]
+        piece[...] = x[:, pl.ds(pl.multiple_of((node ^ d) * lanes, lanes), lanes)]
+
+
+def combine_kernel(*refs):
+    *pieces, weights, out = refs
+    nodes = len(pieces)
+    half = pieces[0].shape[0] // 4
+    share = out.shape[1]
+    groups = 2 * MOM
+    for b in range(2):
+        parts = [
+            [piece[pl.ds((2 * b + part) * half, half), :] for piece in pieces] for part in range(2)
+        ]
+        for order in range(MOM):
+            w_re, w_im = (
+                [weights[pl.ds((2 * order + part) * nodes + d, 1), :][:, :share] for d in range(nodes)]
+                for part in range(2)
+            )
+            re = [w_re[d] * parts[0][d] - w_im[d] * parts[1][d] for d in range(nodes)]
+            im = [w_re[d] * parts[1][d] + w_im[d] * parts[0][d] for d in range(nodes)]
+            row = (b * groups + 2 * order) * half
+            out[pl.ds(row, half), :] = tree_sum(re)
+            out[pl.ds(row + half, half), :] = tree_sum(im)
+
+
+def gram_kernel(mine, other, moments, *outs):
+    *owns, buf = outs
+    node = lax.axis_index("node")
+    first = lax.axis_index("row") % 2 == 0
+    groups = 2 * MOM
+    half = mine.shape[0] // (2 * groups)
+    gram, both = None, []
+    for b in range(2):
+        part = pl.ds(b * groups * half, groups * half)
+        a, o = mine[part, :], other[part, :]
+        lo, hi = jnp.where(first, a, o), jnp.where(first, o, a)
+        cuts = [slice(g * half, (g + 1) * half) for g in range(groups)]
+        both.append(jnp.concatenate([side[cut] for cut in cuts for side in (lo, hi)], axis=0))
+        product = times(a, parts_of(both[b]), NT)
+        gram = product if gram is None else gram + product
+    buf[...] = gram
+    for d, own in enumerate(owns):
+        rows = own.shape[0]
+        own[...] = buf[pl.ds(pl.multiple_of((node ^ d) * rows, rows), rows), :]
+    moments[...] = jnp.where(first, both[0], both[1])
+
+
+def gather_kernel(*refs):
+    *pieces, out = refs
+    node = lax.axis_index("node")
+    for d, piece in enumerate(pieces):
+        rows = piece.shape[0]
+        out[pl.ds(pl.multiple_of((node ^ d) * rows, rows), rows), :] = piece[...]
+
+
+def join_kernel(mine, other, out):
+    first = lax.axis_index("row") % 2 == 0
+    groups = 2 * MOM
+    half = mine.shape[0] // groups
+    for g in range(groups):
+        cut = pl.ds(g * half, half)
+        out[pl.ds(2 * g * half, half), :] = jnp.where(first, mine[cut, :], other[cut, :])
+        out[pl.ds((2 * g + 1) * half, half), :] = jnp.where(first, other[cut, :], mine[cut, :])
 
 
 def after(*values, every=False):
@@ -227,9 +312,6 @@
     rows = lax.axis_size("row")
     nodes = lax.axis_size("node")
     layers = rows // 2
-    core = lax.axis_index("row") % 2
-    node = lax.axis_index("node")
-    first = core == 0
 
     def swap_core(value):
         return lax.ppermute(value, "row", [(r, r ^ 1) for r in range(rows)])
@@ -263,7 +345,7 @@
             pltpu.VMEM((2, n, n), F32),
             pltpu.VMEM((n, n), F32),
             pltpu.VMEM((width, n), F32),
-            pltpu.SemaphoreType.DMA((CHUNKS + 2,)),
+            pltpu.SemaphoreType.DMA((ENTER_CHUNKS + 2,)),
         ],
         compiler_params=pltpu.CompilerParams(vmem_limit_bytes=20 << 20),
         name="enter",
@@ -279,74 +361,76 @@
     a_re_other = swap_core(after(a_re, from_a))
     a_im_other = swap_core(a_im)
     v_other = swap_core(after(v_t, lo))
-    va, vb, *a_mats = roles([a_re, a_im], [a_re_other, a_im_other], [v_t, v_other])
+    va, vb, a_mats = roles([a_re, a_im], [a_re_other, a_im_other], [v_t, v_other])
     f_other = swap_core(after(factor, a_re_other, a_im_other))
-    carry = jnp.zeros((2 * half, n), F32)
+    arrived = []
     for t in range(layers - 1):
         if t > 0:
             got = [hop(leaving, t, t + 1)]
-        carry = sum(got, carry)
+        arrived += got
         if t < layers - 2:
-            (leaving,) = call(forward_kernel, [block], *got, va, vb, *a_mats)
+            (leaving,) = call(forward_kernel, [block], *got, va, vb, a_mats)
         if t == 0:
-            f_mats = roles([after(factor, leaving)], [f_other])
+            (f_mats,) = roles([after(factor, leaving)], [f_other])
             (b_own,) = call(b_kernel, [((2, n, n), F32)], after(fh, leaving), fl, ch, cl)
             b_other = swap_core(b_own)
         if t == 1:
-            b_mats = roles([after(b_own, leaving)], [b_other])
-    u_a, u_b, leaving = call(turn_kernel, [block] * 3, carry, va, vb, *f_mats, *a_mats, *b_mats)
-
-    following = jnp.zeros((2 * half, n), F32)
+            (b_mats,) = roles([after(b_own, leaving, f_mats)], [b_other])
+    u_a, u_b, leaving, weights = call(
+        turn_kernel, [block] * 3 + [((2 * MOM * nodes, 128), F32)], *arrived, va, vb, f_mats, a_mats, b_mats
+    )
+
+    arrived = []
     for t in range(layers - 1, 0, -1):
         got = hop(leaving, t, t - 1)
-        following = following + got
+        arrived.append(got)
         if t > 1:
-            (leaving,) = call(backward_kernel, [block], got, u_a, u_b, *b_mats)
-    x_a, x_b = call(backward_kernel, [block] * 2, following, u_a, u_b, *b_mats)
-
+            (leaving,) = call(backward_kernel, [block], got, u_a, u_b, b_mats)
     share = n // nodes
-    x_both = jnp.concatenate([x_a, x_b], axis=0)
-    pieces = [lax.dynamic_slice_in_dim(x_both, (node ^ d) * share, share, 1) for d in range(nodes)]
+    shares = nodes if share % 128 == 0 else 0
+    x_both = ((4 * half, n), F32)
+    pieces = call(
+        functools.partial(leave_backward_kernel, shares),
+        [((4 * half, share), F32)] * shares or [x_both],
+        *arrived, u_a, u_b, b_mats,
+        scratch=[x_both] if shares else [],
+    )
+
+    if not shares:
+        node = lax.axis_index("node")
+        pieces = [
+            lax.dynamic_slice_in_dim(pieces[0], (node ^ d) * share, share, 1)
+            for d in range(nodes)
+        ]
     pieces = [pieces[0]] + [exchange_node(pieces[d], d) for d in range(1, nodes)]
-    pieces = [p.reshape(2, 2, half, share) for p in pieces]
-    terms = []
-    for order in range(MOM):
-        re_terms, im_terms = [], []
-        for d in range(nodes):
-            theta = 2.0 * math.pi * ((node ^ d).astype(F32) + 0.5) / nodes
-            w_re = jnp.cos((order + 1) * theta) / nodes
-            w_im = jnp.sin((order + 1) * theta) / nodes
-            re, im = pieces[d][:, 0], pieces[d][:, 1]
-            re_terms.append(w_re * re - w_im * im)
-            im_terms.append(w_re * im + w_im * re)
-        terms += [tree_sum(re_terms), tree_sum(im_terms)]
-    mine = jnp.stack(terms, axis=1)
     groups = 2 * MOM
     cols = groups * width
-    other = swap_core(mine.reshape(2 * groups * half, share)).reshape(mine.shape)
-    both = jnp.stack([jnp.where(first, mine, other), jnp.where(first, other, mine)], axis=2)
-    both = both.reshape(2, cols, share)
-    moments = jnp.where(first, both[0], both[1])
-
-    mine = mine.reshape(2, groups * half, share)
-    gram = lax.dot_general(mine[0], both[0], NT, precision=PREC) + lax.dot_general(
-        mine[1], both[1], NT, precision=PREC
-    )
+    (mine,) = call(combine_kernel, [((2 * groups * half, share), F32)], *pieces, weights)
+    other = swap_core(mine)
+
     hc = groups * half
     gs = hc // nodes
-    own = [lax.dynamic_slice_in_dim(gram, (node ^ d) * gs, gs, 0) for d in range(nodes)]
+    moments, *own = call(
+        gram_kernel,
+        [((cols, share), F32)] + [((gs, cols), F32)] * nodes,
+        mine, other,
+        scratch=[((hc, cols), F32)],
+    )
     piece = tree_sum([own[0]] + [exchange_node(own[d], d) for d in range(1, nodes)])
     piece = tree_sum([piece] + [exchange_layer(piece, d) for d in range(1, layers)])
     piece = piece * (nodes / (rows * n))
     got = [piece] + [exchange_node(piece, d) for d in range(1, nodes)]
-    gram = jnp.zeros((hc, cols), F32)
-    for d in range(nodes):
-        gram = lax.dynamic_update_slice_in_dim(gram, got[d], (node ^ d) * gs, 0)
+    (gram,) = call(gather_kernel, [((hc, cols), F32)], *got)
     other = swap_core(gram)
-    gram = gram.reshape(groups, half, cols)
-    other = other.reshape(groups, half, cols)
-    gram = jnp.stack([jnp.where(first, gram, other), jnp.where(first, other, gram)], axis=1)
-    return moments.T[None], gram.reshape(cols, cols)
+    gram = pl.pallas_call(
+        join_kernel,
+        out_shape=jax.ShapeDtypeStruct((cols, cols), F32),
+        in_specs=[VMEM] * 2,
+        out_specs=VMEM,
+        compiler_params=pltpu.CompilerParams(vmem_limit_bytes=20 << 20),
+        name="join",
+    )(*[pltpu.with_memory_space_constraint(x, pltpu.VMEM) for x in (gram, other)])
+    return moments.T[None], gram
 
 
 def solution(mesh):

time: 92.6 us -> 87.1 us (0.941)
  local copies, waits for them, and re-layouts: 2.48 us -> 0.78 us
  waiting for transfers between devices: 40.1 us -> 38.6 us
  between operations: 2.38 us -> 0.96 us
  other arithmetic: 1.02 us -> 0.02 us
    ppermute x8, waiting for transfers between devices: 6.46 us -> 4.01 us  [swap_core(): return lax.ppermute(value, 'row', [(r, r ^ 1) for r in range(rows)])]
    ppermute x9, waiting for transfers between devices: 8.64 us -> 10.5 us  [exchange_node(): return lax.ppermute(value, 'node', [(j, j ^ d) for j in range(nodes)])]
    unnamed x14 -> x9, local copies, waits for them, and re-layouts: 2.37 us -> 0.78 us
    pallas_call x10 -> x13, Pallas kernels: 11.5 us -> 12 us  [call(): pl.pallas_call(kernel, out_shape=tuple((pltpu.VMEM(shape, dtype) for shap...]
  transfers between devices with their start and end apart: 27 -> 27, of which waited for: 18 -> 17; matrix products, arithmetic and copies ran while one was open for 1% -> 1% of each run, Pallas kernels for 6% -> 12%
where the time goes in v3:
time: 87.1 us; the launch traced here: 86.8 us
  waiting for transfers between devices  38.6 us (44%)
  starting transfers between devices  24.9 us (29%)
  Pallas kernels  21.5 us (25%)
  between operations  0.96 us (1%)
    ppermute x5, waiting for transfers between devices, hop(): lax.ppermute(value, 'row', [(2 * source + c, 2 * target + c) for c in ran...  22.2 us
    pallas_call x13, Pallas kernels, call(): pl.pallas_call(kernel, out_shape=tuple((pltpu.VMEM(shape, dtype) for shap...  12 us
    ppermute x9, starting transfers between devices, exchange_node(): return lax.ppermute(value, 'node', [(j, j ^ d) for j in range(nodes)])  10.7 us
    ppermute x9, waiting for transfers between devices, exchange_node(): return lax.ppermute(value, 'node', [(j, j ^ d) for j in range(nodes)])  10.5 us
    pallas_call x3, Pallas kernels, roles(): pl.pallas_call(functools.partial(body, len(others)), out_shape=tuple((plt...  6.13 us
    ppermute x8, starting transfers between devices, swap_core(): return lax.ppermute(value, 'row', [(r, r ^ 1) for r in range(rows)])  4.56 us
    ppermute x3, starting transfers between devices, exchange_layer(): return lax.ppermute(value, 'row', [(r, r ^ 2 * d) for r in range(rows)])  4.45 us
    ppermute x8, waiting for transfers between devices, swap_core(): return lax.ppermute(value, 'row', [(r, r ^ 1) for r in range(rows)])  4.01 us
  transfers between devices with their start and end apart: 27, of which 17 were waited for; matrix products, arithmetic and copies ran while one was open for 1% of the time, Pallas kernels for 12%

profile of v3, /device:TPU:0, one launch (start us, length us, event | category | flops | bytes accessed | tf_op | source)
XLA Modules:
  0.0 86.8 jit_solution(13053782411372413810)
XLA Ops:
  0.6 2.7 %enter.1 = (bf16[2,512,512]{2,1,0:T(8,128)(2,1)S(1)}, bf16[2,512,512]{2,1,0:T(8,128)(2,1)S(1)}, bf16[512,512]{1,0:T(8,128)(2,1)S(1)}, bf16[512,512]{1,0:T(8,128)...) custom-call(f32[2,512,512]{2,1,0:T(8,128)} %bitcast.9, f32[512,512]{1,0:T(8,128)} %bitcast.12, f32[64,512]{1,0:T(8,128)} %bitcast.13), custom_call_target="tpu_custom_call" | custom-call | tf_op jit(solution)/shard_map/enter/pallas_call | solution.py:332
  3.4 0.6 collective-permute-start
  3.9 1.0 %shard_map.51.refs_0_ = f32[512,512]{1,0:T(8,128)S(1)} custom-call(bf16[2,512,512]{2,1,0:T(8,128)(2,1)S(1)} %get-tuple-element.53.fh, bf16[2,512,512]{2,1,0:T(8,128)(2,1)S(1)} %get-tuple-element.39.fl, bf16[512,512]{1,0:T(8,128)(2,1)S(1)} %get-tuple-element.40.ch, bf16[512,512]{1,0:T(8,128)(2,1)S(1)} %get-tuple-element.41.cl), custom_call_target="tpu_custom_call" | custom-call | tf_op jit(solution)/shard_map/pallas_call | solution.py:64
  4.9 0.2 collective-permute-done.g
  5.1 1.1 %shard_map.50 = (f32[64,512]{1,0:T(8,128)S(1)}, f32[64,512]{1,0:T(8,128)S(1)}) custom-call(f32[64,512]{1,0:T(8,128)S(1)} %get-tuple-element.47.vt.refs_4_, f32[128,512]{1,0:T(8,128)S(1)} %collective-permute-done.g, bf16[2,512,512]{2,1,0:T(8,128)(2,1)S(1)} %get-tuple-element.53.fh, bf16[2,512,512]{2,1,0:T(8,128)(2,1)S(1)} %get-tuple-element.39.fl, ...), custom_call_target="tpu_custom_call" | custom-call | tf_op jit(solution)/shard_map/pallas_call | solution.py:64
  6.2 0.0 copy-start.3
  6.2 1.0 %shard_map.52.refs_1_ = f32[512,512]{1,0:T(8,128)S(1)} custom-call(bf16[2,512,512]{2,1,0:T(8,128)(2,1)S(1)} %get-tuple-element.53.fh, bf16[2,512,512]{2,1,0:T(8,128)(2,1)S(1)} %get-tuple-element.39.fl, bf16[512,512]{1,0:T(8,128)(2,1)S(1)} %get-tuple-element.40.ch, bf16[512,512]{1,0:T(8,128)(2,1)S(1)} %get-tuple-element.41.cl), custom_call_target="tpu_custom_call" | custom-call | tf_op jit(solution)/shard_map/pallas_call | solution.py:64
  7.2 0.4 collective-permute-start.3
  7.6 0.1 collective-permute-start.4
  7.8 0.4 collective-permute-start.5
  8.1 0.7 collective-permute-start.2
  8.8 0.7 collective-permute-start.1
  9.5 0.4 collective-permute-done.3.refs_2_
  9.9 1.5 %collective-permute-done.4.refs_3_ = f32[512,512]{1,0:T(8,128)S(1)} collective-permute-done((f32[512,512]{1,0:T(8,128)S(1)}, f32[512,512]{1,0:T(8,128)S(1)}, u32[]{:S(2)}, u32[]{:S(2)}) %collective-permute-start.4) | collective-permute-done | bytes 1048608 | tf_op jit(solution)/shard_map/ppermute | solution.py:317
  11.4 2.8 %collective-permute-start.8 = (f32[2,512,512]{2,1,0:T(8,128)S(1)}, f32[2,512,512]{2,1,0:T(8,128)S(1)}, u32[]{:S(2)}, u32[]{:S(2)}) collective-permute-start(f32[2,512,512]{2,1,0:T(8,128)S(1)} %bitcast.11), channel_id=1, source_target_pairs={{0,1},{1,0},{2,3},{3,2},{4,5},{5,4},{6,7},{7,6},{8,9},{9,8},{10,11... | collective-permute-start | bytes 6291464 | tf_op jit(solution)/shard_map/ppermute | solution.py:317
  14.2 0.0 collective-permute-done.5.refs_5_
  14.2 2.0 %shard_map.53 = (f32[32,512]{1,0:T(8,128)S(1)}, f32[32,512]{1,0:T(8,128)S(1)}, bf16[2,2,2,512,512]{4,3,2,1,0:T(8,128)(2,1)S(1)}) custom-call(f32[512,512]{1,0:T(8,128)} %copy-done.1, f32[512,512]{1,0:T(8,128)} %copy-done.2, f32[512,512]{1,0:T(8,128)S(1)} %collective-permute-done.3.refs_2_, f32[512,512]{1,0:T(8,128)S(1)} %collective-permute-done.4.refs_3_, ...), custom_call_target="tpu_custom_call" | custom-call | tf_op jit(solution)/shard_map/pallas_call | solution.py:172
  16.3 0.9 %shard_map.54 = f32[64,512]{1,0:T(8,128)S(1)} custom-call(f32[64,512]{1,0:T(8,128)S(1)} %collective-permute-done.1.refs_0_, f32[64,512]{1,0:T(8,128)S(1)} %collective-permute-done.2.refs_1_, f32[32,512]{1,0:T(8,128)S(1)} %get-tuple-element.48.refs_2_.refs_1_.refs_4_, f32[32,512]{1,0:T(8,128)S(1)} %get-tuple-element.49.refs_3_.refs_2_.refs_5_, ...), custom_call_target="tpu_custom_call" | custom-call | tf_op jit(solution)/shard_map/pallas_call | solution.py:64
  17.2 1.8 %shard_map.57.refs_0_ = f32[2,512,512]{2,1,0:T(8,128)S(1)} custom-call(bf16[2,512,512]{2,1,0:T(8,128)(2,1)S(1)} %get-tuple-element.53.fh, bf16[2,512,512]{2,1,0:T(8,128)(2,1)S(1)} %get-tuple-element.39.fl, bf16[512,512]{1,0:T(8,128)(2,1)S(1)} %get-tuple-element.40.ch, bf16[512,512]{1,0:T(8,128)(2,1)S(1)} %get-tuple-element.41.cl), custom_call_target="tpu_custom_call" | custom-call | tf_op jit(solution)/shard_map/pallas_call | solution.py:64
  19.1 0.1 collective-permute-start.9
  19.2 0.7 collective-permute-start.6
  19.8 0.9 %shard_map.55 = f32[64,512]{1,0:T(8,128)S(1)} custom-call(f32[64,512]{1,0:T(8,128)S(1)} %collective-permute-done.6.refs_0_.refs_2_, f32[32,512]{1,0:T(8,128)S(1)} %get-tuple-element.48.refs_2_.refs_1_.refs_4_, f32[32,512]{1,0:T(8,128)S(1)} %get-tuple-element.49.refs_3_.refs_2_.refs_5_, bf16[2,2,2,512,512]{4,3,2,1,0:T(8,128)(2,1)S(1)} %get-tuple-element.50.refs_4_.refs_3_.refs_7_), custom_call_target="tpu_custom_call" | custom-call | tf_op jit(solution)/shard_map/pallas_call | solution.py:64
  20.8 0.7 collective-permute-start.7
  21.4 2.0 %shard_map.56.refs_6_ = bf16[2,2,2,512,512]{4,3,2,1,0:T(8,128)(2,1)S(1)} custom-call(f32[2,512,512]{2,1,0:T(8,128)} %bitcast.10, f32[2,512,512]{2,1,0:T(8,128)S(1)} %collective-permute-done.8.refs_1_), custom_call_target="tpu_custom_call" | custom-call | tf_op jit(solution)/shard_map/pallas_call | solution.py:172
  23.5 2.0 %shard_map.58.refs_8_.b_mats.refs_5_ = bf16[2,2,2,512,512]{4,3,2,1,0:T(8,128)(2,1)S(1)} custom-call(f32[2,512,512]{2,1,0:T(8,128)} %copy-done, f32[2,512,512]{2,1,0:T(8,128)S(1)} %collective-permute-done.9.refs_1_), custom_call_target="tpu_custom_call" | custom-call | tf_op jit(solution)/shard_map/pallas_call | solution.py:172
  25.6 2.2 %shard_map.59 = (f32[64,512]{1,0:T(8,128)S(1)}, f32[64,512]{1,0:T(8,128)S(1)}, f32[64,512]{1,0:T(8,128)S(1)}, f32[16,128]{1,0:T(8,128)S(1)}) custom-call(f32[64,512]{1,0:T(8,128)S(1)} %collective-permute-done.1.refs_0_, f32[64,512]{1,0:T(8,128)S(1)} %collective-permute-done.2.refs_1_, f32[64,512]{1,0:T(8,128)S(1)} %collective-permute-done.6.refs_0_.refs_2_, ...), custom_call_target="tpu_custom_call" | custom-call | tf_op jit(solution)/shard_map/pallas_call | solution.py:64
  27.7 0.7 collective-permute-start.10
  28.4 0.9 %shard_map.60 = f32[64,512]{1,0:T(8,128)S(1)} custom-call(f32[64,512]{1,0:T(8,128)S(1)} %collective-permute-done.10.r.refs_0_, f32[64,512]{1,0:T(8,128)S(1)} %get-tuple-element.56.ua.refs_3_, f32[64,512]{1,0:T(8,128)S(1)} %get-tuple-element.57.ub.refs_4_, bf16[2,2,2,512,512]{4,3,2,1,0:T(8,128)(2,1)S(1)} %shard_map.58.refs_8_.b_mats.refs_5_), custom_call_target="tpu_custom_call" | custom-call | tf_op jit(solution)/shard_map/pallas_call | solution.py:64
  29.3 0.7 collective-permute-start.11
  30.0 0.9 %shard_map.61 = f32[64,512]{1,0:T(8,128)S(1)} custom-call(f32[64,512]{1,0:T(8,128)S(1)} %collective-permute-done.11.r.refs_1_, f32[64,512]{1,0:T(8,128)S(1)} %get-tuple-element.56.ua.refs_3_, f32[64,512]{1,0:T(8,128)S(1)} %get-tuple-element.57.ub.refs_4_, bf16[2,2,2,512,512]{4,3,2,1,0:T(8,128)(2,1)S(1)} %shard_map.58.refs_8_.b_mats.refs_5_), custom_call_target="tpu_custom_call" | custom-call | tf_op jit(solution)/shard_map/pallas_call | solution.py:64
  30.9 1.3 %collective-permute-start.12 = (f32[64,512]{1,0:T(8,128)S(1)}, f32[64,512]{1,0:T(8,128)S(1)}, u32[]{:S(2)}, u32[]{:S(2)}) collective-permute-start(f32[64,512]{1,0:T(8,128)S(1)} %shard_map.61), channel_id=1, source_target_pairs={{2,0},{3,1},{10,8},{11,9},{18,16},{19,17},{26,24},{27,25}} | collective-permute-start | bytes 393224 | tf_op jit(solution)/shard_map/ppermute | solution.py:320
  32.2 22.2 %collective-permute-done.12.refs_2_ = f32[64,512]{1,0:T(8,128)S(1)} collective-permute-done((f32[64,512]{1,0:T(8,128)S(1)}, f32[64,512]{1,0:T(8,128)S(1)}, u32[]{:S(2)}, u32[]{:S(2)}) %collective-permute-start.12) | collective-permute-done | bytes 131104 | tf_op jit(solution)/shard_map/ppermute | solution.py:320
  54.4 0.9 %shard_map.62 = (f32[128,128]{1,0:T(8,128)S(1)}, f32[128,128]{1,0:T(8,128)S(1)}, f32[128,128]{1,0:T(8,128)S(1)}, f32[128,128]{1,0:T(8,128)S(1)}) custom-call(f32[64,512]{1,0:T(8,128)S(1)} %collective-permute-done.10.r.refs_0_, f32[64,512]{1,0:T(8,128)S(1)} %collective-permute-done.11.r.refs_1_, f32[64,512]{1,0:T(8,128)S(1)} %collective-permute-done.12.refs_2_, ...), custom_call_target="tpu_custom_call" | custom-call | tf_op jit(solution)/shard_map/pallas_call | solution.py:64
  55.4 1.6 %collective-permute-start.13 = (f32[128,128]{1,0:T(8,128)S(1)}, f32[128,128]{1,0:T(8,128)S(1)}, u32[]{:S(2)}, u32[]{:S(2)}) collective-permute-start(f32[128,128]{1,0:T(8,128)S(1)} %get-tuple-element.59), channel_id=1, source_target_pairs={{0,8},{8,0},{16,24},{24,16},{1,9},{9,1},{17,25},{25,17},{2,10},{10... | collective-permute-start | bytes 196616 | tf_op jit(solution)/shard_map/ppermute | solution.py:323
  57.0 1.5 %collective-permute-start.14 = (f32[128,128]{1,0:T(8,128)S(1)}, f32[128,128]{1,0:T(8,128)S(1)}, u32[]{:S(2)}, u32[]{:S(2)}) collective-permute-start(f32[128,128]{1,0:T(8,128)S(1)} %get-tuple-element.60), channel_id=1, source_target_pairs={{0,16},{8,24},{16,0},{24,8},{1,17},{9,25},{17,1},{25,9},{2,18},{10... | collective-permute-start | bytes 196616 | tf_op jit(solution)/shard_map/ppermute | solution.py:323
  58.5 0.4 collective-permute-start.15
  58.9 0.8 collective-permute-done.13.refs_1_
  59.7 1.5 %collective-permute-done.14.refs_2_ = f32[128,128]{1,0:T(8,128)S(1)} collective-permute-done((f32[128,128]{1,0:T(8,128)S(1)}, f32[128,128]{1,0:T(8,128)S(1)}, u32[]{:S(2)}, u32[]{:S(2)}) %collective-permute-start.14) | collective-permute-done | bytes 65568 | tf_op jit(solution)/shard_map/ppermute | solution.py:323
  61.2 2.4 %collective-permute-done.15.refs_3_ = f32[128,128]{1,0:T(8,128)S(1)} collective-permute-done((f32[128,128]{1,0:T(8,128)S(1)}, f32[128,128]{1,0:T(8,128)S(1)}, u32[]{:S(2)}, u32[]{:S(2)}) %collective-permute-start.15) | collective-permute-done | bytes 65568 | tf_op jit(solution)/shard_map/ppermute | solution.py:323
  63.7 0.1 shard_map.63.mine
  63.7 0.1 collective-permute-start.16
  63.8 1.3 %collective-permute-done.16.other = f32[256,128]{1,0:T(8,128)S(1)} collective-permute-done((f32[256,128]{1,0:T(8,128)S(1)}, f32[256,128]{1,0:T(8,128)S(1)}, u32[]{:S(2)}, u32[]{:S(2)}) %collective-permute-start.16) | collective-permute-done | bytes 131104 | tf_op jit(solution)/shard_map/ppermute | solution.py:317
  65.1 0.3 shard_map.64
  65.4 0.6 collective-permute-start.17
  66.0 0.5 collective-permute-start.18
  66.5 2.5 %collective-permute-start.19 = (f32[32,256]{1,0:T(8,128)S(1)}, f32[32,256]{1,0:T(8,128)S(1)}, u32[]{:S(2)}, u32[]{:S(2)}) collective-permute-start(f32[32,256]{1,0:T(8,128)S(1)} %get-tuple-element.67), channel_id=1, source_target_pairs={{0,24},{8,16},{16,8},{24,0},{1,25},{9,17},{17,9},{25,1},{2,26},{10... | collective-permute-start | bytes 98312 | tf_op jit(solution)/shard_map/ppermute | solution.py:323
  69.0 0.4 collective-permute-done.17
  69.4 0.9 collective-permute-done.18
  70.3 1.0 %collective-permute-done.19 = f32[32,256]{1,0:T(8,128)S(1)} collective-permute-done((f32[32,256]{1,0:T(8,128)S(1)}, f32[32,256]{1,0:T(8,128)S(1)}, u32[]{:S(2)}, u32[]{:S(2)}) %collective-permute-start.19) | collective-permute-done | bytes 32800 | tf_op jit(solution)/shard_map/ppermute | solution.py:323
  71.3 0.1 collective-permute-start.22
  71.4 1.0 %collective-permute-start.21 = (f32[32,256]{1,0:T(8,128)S(1)}, f32[32,256]{1,0:T(8,128)S(1)}, u32[]{:S(2)}, u32[]{:S(2)}) collective-permute-start(f32[32,256]{1,0:T(8,128)S(1)} %add_add_fusion), channel_id=1, source_target_pairs={{0,4},{1,5},{2,6},{3,7},{4,0},{5,1},{6,2},{7,3},{8,12},{9,13},{10,... | collective-permute-start | bytes 98312 | tf_op jit(solution)/shard_map/ppermute | solution.py:326
  72.5 3.3 %collective-permute-start.20 = (f32[32,256]{1,0:T(8,128)S(1)}, f32[32,256]{1,0:T(8,128)S(1)}, u32[]{:S(2)}, u32[]{:S(2)}) collective-permute-start(f32[32,256]{1,0:T(8,128)S(1)} %add_add_fusion), channel_id=1, source_target_pairs={{0,2},{1,3},{2,0},{3,1},{4,6},{5,7},{6,4},{7,5},{8,10},{9,11},{10,... | collective-permute-start | bytes 98312 | tf_op jit(solution)/shard_map/ppermute | solution.py:326
  75.8 1.3 %collective-permute-done.22 = f32[32,256]{1,0:T(8,128)S(1)} collective-permute-done((f32[32,256]{1,0:T(8,128)S(1)}, f32[32,256]{1,0:T(8,128)S(1)}, u32[]{:S(2)}, u32[]{:S(2)}) %collective-permute-start.22) | collective-permute-done | bytes 32800 | tf_op jit(solution)/shard_map/ppermute | solution.py:326
  77.1 0.6 collective-permute-done.20
  77.7 2.5 %collective-permute-start.25 = (f32[32,256]{1,0:T(8,128)S(1)}, f32[32,256]{1,0:T(8,128)S(1)}, u32[]{:S(2)}, u32[]{:S(2)}) collective-permute-start(f32[32,256]{1,0:T(8,128)S(1)} %add_multiply_fusion.refs_0_), channel_id=1, source_target_pairs={{0,24},{8,16},{16,8},{24,0},{1,25},{9,17},{17,9},{25,1},{2,26},{10... | collective-permute-start | bytes 98312 | tf_op jit(solution)/shard_map/ppermute | solution.py:323
  80.2 0.5 collective-permute-start.24
  80.7 0.5 collective-permute-start.23
  81.3 1.3 %collective-permute-done.25.refs_3_ = f32[32,256]{1,0:T(8,128)S(1)} collective-permute-done((f32[32,256]{1,0:T(8,128)S(1)}, f32[32,256]{1,0:T(8,128)S(1)}, u32[]{:S(2)}, u32[]{:S(2)}) %collective-permute-start.25) | collective-permute-done | bytes 32800 | tf_op jit(solution)/shard_map/ppermute | solution.py:323
  82.6 1.6 %collective-permute-done.24.refs_2_ = f32[32,256]{1,0:T(8,128)S(1)} collective-permute-done((f32[32,256]{1,0:T(8,128)S(1)}, f32[32,256]{1,0:T(8,128)S(1)}, u32[]{:S(2)}, u32[]{:S(2)}) %collective-permute-start.24) | collective-permute-done | bytes 32800 | tf_op jit(solution)/shard_map/ppermute | solution.py:323
  84.2 0.5 collective-permute-done.23.refs_1_
  84.7 0.1 collective-permute-start.26
  84.8 0.8 copy.5
  85.5 0.6 collective-permute-done.26.other
  86.1 0.7 join.1
  (19 shorter events, 0.1 us)
Async XLA Ops:
  3.4 1.7 %collective-permute-start = (f32[128,512]{1,0:T(8,128)S(1)}, f32[128,512]{1,0:T(8,128)S(1)}, u32[]{:S(2)}, u32[]{:S(2)}) collective-permute-start(f32[128,512]{1,0:T(8,128)S(1)} %get-tuple-element.36), channel_id=1, source_target_pairs={{0,1},{1,0},{2,3},{3,2},{4,5},{5,4},{6,7},{7,6},{8,9},{9,8},{10,11... | collective-permute-start | bytes 786440 | tf_op jit(solution)/shard_map/ppermute | solution.py:317
  4.9 2.3 %copy-start.1 = (f32[512,512]{1,0:T(8,128)}, f32[512,512]{1,0:T(8,128)S(1)}, u32[]{:S(2)}) copy-start(f32[512,512]{1,0:T(8,128)S(1)} %shard_map.51.refs_0_) | copy-start | bytes 3145732
  6.2 5.3 %copy-start.3 = (f32[1,1,2,512,512]{4,3,2,1,0:T(8,128)S(1)}, f32[1,1,2,512,512]{4,3,2,1,0:T(8,128)}, u32[]{:S(2)}) copy-start(f32[1,1,2,512,512]{4,3,2,1,0:T(8,128)} %param.3) | copy-start | bytes 6291460
  7.2 7.1 %copy-start.2 = (f32[512,512]{1,0:T(8,128)}, f32[512,512]{1,0:T(8,128)S(1)}, u32[]{:S(2)}) copy-start(f32[512,512]{1,0:T(8,128)S(1)} %shard_map.52.refs_1_) | copy-start | bytes 3145732
  7.2 2.7 %collective-permute-start.3 = (f32[512,512]{1,0:T(8,128)S(1)}, f32[512,512]{1,0:T(8,128)S(1)}, u32[]{:S(2)}, u32[]{:S(2)}) collective-permute-start(f32[512,512]{1,0:T(8,128)S(1)} %shard_map.51.refs_0_), channel_id=1, source_target_pairs={{0,1},{1,0},{2,3},{3,2},{4,5},{5,4},{6,7},{7,6},{8,9},{9,8},{10,11... | collective-permute-start | bytes 3145736 | tf_op jit(solution)/shard_map/ppermute | solution.py:317
  7.6 3.8 %collective-permute-start.4 = (f32[512,512]{1,0:T(8,128)S(1)}, f32[512,512]{1,0:T(8,128)S(1)}, u32[]{:S(2)}, u32[]{:S(2)}) collective-permute-start(f32[512,512]{1,0:T(8,128)S(1)} %shard_map.52.refs_1_), channel_id=1, source_target_pairs={{0,1},{1,0},{2,3},{3,2},{4,5},{5,4},{6,7},{7,6},{8,9},{9,8},{10,11... | collective-permute-start | bytes 3145736 | tf_op jit(solution)/shard_map/ppermute | solution.py:317
  7.8 6.5 %collective-permute-start.5 = (f32[64,512]{1,0:T(8,128)S(1)}, f32[64,512]{1,0:T(8,128)S(1)}, u32[]{:S(2)}, u32[]{:S(2)}) collective-permute-start(f32[64,512]{1,0:T(8,128)S(1)} %get-tuple-element.47.vt.refs_4_), channel_id=1, source_target_pairs={{0,1},{1,0},{2,3},{3,2},{4,5},{5,4},{6,7},{7,6},{8,9},{9,8},{10,11... | collective-permute-start | bytes 393224 | tf_op jit(solution)/shard_map/ppermute | solution.py:317
  8.1 8.2 %collective-permute-start.2 = (f32[64,512]{1,0:T(8,128)S(1)}, f32[64,512]{1,0:T(8,128)S(1)}, u32[]{:S(2)}, u32[]{:S(2)}) collective-permute-start(f32[64,512]{1,0:T(8,128)S(1)} %get-tuple-element.43), channel_id=1, source_target_pairs={{1,3},{9,11},{17,19},{25,27}} | collective-permute-start | bytes 393224 | tf_op jit(solution)/shard_map/ppermute | solution.py:358
  8.8 7.5 %collective-permute-start.1 = (f32[64,512]{1,0:T(8,128)S(1)}, f32[64,512]{1,0:T(8,128)S(1)}, u32[]{:S(2)}, u32[]{:S(2)}) collective-permute-start(f32[64,512]{1,0:T(8,128)S(1)} %get-tuple-element.42), channel_id=1, source_target_pairs={{1,2},{9,10},{17,18},{25,26}} | collective-permute-start | bytes 393224 | tf_op jit(solution)/shard_map/ppermute | solution.py:357
  11.4 10.0 %collective-permute-start.8 = (f32[2,512,512]{2,1,0:T(8,128)S(1)}, f32[2,512,512]{2,1,0:T(8,128)S(1)}, u32[]{:S(2)}, u32[]{:S(2)}) collective-permute-start(f32[2,512,512]{2,1,0:T(8,128)S(1)} %bitcast.11), channel_id=1, source_target_pairs={{0,1},{1,0},{2,3},{3,2},{4,5},{5,4},{6,7},{7,6},{8,9},{9,8},{10,11... | collective-permute-start | bytes 6291464 | tf_op jit(solution)/shard_map/ppermute | solution.py:317
  19.0 1.7 %copy-start = (f32[2,512,512]{2,1,0:T(8,128)}, f32[2,512,512]{2,1,0:T(8,128)S(1)}, u32[]{:S(2)}) copy-start(f32[2,512,512]{2,1,0:T(8,128)S(1)} %shard_map.57.refs_0_) | copy-start | bytes 6291460
  19.1 4.4 %collective-permute-start.9 = (f32[2,512,512]{2,1,0:T(8,128)S(1)}, f32[2,512,512]{2,1,0:T(8,128)S(1)}, u32[]{:S(2)}, u32[]{:S(2)}) collective-permute-start(f32[2,512,512]{2,1,0:T(8,128)S(1)} %shard_map.57.refs_0_), channel_id=1, source_target_pairs={{0,1},{1,0},{2,3},{3,2},{4,5},{5,4},{6,7},{7,6},{8,9},{9,8},{10,11... | collective-permute-start | bytes 6291464 | tf_op jit(solution)/shard_map/ppermute | solution.py:317
  19.2 0.7 collective-permute-start.6
  20.8 4.8 %collective-permute-start.7 = (f32[64,512]{1,0:T(8,128)S(1)}, f32[64,512]{1,0:T(8,128)S(1)}, u32[]{:S(2)}, u32[]{:S(2)}) collective-permute-start(f32[64,512]{1,0:T(8,128)S(1)} %shard_map.55), channel_id=1, source_target_pairs={{4,6},{5,7},{12,14},{13,15},{20,22},{21,23},{28,30},{29,31}} | collective-permute-start | bytes 393224 | tf_op jit(solution)/shard_map/ppermute | solution.py:320
  27.7 0.7 collective-permute-start.10
  29.3 0.7 collective-permute-start.11
  30.9 23.5 %collective-permute-start.12 = (f32[64,512]{1,0:T(8,128)S(1)}, f32[64,512]{1,0:T(8,128)S(1)}, u32[]{:S(2)}, u32[]{:S(2)}) collective-permute-start(f32[64,512]{1,0:T(8,128)S(1)} %shard_map.61), channel_id=1, source_target_pairs={{2,0},{3,1},{10,8},{11,9},{18,16},{19,17},{26,24},{27,25}} | collective-permute-start | bytes 393224 | tf_op jit(solution)/shard_map/ppermute | solution.py:320
  55.4 4.3 %collective-permute-start.13 = (f32[128,128]{1,0:T(8,128)S(1)}, f32[128,128]{1,0:T(8,128)S(1)}, u32[]{:S(2)}, u32[]{:S(2)}) collective-permute-start(f32[128,128]{1,0:T(8,128)S(1)} %get-tuple-element.59), channel_id=1, source_target_pairs={{0,8},{8,0},{16,24},{24,16},{1,9},{9,1},{17,25},{25,17},{2,10},{10... | collective-permute-start | bytes 196616 | tf_op jit(solution)/shard_map/ppermute | solution.py:323
  57.0 4.3 %collective-permute-start.14 = (f32[128,128]{1,0:T(8,128)S(1)}, f32[128,128]{1,0:T(8,128)S(1)}, u32[]{:S(2)}, u32[]{:S(2)}) collective-permute-start(f32[128,128]{1,0:T(8,128)S(1)} %get-tuple-element.60), channel_id=1, source_target_pairs={{0,16},{8,24},{16,0},{24,8},{1,17},{9,25},{17,1},{25,9},{2,18},{10... | collective-permute-start | bytes 196616 | tf_op jit(solution)/shard_map/ppermute | solution.py:323
  58.5 5.2 %collective-permute-start.15 = (f32[128,128]{1,0:T(8,128)S(1)}, f32[128,128]{1,0:T(8,128)S(1)}, u32[]{:S(2)}, u32[]{:S(2)}) collective-permute-start(f32[128,128]{1,0:T(8,128)S(1)} %get-tuple-element.61), channel_id=1, source_target_pairs={{0,24},{8,16},{16,8},{24,0},{1,25},{9,17},{17,9},{25,1},{2,26},{10... | collective-permute-start | bytes 196616 | tf_op jit(solution)/shard_map/ppermute | solution.py:323
  63.7 1.4 %collective-permute-start.16 = (f32[256,128]{1,0:T(8,128)S(1)}, f32[256,128]{1,0:T(8,128)S(1)}, u32[]{:S(2)}, u32[]{:S(2)}) collective-permute-start(f32[256,128]{1,0:T(8,128)S(1)} %shard_map.63.mine), channel_id=1, source_target_pairs={{0,1},{1,0},{2,3},{3,2},{4,5},{5,4},{6,7},{7,6},{8,9},{9,8},{10,11... | collective-permute-start | bytes 393224 | tf_op jit(solution)/shard_map/ppermute | solution.py:317
  65.4 4.0 %collective-permute-start.17 = (f32[32,256]{1,0:T(8,128)S(1)}, f32[32,256]{1,0:T(8,128)S(1)}, u32[]{:S(2)}, u32[]{:S(2)}) collective-permute-start(f32[32,256]{1,0:T(8,128)S(1)} %get-tuple-element.65), channel_id=1, source_target_pairs={{0,8},{8,0},{16,24},{24,16},{1,9},{9,1},{17,25},{25,17},{2,10},{10... | collective-permute-start | bytes 98312 | tf_op jit(solution)/shard_map/ppermute | solution.py:323
  66.0 4.3 %collective-permute-start.18 = (f32[32,256]{1,0:T(8,128)S(1)}, f32[32,256]{1,0:T(8,128)S(1)}, u32[]{:S(2)}, u32[]{:S(2)}) collective-permute-start(f32[32,256]{1,0:T(8,128)S(1)} %get-tuple-element.66), channel_id=1, source_target_pairs={{0,16},{8,24},{16,0},{24,8},{1,17},{9,25},{17,1},{25,9},{2,18},{10... | collective-permute-start | bytes 98312 | tf_op jit(solution)/shard_map/ppermute | solution.py:323
  66.5 4.8 %collective-permute-start.19 = (f32[32,256]{1,0:T(8,128)S(1)}, f32[32,256]{1,0:T(8,128)S(1)}, u32[]{:S(2)}, u32[]{:S(2)}) collective-permute-start(f32[32,256]{1,0:T(8,128)S(1)} %get-tuple-element.67), channel_id=1, source_target_pairs={{0,24},{8,16},{16,8},{24,0},{1,25},{9,17},{17,9},{25,1},{2,26},{10... | collective-permute-start | bytes 98312 | tf_op jit(solution)/shard_map/ppermute | solution.py:323
  71.3 5.8 %collective-permute-start.22 = (f32[32,256]{1,0:T(8,128)S(1)}, f32[32,256]{1,0:T(8,128)S(1)}, u32[]{:S(2)}, u32[]{:S(2)}) collective-permute-start(f32[32,256]{1,0:T(8,128)S(1)} %add_add_fusion), channel_id=1, source_target_pairs={{0,6},{1,7},{2,4},{3,5},{4,2},{5,3},{6,0},{7,1},{8,14},{9,15},{10,... | collective-permute-start | bytes 98312 | tf_op jit(solution)/shard_map/ppermute | solution.py:326
  71.4 5.7 %collective-permute-start.21 = (f32[32,256]{1,0:T(8,128)S(1)}, f32[32,256]{1,0:T(8,128)S(1)}, u32[]{:S(2)}, u32[]{:S(2)}) collective-permute-start(f32[32,256]{1,0:T(8,128)S(1)} %add_add_fusion), channel_id=1, source_target_pairs={{0,4},{1,5},{2,6},{3,7},{4,0},{5,1},{6,2},{7,3},{8,12},{9,13},{10,... | collective-permute-start | bytes 98312 | tf_op jit(solution)/shard_map/ppermute | solution.py:326
  72.5 5.2 %collective-permute-start.20 = (f32[32,256]{1,0:T(8,128)S(1)}, f32[32,256]{1,0:T(8,128)S(1)}, u32[]{:S(2)}, u32[]{:S(2)}) collective-permute-start(f32[32,256]{1,0:T(8,128)S(1)} %add_add_fusion), channel_id=1, source_target_pairs={{0,2},{1,3},{2,0},{3,1},{4,6},{5,7},{6,4},{7,5},{8,10},{9,11},{10,... | collective-permute-start | bytes 98312 | tf_op jit(solution)/shard_map/ppermute | solution.py:326
  77.7 4.9 %collective-permute-start.25 = (f32[32,256]{1,0:T(8,128)S(1)}, f32[32,256]{1,0:T(8,128)S(1)}, u32[]{:S(2)}, u32[]{:S(2)}) collective-permute-start(f32[32,256]{1,0:T(8,128)S(1)} %add_multiply_fusion.refs_0_), channel_id=1, source_target_pairs={{0,24},{8,16},{16,8},{24,0},{1,25},{9,17},{17,9},{25,1},{2,26},{10... | collective-permute-start | bytes 98312 | tf_op jit(solution)/shard_map/ppermute | solution.py:323
  80.2 3.9 %collective-permute-start.24 = (f32[32,256]{1,0:T(8,128)S(1)}, f32[32,256]{1,0:T(8,128)S(1)}, u32[]{:S(2)}, u32[]{:S(2)}) collective-permute-start(f32[32,256]{1,0:T(8,128)S(1)} %add_multiply_fusion.refs_0_), channel_id=1, source_target_pairs={{0,16},{8,24},{16,0},{24,8},{1,17},{9,25},{17,1},{25,9},{2,18},{10... | collective-permute-start | bytes 98312 | tf_op jit(solution)/shard_map/ppermute | solution.py:323
  80.7 3.9 %collective-permute-start.23 = (f32[32,256]{1,0:T(8,128)S(1)}, f32[32,256]{1,0:T(8,128)S(1)}, u32[]{:S(2)}, u32[]{:S(2)}) collective-permute-start(f32[32,256]{1,0:T(8,128)S(1)} %add_multiply_fusion.refs_0_), channel_id=1, source_target_pairs={{0,8},{8,0},{16,24},{24,16},{1,9},{9,1},{17,25},{25,17},{2,10},{10... | collective-permute-start | bytes 98312 | tf_op jit(solution)/shard_map/ppermute | solution.py:323
  84.7 1.4 %collective-permute-start.26 = (f32[128,256]{1,0:T(8,128)S(1)}, f32[128,256]{1,0:T(8,128)S(1)}, u32[]{:S(2)}, u32[]{:S(2)}) collective-permute-start(f32[128,256]{1,0:T(8,128)S(1)} %shard_map.65.mine), channel_id=1, source_target_pairs={{0,1},{1,0},{2,3},{3,2},{4,5},{5,4},{6,7},{7,6},{8,9},{9,8},{10,11... | collective-permute-start | bytes 393224 | tf_op jit(solution)/shard_map/ppermute | solution.py:317

commit v4 on v3

--- a/solution.py
+++ b/solution.py
@@ -153,9 +153,18 @@
         mats[1, slots[side], index, part, :] = l
 
 
+def resident_roles_kernel(count, *refs):
+    sources, mats = (refs[:count], refs[count : 2 * count]), refs[-1]
+    mine = lax.axis_index("row") % 2
+    for side, slot in enumerate((mine, 1 - mine)):
+        for index in range(2):
+            value = sources[side][index][...] if count == 2 else sources[side][0][index]
+            mats[0, slot, index], mats[1, slot, index] = parts_of(value)
+
+
 def roles_and_vectors_kernel(count, *refs):
-    v_own, v_other, va, vb = refs[2 * count : 2 * count + 4]
-    roles_kernel(count, *refs[: 2 * count], *refs[-3:])
+    v_own, v_other, va, vb, mats = refs[2 * count :]
+    resident_roles_kernel(count, *refs[: 2 * count], mats)
     mine = lax.axis_index("row") % 2
     half = va.shape[0]
     own = v_own[pl.ds(pl.multiple_of(mine * half, half), half), :]
@@ -164,24 +173,28 @@
     vb[...] = jnp.where(mine == 0, other, own)
 
 
-def roles(owns, others, vectors=()):
+def resident_roles(owns, others, vectors=()):
+    n = others[0].shape[-1]
+    halves = [((v.shape[0] // 2, n), F32) for v in vectors]
+    body = roles_and_vectors_kernel if vectors else resident_roles_kernel
+    return call(
+        functools.partial(body, len(others)),
+        halves + [((2, 2, 2, n, n), BF16)],
+        *owns, *others, *vectors,
+    )
+
+
+def roles(owns, others):
     n = others[0].shape[-1]
     shape = (2, 2, 2, n, n)
-    halves = [(v.shape[0] // 2, n) for v in vectors]
-    body = roles_and_vectors_kernel if vectors else roles_kernel
     return pl.pallas_call(
-        functools.partial(body, len(others)),
-        out_shape=tuple(pltpu.VMEM(half, F32) for half in halves)
-        + (pltpu.VMEM(shape, BF16),),
-        in_specs=[HBM] * (2 * len(others)) + [VMEM] * len(vectors),
-        out_specs=(VMEM,) * (1 + len(halves)),
+        functools.partial(roles_kernel, len(others)),
+        out_shape=(pltpu.VMEM(shape, BF16),),
+        in_specs=[HBM] * (2 * len(others)),
+        out_specs=(VMEM,),
         scratch_shapes=[pltpu.VMEM(shape[1:], F32), pltpu.SemaphoreType.DMA((2, CHUNKS))],
         compiler_params=pltpu.CompilerParams(vmem_limit_bytes=20 << 20),
-    )(
-        *[pltpu.with_memory_space_constraint(x, pltpu.HBM) for x in owns],
-        *others,
-        *[pltpu.with_memory_space_constraint(x, pltpu.VMEM) for x in vectors],
-    )
+    )(*[pltpu.with_memory_space_constraint(x, pltpu.HBM) for x in owns], *others)
 
 
 def total(refs):
@@ -361,7 +374,7 @@
     a_re_other = swap_core(after(a_re, from_a))
     a_im_other = swap_core(a_im)
     v_other = swap_core(after(v_t, lo))
-    va, vb, a_mats = roles([a_re, a_im], [a_re_other, a_im_other], [v_t, v_other])
+    va, vb, a_mats = resident_roles([a_re, a_im], [a_re_other, a_im_other], [v_t, v_other])
     f_other = swap_core(after(factor, a_re_other, a_im_other))
     arrived = []
     for t in range(layers - 1):
@@ -375,7 +388,7 @@
             (b_own,) = call(b_kernel, [((2, n, n), F32)], after(fh, leaving), fl, ch, cl)
             b_other = swap_core(b_own)
         if t == 1:
-            (b_mats,) = roles([after(b_own, leaving, f_mats)], [b_other])
+            (b_mats,) = resident_roles([after(b_own, leaving, f_mats)], [b_other])
     u_a, u_b, leaving, weights = call(
         turn_kernel, [block] * 3 + [((2 * MOM * nodes, 128), F32)], *arrived, va, vb, f_mats, a_mats, b_mats
     )

time: 87.1 us -> 85.9 us (0.986)
  Pallas kernels: 21.5 us -> 18.7 us
  starting transfers between devices: 24.9 us -> 26.2 us
    pallas_call x3 -> x1, Pallas kernels: 6.13 us -> 2.04 us  [roles(): pl.pallas_call(functools.partial(roles_kernel, len(others)), out_shape=(p...]
    pallas_call x13 -> x15, Pallas kernels: 12 us -> 13.3 us  [call(): pl.pallas_call(kernel, out_shape=tuple((pltpu.VMEM(shape, dtype) for shap...]
    ppermute x8, starting transfers between devices: 4.56 us -> 5.77 us  [swap_core(): return lax.ppermute(value, 'row', [(r, r ^ 1) for r in range(rows)])]
  transfers between devices with their start and end apart: 27 -> 27, of which waited for: 17 -> 17; matrix products, arithmetic and copies ran while one was open for 1% -> 1% of each run, Pallas kernels for 12% -> 9%
where the time goes in v4:
time: 85.9 us; the launch traced here: 85.7 us
  waiting for transfers between devices  39.1 us (46%)
  starting transfers between devices  26.2 us (31%)
  Pallas kernels  18.7 us (22%)
  between operations  0.91 us (1%)
    ppermute x5, waiting for transfers between devices, hop(): lax.ppermute(value, 'row', [(2 * source + c, 2 * target + c) for c in ran...  22.7 us
    pallas_call x15, Pallas kernels, call(): pl.pallas_call(kernel, out_shape=tuple((pltpu.VMEM(shape, dtype) for shap...  13.3 us
    ppermute x9, starting transfers between devices, exchange_node(): return lax.ppermute(value, 'node', [(j, j ^ d) for j in range(nodes)])  10.7 us
    ppermute x9, waiting for transfers between devices, exchange_node(): return lax.ppermute(value, 'node', [(j, j ^ d) for j in range(nodes)])  10.5 us
    ppermute x8, starting transfers between devices, swap_core(): return lax.ppermute(value, 'row', [(r, r ^ 1) for r in range(rows)])  5.77 us
    ppermute x3, starting transfers between devices, exchange_layer(): return lax.ppermute(value, 'row', [(r, r ^ 2 * d) for r in range(rows)])  4.45 us
    ppermute x8, waiting for transfers between devices, swap_core(): return lax.ppermute(value, 'row', [(r, r ^ 1) for r in range(rows)])  4.02 us
    ppermute x5, starting transfers between devices, hop(): lax.ppermute(value, 'row', [(2 * source + c, 2 * target + c) for c in ran...  3.96 us
  transfers between devices with their start and end apart: 27, of which 17 were waited for; matrix products, arithmetic and copies ran while one was open for 1% of the time, Pallas kernels for 9%

profile of v4, /device:TPU:0, one launch (start us, length us, event | category | flops | bytes accessed | tf_op | source)
XLA Modules:
  0.0 85.7 jit_solution(2945117880829253620)
XLA Ops:
  0.6 2.7 %enter.1 = (bf16[2,512,512]{2,1,0:T(8,128)(2,1)S(1)}, bf16[2,512,512]{2,1,0:T(8,128)(2,1)S(1)}, bf16[512,512]{1,0:T(8,128)(2,1)S(1)}, bf16[512,512]{1,0:T(8,128)...) custom-call(f32[2,512,512]{2,1,0:T(8,128)} %bitcast.9, f32[512,512]{1,0:T(8,128)} %bitcast.12, f32[64,512]{1,0:T(8,128)} %bitcast.13), custom_call_target="tpu_custom_call" | custom-call | tf_op jit(solution)/shard_map/enter/pallas_call | solution.py:345
  3.4 0.6 collective-permute-start
  3.9 1.0 %shard_map.51.refs_0_ = f32[512,512]{1,0:T(8,128)S(1)} custom-call(bf16[2,512,512]{2,1,0:T(8,128)(2,1)S(1)} %get-tuple-element.53.fh, bf16[2,512,512]{2,1,0:T(8,128)(2,1)S(1)} %get-tuple-element.39.fl, bf16[512,512]{1,0:T(8,128)(2,1)S(1)} %get-tuple-element.40.ch, bf16[512,512]{1,0:T(8,128)(2,1)S(1)} %get-tuple-element.41.cl), custom_call_target="tpu_custom_call" | custom-call | tf_op jit(solution)/shard_map/pallas_call | solution.py:64
  4.9 0.2 collective-permute-done.g
  5.1 1.1 %shard_map.50 = (f32[64,512]{1,0:T(8,128)S(1)}, f32[64,512]{1,0:T(8,128)S(1)}) custom-call(f32[64,512]{1,0:T(8,128)S(1)} %get-tuple-element.47.vt.refs_4_, f32[128,512]{1,0:T(8,128)S(1)} %collective-permute-done.g, bf16[2,512,512]{2,1,0:T(8,128)(2,1)S(1)} %get-tuple-element.53.fh, bf16[2,512,512]{2,1,0:T(8,128)(2,1)S(1)} %get-tuple-element.39.fl, ...), custom_call_target="tpu_custom_call" | custom-call | tf_op jit(solution)/shard_map/pallas_call | solution.py:64
  6.2 0.0 copy-start
  6.2 1.0 %shard_map.52.refs_1_ = f32[512,512]{1,0:T(8,128)S(1)} custom-call(bf16[2,512,512]{2,1,0:T(8,128)(2,1)S(1)} %get-tuple-element.53.fh, bf16[2,512,512]{2,1,0:T(8,128)(2,1)S(1)} %get-tuple-element.39.fl, bf16[512,512]{1,0:T(8,128)(2,1)S(1)} %get-tuple-element.40.ch, bf16[512,512]{1,0:T(8,128)(2,1)S(1)} %get-tuple-element.41.cl), custom_call_target="tpu_custom_call" | custom-call | tf_op jit(solution)/shard_map/pallas_call | solution.py:64
  7.2 0.4 collective-permute-start.3
  7.6 0.1 collective-permute-start.4
  7.7 0.4 collective-permute-start.5
  8.1 0.7 collective-permute-start.2
  8.8 0.7 collective-permute-start.1
  9.5 0.4 collective-permute-done.3.refs_2_
  9.9 1.5 %collective-permute-done.4.refs_3_ = f32[512,512]{1,0:T(8,128)S(1)} collective-permute-done((f32[512,512]{1,0:T(8,128)S(1)}, f32[512,512]{1,0:T(8,128)S(1)}, u32[]{:S(2)}, u32[]{:S(2)}) %collective-permute-start.4) | collective-permute-done | bytes 1048608 | tf_op jit(solution)/shard_map/ppermute | solution.py:330
  11.4 2.8 %collective-permute-start.8 = (f32[2,512,512]{2,1,0:T(8,128)S(1)}, f32[2,512,512]{2,1,0:T(8,128)S(1)}, u32[]{:S(2)}, u32[]{:S(2)}) collective-permute-start(f32[2,512,512]{2,1,0:T(8,128)S(1)} %bitcast.11), channel_id=1, source_target_pairs={{0,1},{1,0},{2,3},{3,2},{4,5},{5,4},{6,7},{7,6},{8,9},{9,8},{10,11... | collective-permute-start | bytes 6291464 | tf_op jit(solution)/shard_map/ppermute | solution.py:330
  14.2 0.0 collective-permute-done.5.refs_5_
  14.2 0.6 shard_map.53
  14.8 0.9 %shard_map.54 = f32[64,512]{1,0:T(8,128)S(1)} custom-call(f32[64,512]{1,0:T(8,128)S(1)} %collective-permute-done.1.refs_0_, f32[64,512]{1,0:T(8,128)S(1)} %collective-permute-done.2.refs_1_, f32[32,512]{1,0:T(8,128)S(1)} %get-tuple-element.48.refs_2_.refs_1_.refs_4_, f32[32,512]{1,0:T(8,128)S(1)} %get-tuple-element.49.refs_3_.refs_2_.refs_5_, ...), custom_call_target="tpu_custom_call" | custom-call | tf_op jit(solution)/shard_map/pallas_call | solution.py:64
  15.8 1.8 %shard_map.57.refs_0_ = f32[2,512,512]{2,1,0:T(8,128)S(1)} custom-call(bf16[2,512,512]{2,1,0:T(8,128)(2,1)S(1)} %get-tuple-element.53.fh, bf16[2,512,512]{2,1,0:T(8,128)(2,1)S(1)} %get-tuple-element.39.fl, bf16[512,512]{1,0:T(8,128)(2,1)S(1)} %get-tuple-element.40.ch, bf16[512,512]{1,0:T(8,128)(2,1)S(1)} %get-tuple-element.41.cl), custom_call_target="tpu_custom_call" | custom-call | tf_op jit(solution)/shard_map/pallas_call | solution.py:64
  17.6 1.3 %collective-permute-start.9 = (f32[2,512,512]{2,1,0:T(8,128)S(1)}, f32[2,512,512]{2,1,0:T(8,128)S(1)}, u32[]{:S(2)}, u32[]{:S(2)}) collective-permute-start(f32[2,512,512]{2,1,0:T(8,128)S(1)} %shard_map.57.refs_0_), channel_id=1, source_target_pairs={{0,1},{1,0},{2,3},{3,2},{4,5},{5,4},{6,7},{7,6},{8,9},{9,8},{10,11... | collective-permute-start | bytes 6291464 | tf_op jit(solution)/shard_map/ppermute | solution.py:330
  18.9 0.7 collective-permute-start.6
  19.6 0.9 %shard_map.55 = f32[64,512]{1,0:T(8,128)S(1)} custom-call(f32[64,512]{1,0:T(8,128)S(1)} %collective-permute-done.6.refs_0_.refs_2_, f32[32,512]{1,0:T(8,128)S(1)} %get-tuple-element.48.refs_2_.refs_1_.refs_4_, f32[32,512]{1,0:T(8,128)S(1)} %get-tuple-element.49.refs_3_.refs_2_.refs_5_, bf16[2,2,2,512,512]{4,3,2,1,0:T(8,128)(2,1)S(1)} %get-tuple-element.50.refs_4_.refs_3_.refs_7_), custom_call_target="tpu_custom_call" | custom-call | tf_op jit(solution)/shard_map/pallas_call | solution.py:64
  20.5 0.7 collective-permute-start.7
  21.2 2.0 %shard_map.56.refs_6_ = bf16[2,2,2,512,512]{4,3,2,1,0:T(8,128)(2,1)S(1)} custom-call(f32[2,512,512]{2,1,0:T(8,128)} %bitcast.10, f32[2,512,512]{2,1,0:T(8,128)S(1)} %collective-permute-done.8.refs_1_), custom_call_target="tpu_custom_call" | custom-call | tf_op jit(solution)/shard_map/pallas_call | solution.py:190
  23.2 0.7 shard_map.58.refs_8_.b_mats.refs_5_
  23.9 2.2 %shard_map.59 = (f32[64,512]{1,0:T(8,128)S(1)}, f32[64,512]{1,0:T(8,128)S(1)}, f32[64,512]{1,0:T(8,128)S(1)}, f32[16,128]{1,0:T(8,128)S(1)}) custom-call(f32[64,512]{1,0:T(8,128)S(1)} %collective-permute-done.1.refs_0_, f32[64,512]{1,0:T(8,128)S(1)} %collective-permute-done.2.refs_1_, f32[64,512]{1,0:T(8,128)S(1)} %collective-permute-done.6.refs_0_.refs_2_, ...), custom_call_target="tpu_custom_call" | custom-call | tf_op jit(solution)/shard_map/pallas_call | solution.py:64
  26.1 0.7 collective-permute-start.10
  26.8 0.9 %shard_map.60 = f32[64,512]{1,0:T(8,128)S(1)} custom-call(f32[64,512]{1,0:T(8,128)S(1)} %collective-permute-done.10.r.refs_0_, f32[64,512]{1,0:T(8,128)S(1)} %get-tuple-element.56.ua.refs_3_, f32[64,512]{1,0:T(8,128)S(1)} %get-tuple-element.57.ub.refs_4_, bf16[2,2,2,512,512]{4,3,2,1,0:T(8,128)(2,1)S(1)} %shard_map.58.refs_8_.b_mats.refs_5_), custom_call_target="tpu_custom_call" | custom-call | tf_op jit(solution)/shard_map/pallas_call | solution.py:64
  27.7 0.7 collective-permute-start.11
  28.4 0.9 %shard_map.61 = f32[64,512]{1,0:T(8,128)S(1)} custom-call(f32[64,512]{1,0:T(8,128)S(1)} %collective-permute-done.11.r.refs_1_, f32[64,512]{1,0:T(8,128)S(1)} %get-tuple-element.56.ua.refs_3_, f32[64,512]{1,0:T(8,128)S(1)} %get-tuple-element.57.ub.refs_4_, bf16[2,2,2,512,512]{4,3,2,1,0:T(8,128)(2,1)S(1)} %shard_map.58.refs_8_.b_mats.refs_5_), custom_call_target="tpu_custom_call" | custom-call | tf_op jit(solution)/shard_map/pallas_call | solution.py:64
  29.3 1.3 %collective-permute-start.12 = (f32[64,512]{1,0:T(8,128)S(1)}, f32[64,512]{1,0:T(8,128)S(1)}, u32[]{:S(2)}, u32[]{:S(2)}) collective-permute-start(f32[64,512]{1,0:T(8,128)S(1)} %shard_map.61), channel_id=1, source_target_pairs={{2,0},{3,1},{10,8},{11,9},{18,16},{19,17},{26,24},{27,25}} | collective-permute-start | bytes 393224 | tf_op jit(solution)/shard_map/ppermute | solution.py:333
  30.6 22.7 %collective-permute-done.12.refs_2_ = f32[64,512]{1,0:T(8,128)S(1)} collective-permute-done((f32[64,512]{1,0:T(8,128)S(1)}, f32[64,512]{1,0:T(8,128)S(1)}, u32[]{:S(2)}, u32[]{:S(2)}) %collective-permute-start.12) | collective-permute-done | bytes 131104 | tf_op jit(solution)/shard_map/ppermute | solution.py:333
  53.3 0.9 %shard_map.62 = (f32[128,128]{1,0:T(8,128)S(1)}, f32[128,128]{1,0:T(8,128)S(1)}, f32[128,128]{1,0:T(8,128)S(1)}, f32[128,128]{1,0:T(8,128)S(1)}) custom-call(f32[64,512]{1,0:T(8,128)S(1)} %collective-permute-done.10.r.refs_0_, f32[64,512]{1,0:T(8,128)S(1)} %collective-permute-done.11.r.refs_1_, f32[64,512]{1,0:T(8,128)S(1)} %collective-permute-done.12.refs_2_, ...), custom_call_target="tpu_custom_call" | custom-call | tf_op jit(solution)/shard_map/pallas_call | solution.py:64
  54.3 1.6 %collective-permute-start.13 = (f32[128,128]{1,0:T(8,128)S(1)}, f32[128,128]{1,0:T(8,128)S(1)}, u32[]{:S(2)}, u32[]{:S(2)}) collective-permute-start(f32[128,128]{1,0:T(8,128)S(1)} %get-tuple-element.59), channel_id=1, source_target_pairs={{0,8},{8,0},{16,24},{24,16},{1,9},{9,1},{17,25},{25,17},{2,10},{10... | collective-permute-start | bytes 196616 | tf_op jit(solution)/shard_map/ppermute | solution.py:336
  55.8 1.5 %collective-permute-start.14 = (f32[128,128]{1,0:T(8,128)S(1)}, f32[128,128]{1,0:T(8,128)S(1)}, u32[]{:S(2)}, u32[]{:S(2)}) collective-permute-start(f32[128,128]{1,0:T(8,128)S(1)} %get-tuple-element.60), channel_id=1, source_target_pairs={{0,16},{8,24},{16,0},{24,8},{1,17},{9,25},{17,1},{25,9},{2,18},{10... | collective-permute-start | bytes 196616 | tf_op jit(solution)/shard_map/ppermute | solution.py:336
  57.4 0.4 collective-permute-start.15
  57.8 0.8 collective-permute-done.13.refs_1_
  58.6 1.5 %collective-permute-done.14.refs_2_ = f32[128,128]{1,0:T(8,128)S(1)} collective-permute-done((f32[128,128]{1,0:T(8,128)S(1)}, f32[128,128]{1,0:T(8,128)S(1)}, u32[]{:S(2)}, u32[]{:S(2)}) %collective-permute-start.14) | collective-permute-done | bytes 65568 | tf_op jit(solution)/shard_map/ppermute | solution.py:336
  60.1 2.4 %collective-permute-done.15.refs_3_ = f32[128,128]{1,0:T(8,128)S(1)} collective-permute-done((f32[128,128]{1,0:T(8,128)S(1)}, f32[128,128]{1,0:T(8,128)S(1)}, u32[]{:S(2)}, u32[]{:S(2)}) %collective-permute-start.15) | collective-permute-done | bytes 65568 | tf_op jit(solution)/shard_map/ppermute | solution.py:336
  62.5 0.1 shard_map.63.mine
  62.6 0.1 collective-permute-start.16
  62.7 1.3 %collective-permute-done.16.other = f32[256,128]{1,0:T(8,128)S(1)} collective-permute-done((f32[256,128]{1,0:T(8,128)S(1)}, f32[256,128]{1,0:T(8,128)S(1)}, u32[]{:S(2)}, u32[]{:S(2)}) %collective-permute-start.16) | collective-permute-done | bytes 131104 | tf_op jit(solution)/shard_map/ppermute | solution.py:330
  64.0 0.3 shard_map.64
  64.3 0.6 collective-permute-start.17
  64.9 0.5 collective-permute-start.18
  65.4 2.5 %collective-permute-start.19 = (f32[32,256]{1,0:T(8,128)S(1)}, f32[32,256]{1,0:T(8,128)S(1)}, u32[]{:S(2)}, u32[]{:S(2)}) collective-permute-start(f32[32,256]{1,0:T(8,128)S(1)} %get-tuple-element.67), channel_id=1, source_target_pairs={{0,24},{8,16},{16,8},{24,0},{1,25},{9,17},{17,9},{25,1},{2,26},{10... | collective-permute-start | bytes 98312 | tf_op jit(solution)/shard_map/ppermute | solution.py:336
  67.9 0.4 collective-permute-done.17
  68.3 0.9 %collective-permute-done.18 = f32[32,256]{1,0:T(8,128)S(1)} collective-permute-done((f32[32,256]{1,0:T(8,128)S(1)}, f32[32,256]{1,0:T(8,128)S(1)}, u32[]{:S(2)}, u32[]{:S(2)}) %collective-permute-start.18) | collective-permute-done | bytes 32800 | tf_op jit(solution)/shard_map/ppermute | solution.py:336
  69.2 1.0 %collective-permute-done.19 = f32[32,256]{1,0:T(8,128)S(1)} collective-permute-done((f32[32,256]{1,0:T(8,128)S(1)}, f32[32,256]{1,0:T(8,128)S(1)}, u32[]{:S(2)}, u32[]{:S(2)}) %collective-permute-start.19) | collective-permute-done | bytes 32800 | tf_op jit(solution)/shard_map/ppermute | solution.py:336
  70.2 0.1 collective-permute-start.22
  70.3 1.0 %collective-permute-start.21 = (f32[32,256]{1,0:T(8,128)S(1)}, f32[32,256]{1,0:T(8,128)S(1)}, u32[]{:S(2)}, u32[]{:S(2)}) collective-permute-start(f32[32,256]{1,0:T(8,128)S(1)} %add_add_fusion), channel_id=1, source_target_pairs={{0,4},{1,5},{2,6},{3,7},{4,0},{5,1},{6,2},{7,3},{8,12},{9,13},{10,... | collective-permute-start | bytes 98312 | tf_op jit(solution)/shard_map/ppermute | solution.py:339
  71.3 3.3 %collective-permute-start.20 = (f32[32,256]{1,0:T(8,128)S(1)}, f32[32,256]{1,0:T(8,128)S(1)}, u32[]{:S(2)}, u32[]{:S(2)}) collective-permute-start(f32[32,256]{1,0:T(8,128)S(1)} %add_add_fusion), channel_id=1, source_target_pairs={{0,2},{1,3},{2,0},{3,1},{4,6},{5,7},{6,4},{7,5},{8,10},{9,11},{10,... | collective-permute-start | bytes 98312 | tf_op jit(solution)/shard_map/ppermute | solution.py:339
  74.7 1.3 %collective-permute-done.22 = f32[32,256]{1,0:T(8,128)S(1)} collective-permute-done((f32[32,256]{1,0:T(8,128)S(1)}, f32[32,256]{1,0:T(8,128)S(1)}, u32[]{:S(2)}, u32[]{:S(2)}) %collective-permute-start.22) | collective-permute-done | bytes 32800 | tf_op jit(solution)/shard_map/ppermute | solution.py:339
  76.0 0.6 collective-permute-done.20
  76.6 2.5 %collective-permute-start.25 = (f32[32,256]{1,0:T(8,128)S(1)}, f32[32,256]{1,0:T(8,128)S(1)}, u32[]{:S(2)}, u32[]{:S(2)}) collective-permute-start(f32[32,256]{1,0:T(8,128)S(1)} %add_multiply_fusion.refs_0_), channel_id=1, source_target_pairs={{0,24},{8,16},{16,8},{24,0},{1,25},{9,17},{17,9},{25,1},{2,26},{10... | collective-permute-start | bytes 98312 | tf_op jit(solution)/shard_map/ppermute | solution.py:336
  79.1 0.5 collective-permute-start.24
  79.6 0.5 collective-permute-start.23
  80.1 1.3 %collective-permute-done.25.refs_3_ = f32[32,256]{1,0:T(8,128)S(1)} collective-permute-done((f32[32,256]{1,0:T(8,128)S(1)}, f32[32,256]{1,0:T(8,128)S(1)}, u32[]{:S(2)}, u32[]{:S(2)}) %collective-permute-start.25) | collective-permute-done | bytes 32800 | tf_op jit(solution)/shard_map/ppermute | solution.py:336
  81.5 1.6 %collective-permute-done.24.refs_2_ = f32[32,256]{1,0:T(8,128)S(1)} collective-permute-done((f32[32,256]{1,0:T(8,128)S(1)}, f32[32,256]{1,0:T(8,128)S(1)}, u32[]{:S(2)}, u32[]{:S(2)}) %collective-permute-start.24) | collective-permute-done | bytes 32800 | tf_op jit(solution)/shard_map/ppermute | solution.py:336
  83.0 0.5 collective-permute-done.23.refs_1_
  83.6 0.1 collective-permute-start.26
  83.6 0.8 copy.5
  84.4 0.6 collective-permute-done.26.other
  85.0 0.7 join.1
  (13 shorter events, 0.1 us)
Async XLA Ops:
  3.4 1.7 %collective-permute-start = (f32[128,512]{1,0:T(8,128)S(1)}, f32[128,512]{1,0:T(8,128)S(1)}, u32[]{:S(2)}, u32[]{:S(2)}) collective-permute-start(f32[128,512]{1,0:T(8,128)S(1)} %get-tuple-element.36), channel_id=1, source_target_pairs={{0,1},{1,0},{2,3},{3,2},{4,5},{5,4},{6,7},{7,6},{8,9},{9,8},{10,11... | collective-permute-start | bytes 786440 | tf_op jit(solution)/shard_map/ppermute | solution.py:330
  6.2 5.2 %copy-start = (f32[1,1,2,512,512]{4,3,2,1,0:T(8,128)S(1)}, f32[1,1,2,512,512]{4,3,2,1,0:T(8,128)}, u32[]{:S(2)}) copy-start(f32[1,1,2,512,512]{4,3,2,1,0:T(8,128)} %param.3) | copy-start | bytes 6291460
  7.2 2.7 %collective-permute-start.3 = (f32[512,512]{1,0:T(8,128)S(1)}, f32[512,512]{1,0:T(8,128)S(1)}, u32[]{:S(2)}, u32[]{:S(2)}) collective-permute-start(f32[512,512]{1,0:T(8,128)S(1)} %shard_map.51.refs_0_), channel_id=1, source_target_pairs={{0,1},{1,0},{2,3},{3,2},{4,5},{5,4},{6,7},{7,6},{8,9},{9,8},{10,11... | collective-permute-start | bytes 3145736 | tf_op jit(solution)/shard_map/ppermute | solution.py:330
  7.6 3.8 %collective-permute-start.4 = (f32[512,512]{1,0:T(8,128)S(1)}, f32[512,512]{1,0:T(8,128)S(1)}, u32[]{:S(2)}, u32[]{:S(2)}) collective-permute-start(f32[512,512]{1,0:T(8,128)S(1)} %shard_map.52.refs_1_), channel_id=1, source_target_pairs={{0,1},{1,0},{2,3},{3,2},{4,5},{5,4},{6,7},{7,6},{8,9},{9,8},{10,11... | collective-permute-start | bytes 3145736 | tf_op jit(solution)/shard_map/ppermute | solution.py:330
  7.7 6.5 %collective-permute-start.5 = (f32[64,512]{1,0:T(8,128)S(1)}, f32[64,512]{1,0:T(8,128)S(1)}, u32[]{:S(2)}, u32[]{:S(2)}) collective-permute-start(f32[64,512]{1,0:T(8,128)S(1)} %get-tuple-element.47.vt.refs_4_), channel_id=1, source_target_pairs={{0,1},{1,0},{2,3},{3,2},{4,5},{5,4},{6,7},{7,6},{8,9},{9,8},{10,11... | collective-permute-start | bytes 393224 | tf_op jit(solution)/shard_map/ppermute | solution.py:330
  8.1 6.7 %collective-permute-start.2 = (f32[64,512]{1,0:T(8,128)S(1)}, f32[64,512]{1,0:T(8,128)S(1)}, u32[]{:S(2)}, u32[]{:S(2)}) collective-permute-start(f32[64,512]{1,0:T(8,128)S(1)} %get-tuple-element.43), channel_id=1, source_target_pairs={{1,3},{9,11},{17,19},{25,27}} | collective-permute-start | bytes 393224 | tf_op jit(solution)/shard_map/ppermute | solution.py:371
  8.8 6.1 %collective-permute-start.1 = (f32[64,512]{1,0:T(8,128)S(1)}, f32[64,512]{1,0:T(8,128)S(1)}, u32[]{:S(2)}, u32[]{:S(2)}) collective-permute-start(f32[64,512]{1,0:T(8,128)S(1)} %get-tuple-element.42), channel_id=1, source_target_pairs={{1,2},{9,10},{17,18},{25,26}} | collective-permute-start | bytes 393224 | tf_op jit(solution)/shard_map/ppermute | solution.py:370
  11.4 9.8 %collective-permute-start.8 = (f32[2,512,512]{2,1,0:T(8,128)S(1)}, f32[2,512,512]{2,1,0:T(8,128)S(1)}, u32[]{:S(2)}, u32[]{:S(2)}) collective-permute-start(f32[2,512,512]{2,1,0:T(8,128)S(1)} %bitcast.11), channel_id=1, source_target_pairs={{0,1},{1,0},{2,3},{3,2},{4,5},{5,4},{6,7},{7,6},{8,9},{9,8},{10,11... | collective-permute-start | bytes 6291464 | tf_op jit(solution)/shard_map/ppermute | solution.py:330
  17.6 5.6 %collective-permute-start.9 = (f32[2,512,512]{2,1,0:T(8,128)S(1)}, f32[2,512,512]{2,1,0:T(8,128)S(1)}, u32[]{:S(2)}, u32[]{:S(2)}) collective-permute-start(f32[2,512,512]{2,1,0:T(8,128)S(1)} %shard_map.57.refs_0_), channel_id=1, source_target_pairs={{0,1},{1,0},{2,3},{3,2},{4,5},{5,4},{6,7},{7,6},{8,9},{9,8},{10,11... | collective-permute-start | bytes 6291464 | tf_op jit(solution)/shard_map/ppermute | solution.py:330
  18.9 0.7 collective-permute-start.6
  20.5 3.4 %collective-permute-start.7 = (f32[64,512]{1,0:T(8,128)S(1)}, f32[64,512]{1,0:T(8,128)S(1)}, u32[]{:S(2)}, u32[]{:S(2)}) collective-permute-start(f32[64,512]{1,0:T(8,128)S(1)} %shard_map.55), channel_id=1, source_target_pairs={{4,6},{5,7},{12,14},{13,15},{20,22},{21,23},{28,30},{29,31}} | collective-permute-start | bytes 393224 | tf_op jit(solution)/shard_map/ppermute | solution.py:333
  26.1 0.7 collective-permute-start.10
  27.7 0.7 collective-permute-start.11
  29.3 24.0 %collective-permute-start.12 = (f32[64,512]{1,0:T(8,128)S(1)}, f32[64,512]{1,0:T(8,128)S(1)}, u32[]{:S(2)}, u32[]{:S(2)}) collective-permute-start(f32[64,512]{1,0:T(8,128)S(1)} %shard_map.61), channel_id=1, source_target_pairs={{2,0},{3,1},{10,8},{11,9},{18,16},{19,17},{26,24},{27,25}} | collective-permute-start | bytes 393224 | tf_op jit(solution)/shard_map/ppermute | solution.py:333
  54.3 4.3 %collective-permute-start.13 = (f32[128,128]{1,0:T(8,128)S(1)}, f32[128,128]{1,0:T(8,128)S(1)}, u32[]{:S(2)}, u32[]{:S(2)}) collective-permute-start(f32[128,128]{1,0:T(8,128)S(1)} %get-tuple-element.59), channel_id=1, source_target_pairs={{0,8},{8,0},{16,24},{24,16},{1,9},{9,1},{17,25},{25,17},{2,10},{10... | collective-permute-start | bytes 196616 | tf_op jit(solution)/shard_map/ppermute | solution.py:336
  55.8 4.3 %collective-permute-start.14 = (f32[128,128]{1,0:T(8,128)S(1)}, f32[128,128]{1,0:T(8,128)S(1)}, u32[]{:S(2)}, u32[]{:S(2)}) collective-permute-start(f32[128,128]{1,0:T(8,128)S(1)} %get-tuple-element.60), channel_id=1, source_target_pairs={{0,16},{8,24},{16,0},{24,8},{1,17},{9,25},{17,1},{25,9},{2,18},{10... | collective-permute-start | bytes 196616 | tf_op jit(solution)/shard_map/ppermute | solution.py:336
  57.4 5.2 %collective-permute-start.15 = (f32[128,128]{1,0:T(8,128)S(1)}, f32[128,128]{1,0:T(8,128)S(1)}, u32[]{:S(2)}, u32[]{:S(2)}) collective-permute-start(f32[128,128]{1,0:T(8,128)S(1)} %get-tuple-element.61), channel_id=1, source_target_pairs={{0,24},{8,16},{16,8},{24,0},{1,25},{9,17},{17,9},{25,1},{2,26},{10... | collective-permute-start | bytes 196616 | tf_op jit(solution)/shard_map/ppermute | solution.py:336
  62.6 1.4 %collective-permute-start.16 = (f32[256,128]{1,0:T(8,128)S(1)}, f32[256,128]{1,0:T(8,128)S(1)}, u32[]{:S(2)}, u32[]{:S(2)}) collective-permute-start(f32[256,128]{1,0:T(8,128)S(1)} %shard_map.63.mine), channel_id=1, source_target_pairs={{0,1},{1,0},{2,3},{3,2},{4,5},{5,4},{6,7},{7,6},{8,9},{9,8},{10,11... | collective-permute-start | bytes 393224 | tf_op jit(solution)/shard_map/ppermute | solution.py:330
  64.3 4.0 %collective-permute-start.17 = (f32[32,256]{1,0:T(8,128)S(1)}, f32[32,256]{1,0:T(8,128)S(1)}, u32[]{:S(2)}, u32[]{:S(2)}) collective-permute-start(f32[32,256]{1,0:T(8,128)S(1)} %get-tuple-element.65), channel_id=1, source_target_pairs={{0,8},{8,0},{16,24},{24,16},{1,9},{9,1},{17,25},{25,17},{2,10},{10... | collective-permute-start | bytes 98312 | tf_op jit(solution)/shard_map/ppermute | solution.py:336
  64.9 4.3 %collective-permute-start.18 = (f32[32,256]{1,0:T(8,128)S(1)}, f32[32,256]{1,0:T(8,128)S(1)}, u32[]{:S(2)}, u32[]{:S(2)}) collective-permute-start(f32[32,256]{1,0:T(8,128)S(1)} %get-tuple-element.66), channel_id=1, source_target_pairs={{0,16},{8,24},{16,0},{24,8},{1,17},{9,25},{17,1},{25,9},{2,18},{10... | collective-permute-start | bytes 98312 | tf_op jit(solution)/shard_map/ppermute | solution.py:336
  65.4 4.8 %collective-permute-start.19 = (f32[32,256]{1,0:T(8,128)S(1)}, f32[32,256]{1,0:T(8,128)S(1)}, u32[]{:S(2)}, u32[]{:S(2)}) collective-permute-start(f32[32,256]{1,0:T(8,128)S(1)} %get-tuple-element.67), channel_id=1, source_target_pairs={{0,24},{8,16},{16,8},{24,0},{1,25},{9,17},{17,9},{25,1},{2,26},{10... | collective-permute-start | bytes 98312 | tf_op jit(solution)/shard_map/ppermute | solution.py:336
  70.2 5.8 %collective-permute-start.22 = (f32[32,256]{1,0:T(8,128)S(1)}, f32[32,256]{1,0:T(8,128)S(1)}, u32[]{:S(2)}, u32[]{:S(2)}) collective-permute-start(f32[32,256]{1,0:T(8,128)S(1)} %add_add_fusion), channel_id=1, source_target_pairs={{0,6},{1,7},{2,4},{3,5},{4,2},{5,3},{6,0},{7,1},{8,14},{9,15},{10,... | collective-permute-start | bytes 98312 | tf_op jit(solution)/shard_map/ppermute | solution.py:339
  70.3 5.7 %collective-permute-start.21 = (f32[32,256]{1,0:T(8,128)S(1)}, f32[32,256]{1,0:T(8,128)S(1)}, u32[]{:S(2)}, u32[]{:S(2)}) collective-permute-start(f32[32,256]{1,0:T(8,128)S(1)} %add_add_fusion), channel_id=1, source_target_pairs={{0,4},{1,5},{2,6},{3,7},{4,0},{5,1},{6,2},{7,3},{8,12},{9,13},{10,... | collective-permute-start | bytes 98312 | tf_op jit(solution)/shard_map/ppermute | solution.py:339
  71.3 5.2 %collective-permute-start.20 = (f32[32,256]{1,0:T(8,128)S(1)}, f32[32,256]{1,0:T(8,128)S(1)}, u32[]{:S(2)}, u32[]{:S(2)}) collective-permute-start(f32[32,256]{1,0:T(8,128)S(1)} %add_add_fusion), channel_id=1, source_target_pairs={{0,2},{1,3},{2,0},{3,1},{4,6},{5,7},{6,4},{7,5},{8,10},{9,11},{10,... | collective-permute-start | bytes 98312 | tf_op jit(solution)/shard_map/ppermute | solution.py:339
  76.6 4.9 %collective-permute-start.25 = (f32[32,256]{1,0:T(8,128)S(1)}, f32[32,256]{1,0:T(8,128)S(1)}, u32[]{:S(2)}, u32[]{:S(2)}) collective-permute-start(f32[32,256]{1,0:T(8,128)S(1)} %add_multiply_fusion.refs_0_), channel_id=1, source_target_pairs={{0,24},{8,16},{16,8},{24,0},{1,25},{9,17},{17,9},{25,1},{2,26},{10... | collective-permute-start | bytes 98312 | tf_op jit(solution)/shard_map/ppermute | solution.py:336
  79.1 3.9 %collective-permute-start.24 = (f32[32,256]{1,0:T(8,128)S(1)}, f32[32,256]{1,0:T(8,128)S(1)}, u32[]{:S(2)}, u32[]{:S(2)}) collective-permute-start(f32[32,256]{1,0:T(8,128)S(1)} %add_multiply_fusion.refs_0_), channel_id=1, source_target_pairs={{0,16},{8,24},{16,0},{24,8},{1,17},{9,25},{17,1},{25,9},{2,18},{10... | collective-permute-start | bytes 98312 | tf_op jit(solution)/shard_map/ppermute | solution.py:336
  79.6 3.9 %collective-permute-start.23 = (f32[32,256]{1,0:T(8,128)S(1)}, f32[32,256]{1,0:T(8,128)S(1)}, u32[]{:S(2)}, u32[]{:S(2)}) collective-permute-start(f32[32,256]{1,0:T(8,128)S(1)} %add_multiply_fusion.refs_0_), channel_id=1, source_target_pairs={{0,8},{8,0},{16,24},{24,16},{1,9},{9,1},{17,25},{25,17},{2,10},{10... | collective-permute-start | bytes 98312 | tf_op jit(solution)/shard_map/ppermute | solution.py:336
  83.6 1.4 %collective-permute-start.26 = (f32[128,256]{1,0:T(8,128)S(1)}, f32[128,256]{1,0:T(8,128)S(1)}, u32[]{:S(2)}, u32[]{:S(2)}) collective-permute-start(f32[128,256]{1,0:T(8,128)S(1)} %shard_map.65.mine), channel_id=1, source_target_pairs={{0,1},{1,0},{2,3},{3,2},{4,5},{5,4},{6,7},{7,6},{8,9},{9,8},{10,11... | collective-permute-start | bytes 393224 | tf_op jit(solution)/shard_map/ppermute | solution.py:330

commit v5 on v4

--- a/solution.py
+++ b/solution.py
@@ -101,7 +101,21 @@
     g[...] = times(u, read((ch, cl)), NN)
 
 
-def leave_kernel(vt, g, fh, fl, ch, cl, lo, hi):
+def only_on(layer, outs, compute):
+    mine = lax.axis_index("row") // 2 == layer
+    pl.when(mine)(compute)
+
+    @pl.when(jnp.logical_not(mine))
+    def _():
+        for out in outs:
+            out[...] = jnp.zeros_like(out)
+
+
+def leave_kernel(*refs):
+    only_on(0, refs[-2:], functools.partial(leave_body, *refs))
+
+
+def leave_body(vt, g, fh, fl, ch, cl, lo, hi):
     y = add_real(g[...], vt[...])
     w = times(apply_to(y, tuple((fh[part], fl[part]) for part in range(2)), NT), read((ch, cl)), NN)
     half = lo.shape[0] // 2
@@ -204,7 +218,11 @@
     return value
 
 
-def forward_kernel(*refs):
+def forward_kernel(layer, *refs):
+    only_on(layer, refs[-1:], functools.partial(forward_body, *refs))
+
+
+def forward_body(*refs):
     *cs, va, vb, a_mats, out = refs
     y = apply_to(add_real(total(cs), va[...]), block_of(a_mats, 0), NN)
     out[...] = apply_to(add_real(y, vb[...]), block_of(a_mats, 1), NN)
@@ -227,7 +245,11 @@
     s[...] = u_a + apply_to(u_b, block_of(b_mats, 0), NN)
 
 
-def backward_kernel(r, ua, ub, b_mats, xa):
+def backward_kernel(layer, *refs):
+    only_on(layer, refs[-1:], functools.partial(backward_body, *refs))
+
+
+def backward_body(r, ua, ub, b_mats, xa):
     x_b = ub[...] + apply_to(r[...], block_of(b_mats, 1), NN)
     xa[...] = ua[...] + apply_to(x_b, block_of(b_mats, 0), NN)
 
@@ -382,7 +404,9 @@
             got = [hop(leaving, t, t + 1)]
         arrived += got
         if t < layers - 2:
-            (leaving,) = call(forward_kernel, [block], *got, va, vb, a_mats)
+            (leaving,) = call(
+                functools.partial(forward_kernel, t + 1), [block], *got, va, vb, a_mats
+            )
         if t == 0:
             (f_mats,) = roles([after(factor, leaving)], [f_other])
             (b_own,) = call(b_kernel, [((2, n, n), F32)], after(fh, leaving), fl, ch, cl)
@@ -398,7 +422,9 @@
         got = hop(leaving, t, t - 1)
         arrived.append(got)
         if t > 1:
-            (leaving,) = call(backward_kernel, [block], got, u_a, u_b, b_mats)
+            (leaving,) = call(
+                functools.partial(backward_kernel, t - 1), [block], got, u_a, u_b, b_mats
+            )
     share = n // nodes
     shares = nodes if share % 128 == 0 else 0
     x_both = ((4 * half, n), F32)

time: 85.9 us -> 84.9 us (0.988)
  waiting for transfers between devices: 39.1 us -> 42.7 us
  Pallas kernels: 18.7 us -> 15.2 us
  starting transfers between devices: 26.2 us -> 25.1 us
    pallas_call x15, Pallas kernels: 13.3 us -> 9.76 us  [call(): pl.pallas_call(kernel, out_shape=tuple((pltpu.VMEM(shape, dtype) for shap...]
    ppermute x5, waiting for transfers between devices: 22.7 us -> 26 us  [hop(): lax.ppermute(value, 'row', [(2 * source + c, 2 * target + c) for c in ran...]
    ppermute x8, starting transfers between devices: 5.77 us -> 4.7 us  [swap_core(): return lax.ppermute(value, 'row', [(r, r ^ 1) for r in range(rows)])]
  transfers between devices with their start and end apart: 27 -> 27, of which waited for: 17 -> 18; matrix products, arithmetic and copies ran while one was open for 1% -> 1% of each run, Pallas kernels for 9% -> 7%
where the time goes in v5:
time: 84.9 us; the launch traced here: 84.7 us
  waiting for transfers between devices  42.7 us (50%)
  starting transfers between devices  25.1 us (30%)
  Pallas kernels  15.2 us (18%)
  between operations  0.9 us (1%)
    ppermute x5, waiting for transfers between devices, hop(): lax.ppermute(value, 'row', [(2 * source + c, 2 * target + c) for c in ran...  26 us
    ppermute x9, starting transfers between devices, exchange_node(): return lax.ppermute(value, 'node', [(j, j ^ d) for j in range(nodes)])  10.7 us
    ppermute x9, waiting for transfers between devices, exchange_node(): return lax.ppermute(value, 'node', [(j, j ^ d) for j in range(nodes)])  10.5 us
    pallas_call x15, Pallas kernels, call(): pl.pallas_call(kernel, out_shape=tuple((pltpu.VMEM(shape, dtype) for shap...  9.76 us
    ppermute x8, starting transfers between devices, swap_core(): return lax.ppermute(value, 'row', [(r, r ^ 1) for r in range(rows)])  4.7 us
    ppermute x3, starting transfers between devices, exchange_layer(): return lax.ppermute(value, 'row', [(r, r ^ 2 * d) for r in range(rows)])  4.45 us
    ppermute x8, waiting for transfers between devices, swap_core(): return lax.ppermute(value, 'row', [(r, r ^ 1) for r in range(rows)])  4.35 us
    ppermute x5, starting transfers between devices, hop(): lax.ppermute(value, 'row', [(2 * source + c, 2 * target + c) for c in ran...  3.96 us
  transfers between devices with their start and end apart: 27, of which 18 were waited for; matrix products, arithmetic and copies ran while one was open for 1% of the time, Pallas kernels for 7%

profile of v5, /device:TPU:0, one launch (start us, length us, event | category | flops | bytes accessed | tf_op | source)
XLA Modules:
  0.0 84.7 jit_solution(16811619226037699229)
XLA Ops:
  0.6 2.7 %enter.1 = (bf16[2,512,512]{2,1,0:T(8,128)(2,1)S(1)}, bf16[2,512,512]{2,1,0:T(8,128)(2,1)S(1)}, bf16[512,512]{1,0:T(8,128)(2,1)S(1)}, bf16[512,512]{1,0:T(8,128)...) custom-call(f32[2,512,512]{2,1,0:T(8,128)} %bitcast.9, f32[512,512]{1,0:T(8,128)} %bitcast.12, f32[64,512]{1,0:T(8,128)} %bitcast.13), custom_call_target="tpu_custom_call" | custom-call | tf_op jit(solution)/shard_map/enter/pallas_call | solution.py:367
  3.4 0.6 collective-permute-start
  3.9 1.0 %shard_map.51.refs_0_ = f32[512,512]{1,0:T(8,128)S(1)} custom-call(bf16[2,512,512]{2,1,0:T(8,128)(2,1)S(1)} %get-tuple-element.53.refs_2_.fh, bf16[2,512,512]{2,1,0:T(8,128)(2,1)S(1)} %get-tuple-element.39.refs_3_.fl, bf16[512,512]{1,0:T(8,128)(2,1)S(1)} %get-tuple-element.40.refs_4_.ch, bf16[512,512]{1,0:T(8,128)(2,1)S(1)} %get-tuple-element.41.refs_5_.cl), custom_call_target="tpu_custom_call" | custom-call | tf_op jit(solution)/shard_map/pallas_call | solution.py:64
  4.9 0.2 collective-permute-done.refs_1_
  5.1 1.1 %shard_map.50 = (f32[64,512]{1,0:T(8,128)S(1)}, f32[64,512]{1,0:T(8,128)S(1)}) custom-call(f32[64,512]{1,0:T(8,128)S(1)} %get-tuple-element.47.refs_0_.refs_4_, f32[128,512]{1,0:T(8,128)S(1)} %collective-permute-done.refs_1_, bf16[2,512,512]{2,1,0:T(8,128)(2,1)S(1)} %get-tuple-element.53.refs_2_.fh, bf16[2,512,512]{2,1,0:T(8,128)(2,1)S(1)} %get-tuple-element.39.refs_3_.fl, ...), custom_call_target="tpu_custom_call" | custom-call | tf_op jit(solution)/shard_map/pallas_call | solution.py:64
  6.2 0.0 copy-start
  6.2 1.0 %shard_map.52.refs_1_ = f32[512,512]{1,0:T(8,128)S(1)} custom-call(bf16[2,512,512]{2,1,0:T(8,128)(2,1)S(1)} %get-tuple-element.53.refs_2_.fh, bf16[2,512,512]{2,1,0:T(8,128)(2,1)S(1)} %get-tuple-element.39.refs_3_.fl, bf16[512,512]{1,0:T(8,128)(2,1)S(1)} %get-tuple-element.40.refs_4_.ch, bf16[512,512]{1,0:T(8,128)(2,1)S(1)} %get-tuple-element.41.refs_5_.cl), custom_call_target="tpu_custom_call" | custom-call | tf_op jit(solution)/shard_map/pallas_call | solution.py:64
  7.2 0.4 collective-permute-start.3
  7.6 0.1 collective-permute-start.4
  7.8 0.4 collective-permute-start.5
  8.1 0.7 collective-permute-start.2
  8.8 0.7 collective-permute-start.1
  9.5 0.4 collective-permute-done.3.refs_2_
  9.9 1.5 %collective-permute-done.4.refs_3_ = f32[512,512]{1,0:T(8,128)S(1)} collective-permute-done((f32[512,512]{1,0:T(8,128)S(1)}, f32[512,512]{1,0:T(8,128)S(1)}, u32[]{:S(2)}, u32[]{:S(2)}) %collective-permute-start.4) | collective-permute-done | bytes 1048608 | tf_op jit(solution)/shard_map/ppermute | solution.py:352
  11.4 1.8 %collective-permute-start.8 = (f32[2,512,512]{2,1,0:T(8,128)S(1)}, f32[2,512,512]{2,1,0:T(8,128)S(1)}, u32[]{:S(2)}, u32[]{:S(2)}) collective-permute-start(f32[2,512,512]{2,1,0:T(8,128)S(1)} %bitcast.11), channel_id=1, source_target_pairs={{0,1},{1,0},{2,3},{3,2},{4,5},{5,4},{6,7},{7,6},{8,9},{9,8},{10,11... | collective-permute-start | bytes 6291464 | tf_op jit(solution)/shard_map/ppermute | solution.py:352
  13.2 0.0 collective-permute-done.5.refs_5_
  13.2 0.6 shard_map.53
  13.8 0.0 collective-permute-done.1.refs_0_
  13.8 1.8 %shard_map.57.refs_0_ = f32[2,512,512]{2,1,0:T(8,128)S(1)} custom-call(bf16[2,512,512]{2,1,0:T(8,128)(2,1)S(1)} %get-tuple-element.53.refs_2_.fh, bf16[2,512,512]{2,1,0:T(8,128)(2,1)S(1)} %get-tuple-element.39.refs_3_.fl, bf16[512,512]{1,0:T(8,128)(2,1)S(1)} %get-tuple-element.40.refs_4_.ch, bf16[512,512]{1,0:T(8,128)(2,1)S(1)} %get-tuple-element.41.refs_5_.cl), custom_call_target="tpu_custom_call" | custom-call | tf_op jit(solution)/shard_map/pallas_call | solution.py:64
  15.7 1.3 %collective-permute-start.9 = (f32[2,512,512]{2,1,0:T(8,128)S(1)}, f32[2,512,512]{2,1,0:T(8,128)S(1)}, u32[]{:S(2)}, u32[]{:S(2)}) collective-permute-start(f32[2,512,512]{2,1,0:T(8,128)S(1)} %shard_map.57.refs_0_), channel_id=1, source_target_pairs={{0,1},{1,0},{2,3},{3,2},{4,5},{5,4},{6,7},{7,6},{8,9},{9,8},{10,11... | collective-permute-start | bytes 6291464 | tf_op jit(solution)/shard_map/ppermute | solution.py:352
  17.0 0.7 collective-permute-start.6
  17.6 0.0 collective-permute-done.6.refs_0_.refs_2_
  17.7 0.7 collective-permute-start.7
  18.3 0.0 collective-permute-done.8.refs_1_
  18.4 2.0 %shard_map.56.refs_6_ = bf16[2,2,2,512,512]{4,3,2,1,0:T(8,128)(2,1)S(1)} custom-call(f32[2,512,512]{2,1,0:T(8,128)} %bitcast.10, f32[2,512,512]{2,1,0:T(8,128)S(1)} %collective-permute-done.8.refs_1_), custom_call_target="tpu_custom_call" | custom-call | tf_op jit(solution)/shard_map/pallas_call | solution.py:204
  20.4 0.3 collective-permute-done.9.refs_1_
  20.7 0.7 shard_map.58.refs_8_.refs_3_.refs_5_
  21.4 2.2 %shard_map.59 = (f32[64,512]{1,0:T(8,128)S(1)}, f32[64,512]{1,0:T(8,128)S(1)}, f32[64,512]{1,0:T(8,128)S(1)}, f32[16,128]{1,0:T(8,128)S(1)}) custom-call(f32[64,512]{1,0:T(8,128)S(1)} %collective-permute-done.1.refs_0_, f32[64,512]{1,0:T(8,128)S(1)} %collective-permute-done.2.refs_1_, f32[64,512]{1,0:T(8,128)S(1)} %collective-permute-done.6.refs_0_.refs_2_, ...), custom_call_target="tpu_custom_call" | custom-call | tf_op jit(solution)/shard_map/pallas_call | solution.py:64
  23.6 0.7 collective-permute-start.10
  24.3 0.7 collective-permute-start.11
  25.0 1.3 %collective-permute-start.12 = (f32[64,512]{1,0:T(8,128)S(1)}, f32[64,512]{1,0:T(8,128)S(1)}, u32[]{:S(2)}, u32[]{:S(2)}) collective-permute-start(f32[64,512]{1,0:T(8,128)S(1)} %shard_map.61), channel_id=1, source_target_pairs={{2,0},{3,1},{10,8},{11,9},{18,16},{19,17},{26,24},{27,25}} | collective-permute-start | bytes 393224 | tf_op jit(solution)/shard_map/ppermute | solution.py:355
  26.3 26.0 %collective-permute-done.12.refs_2_ = f32[64,512]{1,0:T(8,128)S(1)} collective-permute-done((f32[64,512]{1,0:T(8,128)S(1)}, f32[64,512]{1,0:T(8,128)S(1)}, u32[]{:S(2)}, u32[]{:S(2)}) %collective-permute-start.12) | collective-permute-done | bytes 131104 | tf_op jit(solution)/shard_map/ppermute | solution.py:355
  52.3 0.9 %shard_map.62 = (f32[128,128]{1,0:T(8,128)S(1)}, f32[128,128]{1,0:T(8,128)S(1)}, f32[128,128]{1,0:T(8,128)S(1)}, f32[128,128]{1,0:T(8,128)S(1)}) custom-call(f32[64,512]{1,0:T(8,128)S(1)} %collective-permute-done.10.refs_0_, f32[64,512]{1,0:T(8,128)S(1)} %collective-permute-done.11.refs_0_.refs_1_, f32[64,512]{1,0:T(8,128)S(1)} %collective-permute-done.12.refs_2_, ...), custom_call_target="tpu_custom_call" | custom-call | tf_op jit(solution)/shard_map/pallas_call | solution.py:64
  53.2 1.6 %collective-permute-start.13 = (f32[128,128]{1,0:T(8,128)S(1)}, f32[128,128]{1,0:T(8,128)S(1)}, u32[]{:S(2)}, u32[]{:S(2)}) collective-permute-start(f32[128,128]{1,0:T(8,128)S(1)} %get-tuple-element.59), channel_id=1, source_target_pairs={{0,8},{8,0},{16,24},{24,16},{1,9},{9,1},{17,25},{25,17},{2,10},{10... | collective-permute-start | bytes 196616 | tf_op jit(solution)/shard_map/ppermute | solution.py:358
  54.8 1.5 %collective-permute-start.14 = (f32[128,128]{1,0:T(8,128)S(1)}, f32[128,128]{1,0:T(8,128)S(1)}, u32[]{:S(2)}, u32[]{:S(2)}) collective-permute-start(f32[128,128]{1,0:T(8,128)S(1)} %get-tuple-element.60), channel_id=1, source_target_pairs={{0,16},{8,24},{16,0},{24,8},{1,17},{9,25},{17,1},{25,9},{2,18},{10... | collective-permute-start | bytes 196616 | tf_op jit(solution)/shard_map/ppermute | solution.py:358
  56.3 0.4 collective-permute-start.15
  56.8 0.8 collective-permute-done.13.refs_1_
  57.6 1.5 %collective-permute-done.14.refs_2_ = f32[128,128]{1,0:T(8,128)S(1)} collective-permute-done((f32[128,128]{1,0:T(8,128)S(1)}, f32[128,128]{1,0:T(8,128)S(1)}, u32[]{:S(2)}, u32[]{:S(2)}) %collective-permute-start.14) | collective-permute-done | bytes 65568 | tf_op jit(solution)/shard_map/ppermute | solution.py:358
  59.1 2.4 %collective-permute-done.15.refs_3_ = f32[128,128]{1,0:T(8,128)S(1)} collective-permute-done((f32[128,128]{1,0:T(8,128)S(1)}, f32[128,128]{1,0:T(8,128)S(1)}, u32[]{:S(2)}, u32[]{:S(2)}) %collective-permute-start.15) | collective-permute-done | bytes 65568 | tf_op jit(solution)/shard_map/ppermute | solution.py:358
  61.5 0.1 shard_map.63.mine
  61.6 0.1 collective-permute-start.16
  61.7 1.3 %collective-permute-done.16.other = f32[256,128]{1,0:T(8,128)S(1)} collective-permute-done((f32[256,128]{1,0:T(8,128)S(1)}, f32[256,128]{1,0:T(8,128)S(1)}, u32[]{:S(2)}, u32[]{:S(2)}) %collective-permute-start.16) | collective-permute-done | bytes 131104 | tf_op jit(solution)/shard_map/ppermute | solution.py:352
  63.0 0.3 shard_map.64
  63.3 0.6 collective-permute-start.17
  63.9 0.5 collective-permute-start.18
  64.4 2.5 %collective-permute-start.19 = (f32[32,256]{1,0:T(8,128)S(1)}, f32[32,256]{1,0:T(8,128)S(1)}, u32[]{:S(2)}, u32[]{:S(2)}) collective-permute-start(f32[32,256]{1,0:T(8,128)S(1)} %get-tuple-element.67), channel_id=1, source_target_pairs={{0,24},{8,16},{16,8},{24,0},{1,25},{9,17},{17,9},{25,1},{2,26},{10... | collective-permute-start | bytes 98312 | tf_op jit(solution)/shard_map/ppermute | solution.py:358
  66.9 0.4 collective-permute-done.17
  67.3 0.9 %collective-permute-done.18 = f32[32,256]{1,0:T(8,128)S(1)} collective-permute-done((f32[32,256]{1,0:T(8,128)S(1)}, f32[32,256]{1,0:T(8,128)S(1)}, u32[]{:S(2)}, u32[]{:S(2)}) %collective-permute-start.18) | collective-permute-done | bytes 32800 | tf_op jit(solution)/shard_map/ppermute | solution.py:358
  68.1 1.0 %collective-permute-done.19 = f32[32,256]{1,0:T(8,128)S(1)} collective-permute-done((f32[32,256]{1,0:T(8,128)S(1)}, f32[32,256]{1,0:T(8,128)S(1)}, u32[]{:S(2)}, u32[]{:S(2)}) %collective-permute-start.19) | collective-permute-done | bytes 32800 | tf_op jit(solution)/shard_map/ppermute | solution.py:358
  69.2 0.1 collective-permute-start.22
  69.3 1.0 %collective-permute-start.21 = (f32[32,256]{1,0:T(8,128)S(1)}, f32[32,256]{1,0:T(8,128)S(1)}, u32[]{:S(2)}, u32[]{:S(2)}) collective-permute-start(f32[32,256]{1,0:T(8,128)S(1)} %add_add_fusion), channel_id=1, source_target_pairs={{0,4},{1,5},{2,6},{3,7},{4,0},{5,1},{6,2},{7,3},{8,12},{9,13},{10,... | collective-permute-start | bytes 98312 | tf_op jit(solution)/shard_map/ppermute | solution.py:361
  70.3 3.3 %collective-permute-start.20 = (f32[32,256]{1,0:T(8,128)S(1)}, f32[32,256]{1,0:T(8,128)S(1)}, u32[]{:S(2)}, u32[]{:S(2)}) collective-permute-start(f32[32,256]{1,0:T(8,128)S(1)} %add_add_fusion), channel_id=1, source_target_pairs={{0,2},{1,3},{2,0},{3,1},{4,6},{5,7},{6,4},{7,5},{8,10},{9,11},{10,... | collective-permute-start | bytes 98312 | tf_op jit(solution)/shard_map/ppermute | solution.py:361
  73.7 1.3 %collective-permute-done.22 = f32[32,256]{1,0:T(8,128)S(1)} collective-permute-done((f32[32,256]{1,0:T(8,128)S(1)}, f32[32,256]{1,0:T(8,128)S(1)}, u32[]{:S(2)}, u32[]{:S(2)}) %collective-permute-start.22) | collective-permute-done | bytes 32800 | tf_op jit(solution)/shard_map/ppermute | solution.py:361
  75.0 0.6 collective-permute-done.20
  75.6 2.5 %collective-permute-start.25 = (f32[32,256]{1,0:T(8,128)S(1)}, f32[32,256]{1,0:T(8,128)S(1)}, u32[]{:S(2)}, u32[]{:S(2)}) collective-permute-start(f32[32,256]{1,0:T(8,128)S(1)} %add_multiply_fusion.refs_0_), channel_id=1, source_target_pairs={{0,24},{8,16},{16,8},{24,0},{1,25},{9,17},{17,9},{25,1},{2,26},{10... | collective-permute-start | bytes 98312 | tf_op jit(solution)/shard_map/ppermute | solution.py:358
  78.1 0.5 collective-permute-start.24
  78.6 0.5 collective-permute-start.23
  79.1 1.3 %collective-permute-done.25.refs_3_ = f32[32,256]{1,0:T(8,128)S(1)} collective-permute-done((f32[32,256]{1,0:T(8,128)S(1)}, f32[32,256]{1,0:T(8,128)S(1)}, u32[]{:S(2)}, u32[]{:S(2)}) %collective-permute-start.25) | collective-permute-done | bytes 32800 | tf_op jit(solution)/shard_map/ppermute | solution.py:358
  80.4 1.6 %collective-permute-done.24.refs_2_ = f32[32,256]{1,0:T(8,128)S(1)} collective-permute-done((f32[32,256]{1,0:T(8,128)S(1)}, f32[32,256]{1,0:T(8,128)S(1)}, u32[]{:S(2)}, u32[]{:S(2)}) %collective-permute-start.24) | collective-permute-done | bytes 32800 | tf_op jit(solution)/shard_map/ppermute | solution.py:358
  82.0 0.5 collective-permute-done.23.refs_1_
  82.5 0.1 collective-permute-start.26
  82.6 0.8 copy.5
  83.4 0.6 collective-permute-done.26.other
  84.0 0.7 join.1
  (13 shorter events, 0.2 us)
Async XLA Ops:
  3.4 1.7 %collective-permute-start = (f32[128,512]{1,0:T(8,128)S(1)}, f32[128,512]{1,0:T(8,128)S(1)}, u32[]{:S(2)}, u32[]{:S(2)}) collective-permute-start(f32[128,512]{1,0:T(8,128)S(1)} %get-tuple-element.36), channel_id=1, source_target_pairs={{0,1},{1,0},{2,3},{3,2},{4,5},{5,4},{6,7},{7,6},{8,9},{9,8},{10,11... | collective-permute-start | bytes 786440 | tf_op jit(solution)/shard_map/ppermute | solution.py:352
  6.2 5.2 %copy-start = (f32[1,1,2,512,512]{4,3,2,1,0:T(8,128)S(1)}, f32[1,1,2,512,512]{4,3,2,1,0:T(8,128)}, u32[]{:S(2)}) copy-start(f32[1,1,2,512,512]{4,3,2,1,0:T(8,128)} %param.3) | copy-start | bytes 6291460
  7.2 2.7 %collective-permute-start.3 = (f32[512,512]{1,0:T(8,128)S(1)}, f32[512,512]{1,0:T(8,128)S(1)}, u32[]{:S(2)}, u32[]{:S(2)}) collective-permute-start(f32[512,512]{1,0:T(8,128)S(1)} %shard_map.51.refs_0_), channel_id=1, source_target_pairs={{0,1},{1,0},{2,3},{3,2},{4,5},{5,4},{6,7},{7,6},{8,9},{9,8},{10,11... | collective-permute-start | bytes 3145736 | tf_op jit(solution)/shard_map/ppermute | solution.py:352
  7.6 3.8 %collective-permute-start.4 = (f32[512,512]{1,0:T(8,128)S(1)}, f32[512,512]{1,0:T(8,128)S(1)}, u32[]{:S(2)}, u32[]{:S(2)}) collective-permute-start(f32[512,512]{1,0:T(8,128)S(1)} %shard_map.52.refs_1_), channel_id=1, source_target_pairs={{0,1},{1,0},{2,3},{3,2},{4,5},{5,4},{6,7},{7,6},{8,9},{9,8},{10,11... | collective-permute-start | bytes 3145736 | tf_op jit(solution)/shard_map/ppermute | solution.py:352
  7.8 5.4 %collective-permute-start.5 = (f32[64,512]{1,0:T(8,128)S(1)}, f32[64,512]{1,0:T(8,128)S(1)}, u32[]{:S(2)}, u32[]{:S(2)}) collective-permute-start(f32[64,512]{1,0:T(8,128)S(1)} %get-tuple-element.47.refs_0_.refs_4_), channel_id=1, source_target_pairs={{0,1},{1,0},{2,3},{3,2},{4,5},{5,4},{6,7},{7,6},{8,9},{9,8},{10,11... | collective-permute-start | bytes 393224 | tf_op jit(solution)/shard_map/ppermute | solution.py:352
  8.1 5.7 %collective-permute-start.2 = (f32[64,512]{1,0:T(8,128)S(1)}, f32[64,512]{1,0:T(8,128)S(1)}, u32[]{:S(2)}, u32[]{:S(2)}) collective-permute-start(f32[64,512]{1,0:T(8,128)S(1)} %get-tuple-element.43), channel_id=1, source_target_pairs={{1,3},{9,11},{17,19},{25,27}} | collective-permute-start | bytes 393224 | tf_op jit(solution)/shard_map/ppermute | solution.py:393
  8.8 5.0 %collective-permute-start.1 = (f32[64,512]{1,0:T(8,128)S(1)}, f32[64,512]{1,0:T(8,128)S(1)}, u32[]{:S(2)}, u32[]{:S(2)}) collective-permute-start(f32[64,512]{1,0:T(8,128)S(1)} %get-tuple-element.42), channel_id=1, source_target_pairs={{1,2},{9,10},{17,18},{25,26}} | collective-permute-start | bytes 393224 | tf_op jit(solution)/shard_map/ppermute | solution.py:392
  11.4 6.9 %collective-permute-start.8 = (f32[2,512,512]{2,1,0:T(8,128)S(1)}, f32[2,512,512]{2,1,0:T(8,128)S(1)}, u32[]{:S(2)}, u32[]{:S(2)}) collective-permute-start(f32[2,512,512]{2,1,0:T(8,128)S(1)} %bitcast.11), channel_id=1, source_target_pairs={{0,1},{1,0},{2,3},{3,2},{4,5},{5,4},{6,7},{7,6},{8,9},{9,8},{10,11... | collective-permute-start | bytes 6291464 | tf_op jit(solution)/shard_map/ppermute | solution.py:352
  15.7 5.1 %collective-permute-start.9 = (f32[2,512,512]{2,1,0:T(8,128)S(1)}, f32[2,512,512]{2,1,0:T(8,128)S(1)}, u32[]{:S(2)}, u32[]{:S(2)}) collective-permute-start(f32[2,512,512]{2,1,0:T(8,128)S(1)} %shard_map.57.refs_0_), channel_id=1, source_target_pairs={{0,1},{1,0},{2,3},{3,2},{4,5},{5,4},{6,7},{7,6},{8,9},{9,8},{10,11... | collective-permute-start | bytes 6291464 | tf_op jit(solution)/shard_map/ppermute | solution.py:352
  17.0 0.7 collective-permute-start.6
  17.7 3.8 %collective-permute-start.7 = (f32[64,512]{1,0:T(8,128)S(1)}, f32[64,512]{1,0:T(8,128)S(1)}, u32[]{:S(2)}, u32[]{:S(2)}) collective-permute-start(f32[64,512]{1,0:T(8,128)S(1)} %shard_map.55), channel_id=1, source_target_pairs={{4,6},{5,7},{12,14},{13,15},{20,22},{21,23},{28,30},{29,31}} | collective-permute-start | bytes 393224 | tf_op jit(solution)/shard_map/ppermute | solution.py:355
  23.6 0.7 collective-permute-start.10
  24.3 0.7 collective-permute-start.11
  25.0 27.3 %collective-permute-start.12 = (f32[64,512]{1,0:T(8,128)S(1)}, f32[64,512]{1,0:T(8,128)S(1)}, u32[]{:S(2)}, u32[]{:S(2)}) collective-permute-start(f32[64,512]{1,0:T(8,128)S(1)} %shard_map.61), channel_id=1, source_target_pairs={{2,0},{3,1},{10,8},{11,9},{18,16},{19,17},{26,24},{27,25}} | collective-permute-start | bytes 393224 | tf_op jit(solution)/shard_map/ppermute | solution.py:355
  53.2 4.3 %collective-permute-start.13 = (f32[128,128]{1,0:T(8,128)S(1)}, f32[128,128]{1,0:T(8,128)S(1)}, u32[]{:S(2)}, u32[]{:S(2)}) collective-permute-start(f32[128,128]{1,0:T(8,128)S(1)} %get-tuple-element.59), channel_id=1, source_target_pairs={{0,8},{8,0},{16,24},{24,16},{1,9},{9,1},{17,25},{25,17},{2,10},{10... | collective-permute-start | bytes 196616 | tf_op jit(solution)/shard_map/ppermute | solution.py:358
  54.8 4.3 %collective-permute-start.14 = (f32[128,128]{1,0:T(8,128)S(1)}, f32[128,128]{1,0:T(8,128)S(1)}, u32[]{:S(2)}, u32[]{:S(2)}) collective-permute-start(f32[128,128]{1,0:T(8,128)S(1)} %get-tuple-element.60), channel_id=1, source_target_pairs={{0,16},{8,24},{16,0},{24,8},{1,17},{9,25},{17,1},{25,9},{2,18},{10... | collective-permute-start | bytes 196616 | tf_op jit(solution)/shard_map/ppermute | solution.py:358
  56.3 5.2 %collective-permute-start.15 = (f32[128,128]{1,0:T(8,128)S(1)}, f32[128,128]{1,0:T(8,128)S(1)}, u32[]{:S(2)}, u32[]{:S(2)}) collective-permute-start(f32[128,128]{1,0:T(8,128)S(1)} %get-tuple-element.61), channel_id=1, source_target_pairs={{0,24},{8,16},{16,8},{24,0},{1,25},{9,17},{17,9},{25,1},{2,26},{10... | collective-permute-start | bytes 196616 | tf_op jit(solution)/shard_map/ppermute | solution.py:358
  61.6 1.4 %collective-permute-start.16 = (f32[256,128]{1,0:T(8,128)S(1)}, f32[256,128]{1,0:T(8,128)S(1)}, u32[]{:S(2)}, u32[]{:S(2)}) collective-permute-start(f32[256,128]{1,0:T(8,128)S(1)} %shard_map.63.mine), channel_id=1, source_target_pairs={{0,1},{1,0},{2,3},{3,2},{4,5},{5,4},{6,7},{7,6},{8,9},{9,8},{10,11... | collective-permute-start | bytes 393224 | tf_op jit(solution)/shard_map/ppermute | solution.py:352
  63.3 4.0 %collective-permute-start.17 = (f32[32,256]{1,0:T(8,128)S(1)}, f32[32,256]{1,0:T(8,128)S(1)}, u32[]{:S(2)}, u32[]{:S(2)}) collective-permute-start(f32[32,256]{1,0:T(8,128)S(1)} %get-tuple-element.65), channel_id=1, source_target_pairs={{0,8},{8,0},{16,24},{24,16},{1,9},{9,1},{17,25},{25,17},{2,10},{10... | collective-permute-start | bytes 98312 | tf_op jit(solution)/shard_map/ppermute | solution.py:358
  63.9 4.3 %collective-permute-start.18 = (f32[32,256]{1,0:T(8,128)S(1)}, f32[32,256]{1,0:T(8,128)S(1)}, u32[]{:S(2)}, u32[]{:S(2)}) collective-permute-start(f32[32,256]{1,0:T(8,128)S(1)} %get-tuple-element.66), channel_id=1, source_target_pairs={{0,16},{8,24},{16,0},{24,8},{1,17},{9,25},{17,1},{25,9},{2,18},{10... | collective-permute-start | bytes 98312 | tf_op jit(solution)/shard_map/ppermute | solution.py:358
  64.4 4.8 %collective-permute-start.19 = (f32[32,256]{1,0:T(8,128)S(1)}, f32[32,256]{1,0:T(8,128)S(1)}, u32[]{:S(2)}, u32[]{:S(2)}) collective-permute-start(f32[32,256]{1,0:T(8,128)S(1)} %get-tuple-element.67), channel_id=1, source_target_pairs={{0,24},{8,16},{16,8},{24,0},{1,25},{9,17},{17,9},{25,1},{2,26},{10... | collective-permute-start | bytes 98312 | tf_op jit(solution)/shard_map/ppermute | solution.py:358
  69.2 5.8 %collective-permute-start.22 = (f32[32,256]{1,0:T(8,128)S(1)}, f32[32,256]{1,0:T(8,128)S(1)}, u32[]{:S(2)}, u32[]{:S(2)}) collective-permute-start(f32[32,256]{1,0:T(8,128)S(1)} %add_add_fusion), channel_id=1, source_target_pairs={{0,6},{1,7},{2,4},{3,5},{4,2},{5,3},{6,0},{7,1},{8,14},{9,15},{10,... | collective-permute-start | bytes 98312 | tf_op jit(solution)/shard_map/ppermute | solution.py:361
  69.3 5.7 %collective-permute-start.21 = (f32[32,256]{1,0:T(8,128)S(1)}, f32[32,256]{1,0:T(8,128)S(1)}, u32[]{:S(2)}, u32[]{:S(2)}) collective-permute-start(f32[32,256]{1,0:T(8,128)S(1)} %add_add_fusion), channel_id=1, source_target_pairs={{0,4},{1,5},{2,6},{3,7},{4,0},{5,1},{6,2},{7,3},{8,12},{9,13},{10,... | collective-permute-start | bytes 98312 | tf_op jit(solution)/shard_map/ppermute | solution.py:361
  70.3 5.2 %collective-permute-start.20 = (f32[32,256]{1,0:T(8,128)S(1)}, f32[32,256]{1,0:T(8,128)S(1)}, u32[]{:S(2)}, u32[]{:S(2)}) collective-permute-start(f32[32,256]{1,0:T(8,128)S(1)} %add_add_fusion), channel_id=1, source_target_pairs={{0,2},{1,3},{2,0},{3,1},{4,6},{5,7},{6,4},{7,5},{8,10},{9,11},{10,... | collective-permute-start | bytes 98312 | tf_op jit(solution)/shard_map/ppermute | solution.py:361
  75.6 4.9 %collective-permute-start.25 = (f32[32,256]{1,0:T(8,128)S(1)}, f32[32,256]{1,0:T(8,128)S(1)}, u32[]{:S(2)}, u32[]{:S(2)}) collective-permute-start(f32[32,256]{1,0:T(8,128)S(1)} %add_multiply_fusion.refs_0_), channel_id=1, source_target_pairs={{0,24},{8,16},{16,8},{24,0},{1,25},{9,17},{17,9},{25,1},{2,26},{10... | collective-permute-start | bytes 98312 | tf_op jit(solution)/shard_map/ppermute | solution.py:358
  78.1 3.9 %collective-permute-start.24 = (f32[32,256]{1,0:T(8,128)S(1)}, f32[32,256]{1,0:T(8,128)S(1)}, u32[]{:S(2)}, u32[]{:S(2)}) collective-permute-start(f32[32,256]{1,0:T(8,128)S(1)} %add_multiply_fusion.refs_0_), channel_id=1, source_target_pairs={{0,16},{8,24},{16,0},{24,8},{1,17},{9,25},{17,1},{25,9},{2,18},{10... | collective-permute-start | bytes 98312 | tf_op jit(solution)/shard_map/ppermute | solution.py:358
  78.6 3.9 %collective-permute-start.23 = (f32[32,256]{1,0:T(8,128)S(1)}, f32[32,256]{1,0:T(8,128)S(1)}, u32[]{:S(2)}, u32[]{:S(2)}) collective-permute-start(f32[32,256]{1,0:T(8,128)S(1)} %add_multiply_fusion.refs_0_), channel_id=1, source_target_pairs={{0,8},{8,0},{16,24},{24,16},{1,9},{9,1},{17,25},{25,17},{2,10},{10... | collective-permute-start | bytes 98312 | tf_op jit(solution)/shard_map/ppermute | solution.py:358
  82.5 1.4 %collective-permute-start.26 = (f32[128,256]{1,0:T(8,128)S(1)}, f32[128,256]{1,0:T(8,128)S(1)}, u32[]{:S(2)}, u32[]{:S(2)}) collective-permute-start(f32[128,256]{1,0:T(8,128)S(1)} %shard_map.65.mine), channel_id=1, source_target_pairs={{0,1},{1,0},{2,3},{3,2},{4,5},{5,4},{6,7},{7,6},{8,9},{9,8},{10,11... | collective-permute-start | bytes 393224 | tf_op jit(solution)/shard_map/ppermute | solution.py:352

commit v6 on v5

--- a/solution.py
+++ b/solution.py
@@ -237,12 +237,16 @@
     angle = (kind // 2 + 1).astype(F32) * theta
     weights[...] = jnp.where(kind % 2 == 0, jnp.cos(angle), jnp.sin(angle)) / nodes
     y = add_real(total(cs), va[...])
-    y_b = add_real(apply_to(y, block_of(a_mats, 0), NN), vb[...])
-    u_b = apply_to(y_b, block_of(f_mats, 1), NT)
+    a_y = apply_to(y, block_of(a_mats, 0), NN)
     u_a = apply_to(y, block_of(f_mats, 0), NT)
+    u_b = apply_to(add_real(a_y, vb[...]), block_of(f_mats, 1), NT)
     ub[...] = u_b
     ua[...] = u_a
-    s[...] = u_a + apply_to(u_b, block_of(b_mats, 0), NN)
+
+    def send():
+        s[...] = u_a + apply_to(ub[...], block_of(b_mats, 0), NN)
+
+    only_on(lax.axis_size("row") // 2 - 1, [s], send)
 
 
 def backward_kernel(layer, *refs):

time: 84.9 us -> 84.9 us (level)
  no operation moved by 1% of the time
where the time goes in v6:
time: 84.9 us; the launch traced here: 84.6 us
  waiting for transfers between devices  43 us (51%)
  starting transfers between devices  25.1 us (30%)
  Pallas kernels  14.9 us (18%)
  between operations  0.9 us (1%)
    ppermute x5, waiting for transfers between devices, hop(): lax.ppermute(value, 'row', [(2 * source + c, 2 * target + c) for c in ran...  26.3 us
    ppermute x9, starting transfers between devices, exchange_node(): return lax.ppermute(value, 'node', [(j, j ^ d) for j in range(nodes)])  10.7 us
    ppermute x9, waiting for transfers between devices, exchange_node(): return lax.ppermute(value, 'node', [(j, j ^ d) for j in range(nodes)])  10.5 us
    pallas_call x15, Pallas kernels, call(): pl.pallas_call(kernel, out_shape=tuple((pltpu.VMEM(shape, dtype) for shap...  9.39 us
    ppermute x8, starting transfers between devices, swap_core(): return lax.ppermute(value, 'row', [(r, r ^ 1) for r in range(rows)])  4.7 us
    ppermute x3, starting transfers between devices, exchange_layer(): return lax.ppermute(value, 'row', [(r, r ^ 2 * d) for r in range(rows)])  4.45 us
    ppermute x8, waiting for transfers between devices, swap_core(): return lax.ppermute(value, 'row', [(r, r ^ 1) for r in range(rows)])  4.35 us
    ppermute x5, starting transfers between devices, hop(): lax.ppermute(value, 'row', [(2 * source + c, 2 * target + c) for c in ran...  3.96 us
  transfers between devices with their start and end apart: 27, of which 18 were waited for; matrix products, arithmetic and copies ran while one was open for 1% of the time, Pallas kernels for 7%

profile of v6, /device:TPU:0, one launch (start us, length us, event | category | flops | bytes accessed | tf_op | source)
XLA Modules:
  0.0 84.6 jit_solution(8382869709907731532)
XLA Ops:
  0.6 2.7 %enter.1 = (bf16[2,512,512]{2,1,0:T(8,128)(2,1)S(1)}, bf16[2,512,512]{2,1,0:T(8,128)(2,1)S(1)}, bf16[512,512]{1,0:T(8,128)(2,1)S(1)}, bf16[512,512]{1,0:T(8,128)...) custom-call(f32[2,512,512]{2,1,0:T(8,128)} %bitcast.9, f32[512,512]{1,0:T(8,128)} %bitcast.12, f32[64,512]{1,0:T(8,128)} %bitcast.13), custom_call_target="tpu_custom_call" | custom-call | tf_op jit(solution)/shard_map/enter/pallas_call | solution.py:371
  3.4 0.6 collective-permute-start
  3.9 1.0 %shard_map.51.refs_0_ = f32[512,512]{1,0:T(8,128)S(1)} custom-call(bf16[2,512,512]{2,1,0:T(8,128)(2,1)S(1)} %get-tuple-element.53.refs_2_.fh, bf16[2,512,512]{2,1,0:T(8,128)(2,1)S(1)} %get-tuple-element.39.refs_3_.fl, bf16[512,512]{1,0:T(8,128)(2,1)S(1)} %get-tuple-element.40.refs_4_.ch, bf16[512,512]{1,0:T(8,128)(2,1)S(1)} %get-tuple-element.41.refs_5_.cl), custom_call_target="tpu_custom_call" | custom-call | tf_op jit(solution)/shard_map/pallas_call | solution.py:64
  4.9 0.2 collective-permute-done.refs_1_
  5.1 1.1 %shard_map.50 = (f32[64,512]{1,0:T(8,128)S(1)}, f32[64,512]{1,0:T(8,128)S(1)}) custom-call(f32[64,512]{1,0:T(8,128)S(1)} %get-tuple-element.47.refs_0_.refs_4_, f32[128,512]{1,0:T(8,128)S(1)} %collective-permute-done.refs_1_, bf16[2,512,512]{2,1,0:T(8,128)(2,1)S(1)} %get-tuple-element.53.refs_2_.fh, bf16[2,512,512]{2,1,0:T(8,128)(2,1)S(1)} %get-tuple-element.39.refs_3_.fl, ...), custom_call_target="tpu_custom_call" | custom-call | tf_op jit(solution)/shard_map/pallas_call | solution.py:64
  6.2 0.0 copy-start
  6.2 1.0 %shard_map.52.refs_1_ = f32[512,512]{1,0:T(8,128)S(1)} custom-call(bf16[2,512,512]{2,1,0:T(8,128)(2,1)S(1)} %get-tuple-element.53.refs_2_.fh, bf16[2,512,512]{2,1,0:T(8,128)(2,1)S(1)} %get-tuple-element.39.refs_3_.fl, bf16[512,512]{1,0:T(8,128)(2,1)S(1)} %get-tuple-element.40.refs_4_.ch, bf16[512,512]{1,0:T(8,128)(2,1)S(1)} %get-tuple-element.41.refs_5_.cl), custom_call_target="tpu_custom_call" | custom-call | tf_op jit(solution)/shard_map/pallas_call | solution.py:64
  7.2 0.4 collective-permute-start.3
  7.6 0.1 collective-permute-start.4
  7.8 0.4 collective-permute-start.5
  8.1 0.7 collective-permute-start.2
  8.8 0.7 collective-permute-start.1
  9.5 0.4 collective-permute-done.3.refs_2_
  9.9 1.5 %collective-permute-done.4.refs_3_ = f32[512,512]{1,0:T(8,128)S(1)} collective-permute-done((f32[512,512]{1,0:T(8,128)S(1)}, f32[512,512]{1,0:T(8,128)S(1)}, u32[]{:S(2)}, u32[]{:S(2)}) %collective-permute-start.4) | collective-permute-done | bytes 1048608 | tf_op jit(solution)/shard_map/ppermute | solution.py:356
  11.4 1.8 %collective-permute-start.8 = (f32[2,512,512]{2,1,0:T(8,128)S(1)}, f32[2,512,512]{2,1,0:T(8,128)S(1)}, u32[]{:S(2)}, u32[]{:S(2)}) collective-permute-start(f32[2,512,512]{2,1,0:T(8,128)S(1)} %bitcast.11), channel_id=1, source_target_pairs={{0,1},{1,0},{2,3},{3,2},{4,5},{5,4},{6,7},{7,6},{8,9},{9,8},{10,11... | collective-permute-start | bytes 6291464 | tf_op jit(solution)/shard_map/ppermute | solution.py:356
  13.2 0.0 collective-permute-done.5.refs_5_
  13.2 0.6 shard_map.53
  13.8 0.0 collective-permute-done.1.refs_0_
  13.8 1.8 %shard_map.57.refs_0_ = f32[2,512,512]{2,1,0:T(8,128)S(1)} custom-call(bf16[2,512,512]{2,1,0:T(8,128)(2,1)S(1)} %get-tuple-element.53.refs_2_.fh, bf16[2,512,512]{2,1,0:T(8,128)(2,1)S(1)} %get-tuple-element.39.refs_3_.fl, bf16[512,512]{1,0:T(8,128)(2,1)S(1)} %get-tuple-element.40.refs_4_.ch, bf16[512,512]{1,0:T(8,128)(2,1)S(1)} %get-tuple-element.41.refs_5_.cl), custom_call_target="tpu_custom_call" | custom-call | tf_op jit(solution)/shard_map/pallas_call | solution.py:64
  15.7 1.3 %collective-permute-start.9 = (f32[2,512,512]{2,1,0:T(8,128)S(1)}, f32[2,512,512]{2,1,0:T(8,128)S(1)}, u32[]{:S(2)}, u32[]{:S(2)}) collective-permute-start(f32[2,512,512]{2,1,0:T(8,128)S(1)} %shard_map.57.refs_0_), channel_id=1, source_target_pairs={{0,1},{1,0},{2,3},{3,2},{4,5},{5,4},{6,7},{7,6},{8,9},{9,8},{10,11... | collective-permute-start | bytes 6291464 | tf_op jit(solution)/shard_map/ppermute | solution.py:356
  17.0 0.7 collective-permute-start.6
  17.6 0.0 collective-permute-done.6.refs_0_.refs_2_
  17.7 0.7 collective-permute-start.7
  18.3 0.0 collective-permute-done.8.refs_1_
  18.4 2.0 %shard_map.56.refs_6_ = bf16[2,2,2,512,512]{4,3,2,1,0:T(8,128)(2,1)S(1)} custom-call(f32[2,512,512]{2,1,0:T(8,128)} %bitcast.10, f32[2,512,512]{2,1,0:T(8,128)S(1)} %collective-permute-done.8.refs_1_), custom_call_target="tpu_custom_call" | custom-call | tf_op jit(solution)/shard_map/pallas_call | solution.py:204
  20.4 0.3 collective-permute-done.9.refs_1_
  20.7 0.7 shard_map.58.refs_8_.refs_3_.refs_5_
  21.4 1.8 %shard_map.59 = (f32[64,512]{1,0:T(8,128)S(1)}, f32[64,512]{1,0:T(8,128)S(1)}, f32[64,512]{1,0:T(8,128)S(1)}, f32[16,128]{1,0:T(8,128)S(1)}) custom-call(f32[64,512]{1,0:T(8,128)S(1)} %collective-permute-done.1.refs_0_, f32[64,512]{1,0:T(8,128)S(1)} %collective-permute-done.2.refs_1_, f32[64,512]{1,0:T(8,128)S(1)} %collective-permute-done.6.refs_0_.refs_2_, ...), custom_call_target="tpu_custom_call" | custom-call | tf_op jit(solution)/shard_map/pallas_call | solution.py:64
  23.2 0.7 collective-permute-start.10
  24.0 0.7 collective-permute-start.11
  24.7 1.3 %collective-permute-start.12 = (f32[64,512]{1,0:T(8,128)S(1)}, f32[64,512]{1,0:T(8,128)S(1)}, u32[]{:S(2)}, u32[]{:S(2)}) collective-permute-start(f32[64,512]{1,0:T(8,128)S(1)} %shard_map.61), channel_id=1, source_target_pairs={{2,0},{3,1},{10,8},{11,9},{18,16},{19,17},{26,24},{27,25}} | collective-permute-start | bytes 393224 | tf_op jit(solution)/shard_map/ppermute | solution.py:359
  26.0 26.3 %collective-permute-done.12.refs_2_ = f32[64,512]{1,0:T(8,128)S(1)} collective-permute-done((f32[64,512]{1,0:T(8,128)S(1)}, f32[64,512]{1,0:T(8,128)S(1)}, u32[]{:S(2)}, u32[]{:S(2)}) %collective-permute-start.12) | collective-permute-done | bytes 131104 | tf_op jit(solution)/shard_map/ppermute | solution.py:359
  52.3 0.9 %shard_map.62 = (f32[128,128]{1,0:T(8,128)S(1)}, f32[128,128]{1,0:T(8,128)S(1)}, f32[128,128]{1,0:T(8,128)S(1)}, f32[128,128]{1,0:T(8,128)S(1)}) custom-call(f32[64,512]{1,0:T(8,128)S(1)} %collective-permute-done.10.refs_0_, f32[64,512]{1,0:T(8,128)S(1)} %collective-permute-done.11.refs_0_.refs_1_, f32[64,512]{1,0:T(8,128)S(1)} %collective-permute-done.12.refs_2_, ...), custom_call_target="tpu_custom_call" | custom-call | tf_op jit(solution)/shard_map/pallas_call | solution.py:64
  53.2 1.6 %collective-permute-start.13 = (f32[128,128]{1,0:T(8,128)S(1)}, f32[128,128]{1,0:T(8,128)S(1)}, u32[]{:S(2)}, u32[]{:S(2)}) collective-permute-start(f32[128,128]{1,0:T(8,128)S(1)} %get-tuple-element.59), channel_id=1, source_target_pairs={{0,8},{8,0},{16,24},{24,16},{1,9},{9,1},{17,25},{25,17},{2,10},{10... | collective-permute-start | bytes 196616 | tf_op jit(solution)/shard_map/ppermute | solution.py:362
  54.8 1.5 %collective-permute-start.14 = (f32[128,128]{1,0:T(8,128)S(1)}, f32[128,128]{1,0:T(8,128)S(1)}, u32[]{:S(2)}, u32[]{:S(2)}) collective-permute-start(f32[128,128]{1,0:T(8,128)S(1)} %get-tuple-element.60), channel_id=1, source_target_pairs={{0,16},{8,24},{16,0},{24,8},{1,17},{9,25},{17,1},{25,9},{2,18},{10... | collective-permute-start | bytes 196616 | tf_op jit(solution)/shard_map/ppermute | solution.py:362
  56.3 0.4 collective-permute-start.15
  56.8 0.8 collective-permute-done.13.refs_1_
  57.5 1.5 %collective-permute-done.14.refs_2_ = f32[128,128]{1,0:T(8,128)S(1)} collective-permute-done((f32[128,128]{1,0:T(8,128)S(1)}, f32[128,128]{1,0:T(8,128)S(1)}, u32[]{:S(2)}, u32[]{:S(2)}) %collective-permute-start.14) | collective-permute-done | bytes 65568 | tf_op jit(solution)/shard_map/ppermute | solution.py:362
  59.1 2.4 %collective-permute-done.15.refs_3_ = f32[128,128]{1,0:T(8,128)S(1)} collective-permute-done((f32[128,128]{1,0:T(8,128)S(1)}, f32[128,128]{1,0:T(8,128)S(1)}, u32[]{:S(2)}, u32[]{:S(2)}) %collective-permute-start.15) | collective-permute-done | bytes 65568 | tf_op jit(solution)/shard_map/ppermute | solution.py:362
  61.5 0.1 shard_map.63.mine
  61.5 0.1 collective-permute-start.16
  61.6 1.3 %collective-permute-done.16.other = f32[256,128]{1,0:T(8,128)S(1)} collective-permute-done((f32[256,128]{1,0:T(8,128)S(1)}, f32[256,128]{1,0:T(8,128)S(1)}, u32[]{:S(2)}, u32[]{:S(2)}) %collective-permute-start.16) | collective-permute-done | bytes 131104 | tf_op jit(solution)/shard_map/ppermute | solution.py:356
  63.0 0.3 shard_map.64
  63.3 0.6 collective-permute-start.17
  63.8 0.5 collective-permute-start.18
  64.3 2.5 %collective-permute-start.19 = (f32[32,256]{1,0:T(8,128)S(1)}, f32[32,256]{1,0:T(8,128)S(1)}, u32[]{:S(2)}, u32[]{:S(2)}) collective-permute-start(f32[32,256]{1,0:T(8,128)S(1)} %get-tuple-element.67), channel_id=1, source_target_pairs={{0,24},{8,16},{16,8},{24,0},{1,25},{9,17},{17,9},{25,1},{2,26},{10... | collective-permute-start | bytes 98312 | tf_op jit(solution)/shard_map/ppermute | solution.py:362
  66.8 0.4 collective-permute-done.17
  67.2 0.9 %collective-permute-done.18 = f32[32,256]{1,0:T(8,128)S(1)} collective-permute-done((f32[32,256]{1,0:T(8,128)S(1)}, f32[32,256]{1,0:T(8,128)S(1)}, u32[]{:S(2)}, u32[]{:S(2)}) %collective-permute-start.18) | collective-permute-done | bytes 32800 | tf_op jit(solution)/shard_map/ppermute | solution.py:362
  68.1 1.0 %collective-permute-done.19 = f32[32,256]{1,0:T(8,128)S(1)} collective-permute-done((f32[32,256]{1,0:T(8,128)S(1)}, f32[32,256]{1,0:T(8,128)S(1)}, u32[]{:S(2)}, u32[]{:S(2)}) %collective-permute-start.19) | collective-permute-done | bytes 32800 | tf_op jit(solution)/shard_map/ppermute | solution.py:362
  69.2 0.1 collective-permute-start.22
  69.2 1.0 %collective-permute-start.21 = (f32[32,256]{1,0:T(8,128)S(1)}, f32[32,256]{1,0:T(8,128)S(1)}, u32[]{:S(2)}, u32[]{:S(2)}) collective-permute-start(f32[32,256]{1,0:T(8,128)S(1)} %add_add_fusion), channel_id=1, source_target_pairs={{0,4},{1,5},{2,6},{3,7},{4,0},{5,1},{6,2},{7,3},{8,12},{9,13},{10,... | collective-permute-start | bytes 98312 | tf_op jit(solution)/shard_map/ppermute | solution.py:365
  70.3 3.3 %collective-permute-start.20 = (f32[32,256]{1,0:T(8,128)S(1)}, f32[32,256]{1,0:T(8,128)S(1)}, u32[]{:S(2)}, u32[]{:S(2)}) collective-permute-start(f32[32,256]{1,0:T(8,128)S(1)} %add_add_fusion), channel_id=1, source_target_pairs={{0,2},{1,3},{2,0},{3,1},{4,6},{5,7},{6,4},{7,5},{8,10},{9,11},{10,... | collective-permute-start | bytes 98312 | tf_op jit(solution)/shard_map/ppermute | solution.py:365
  73.6 1.3 %collective-permute-done.22 = f32[32,256]{1,0:T(8,128)S(1)} collective-permute-done((f32[32,256]{1,0:T(8,128)S(1)}, f32[32,256]{1,0:T(8,128)S(1)}, u32[]{:S(2)}, u32[]{:S(2)}) %collective-permute-start.22) | collective-permute-done | bytes 32800 | tf_op jit(solution)/shard_map/ppermute | solution.py:365
  74.9 0.6 collective-permute-done.20
  75.5 2.5 %collective-permute-start.25 = (f32[32,256]{1,0:T(8,128)S(1)}, f32[32,256]{1,0:T(8,128)S(1)}, u32[]{:S(2)}, u32[]{:S(2)}) collective-permute-start(f32[32,256]{1,0:T(8,128)S(1)} %add_multiply_fusion.refs_0_), channel_id=1, source_target_pairs={{0,24},{8,16},{16,8},{24,0},{1,25},{9,17},{17,9},{25,1},{2,26},{10... | collective-permute-start | bytes 98312 | tf_op jit(solution)/shard_map/ppermute | solution.py:362
  78.1 0.5 collective-permute-start.24
  78.6 0.5 collective-permute-start.23
  79.1 1.3 %collective-permute-done.25.refs_3_ = f32[32,256]{1,0:T(8,128)S(1)} collective-permute-done((f32[32,256]{1,0:T(8,128)S(1)}, f32[32,256]{1,0:T(8,128)S(1)}, u32[]{:S(2)}, u32[]{:S(2)}) %collective-permute-start.25) | collective-permute-done | bytes 32800 | tf_op jit(solution)/shard_map/ppermute | solution.py:362
  80.4 1.6 %collective-permute-done.24.refs_2_ = f32[32,256]{1,0:T(8,128)S(1)} collective-permute-done((f32[32,256]{1,0:T(8,128)S(1)}, f32[32,256]{1,0:T(8,128)S(1)}, u32[]{:S(2)}, u32[]{:S(2)}) %collective-permute-start.24) | collective-permute-done | bytes 32800 | tf_op jit(solution)/shard_map/ppermute | solution.py:362
  82.0 0.5 collective-permute-done.23.refs_1_
  82.5 0.1 collective-permute-start.26
  82.6 0.8 copy.5
  83.3 0.6 collective-permute-done.26.other
  83.9 0.7 join.1
  (13 shorter events, 0.2 us)
Async XLA Ops:
  3.4 1.7 %collective-permute-start = (f32[128,512]{1,0:T(8,128)S(1)}, f32[128,512]{1,0:T(8,128)S(1)}, u32[]{:S(2)}, u32[]{:S(2)}) collective-permute-start(f32[128,512]{1,0:T(8,128)S(1)} %get-tuple-element.36), channel_id=1, source_target_pairs={{0,1},{1,0},{2,3},{3,2},{4,5},{5,4},{6,7},{7,6},{8,9},{9,8},{10,11... | collective-permute-start | bytes 786440 | tf_op jit(solution)/shard_map/ppermute | solution.py:356
  6.2 5.2 %copy-start = (f32[1,1,2,512,512]{4,3,2,1,0:T(8,128)S(1)}, f32[1,1,2,512,512]{4,3,2,1,0:T(8,128)}, u32[]{:S(2)}) copy-start(f32[1,1,2,512,512]{4,3,2,1,0:T(8,128)} %param.3) | copy-start | bytes 6291460
  7.2 2.7 %collective-permute-start.3 = (f32[512,512]{1,0:T(8,128)S(1)}, f32[512,512]{1,0:T(8,128)S(1)}, u32[]{:S(2)}, u32[]{:S(2)}) collective-permute-start(f32[512,512]{1,0:T(8,128)S(1)} %shard_map.51.refs_0_), channel_id=1, source_target_pairs={{0,1},{1,0},{2,3},{3,2},{4,5},{5,4},{6,7},{7,6},{8,9},{9,8},{10,11... | collective-permute-start | bytes 3145736 | tf_op jit(solution)/shard_map/ppermute | solution.py:356
  7.6 3.8 %collective-permute-start.4 = (f32[512,512]{1,0:T(8,128)S(1)}, f32[512,512]{1,0:T(8,128)S(1)}, u32[]{:S(2)}, u32[]{:S(2)}) collective-permute-start(f32[512,512]{1,0:T(8,128)S(1)} %shard_map.52.refs_1_), channel_id=1, source_target_pairs={{0,1},{1,0},{2,3},{3,2},{4,5},{5,4},{6,7},{7,6},{8,9},{9,8},{10,11... | collective-permute-start | bytes 3145736 | tf_op jit(solution)/shard_map/ppermute | solution.py:356
  7.8 5.4 %collective-permute-start.5 = (f32[64,512]{1,0:T(8,128)S(1)}, f32[64,512]{1,0:T(8,128)S(1)}, u32[]{:S(2)}, u32[]{:S(2)}) collective-permute-start(f32[64,512]{1,0:T(8,128)S(1)} %get-tuple-element.47.refs_0_.refs_4_), channel_id=1, source_target_pairs={{0,1},{1,0},{2,3},{3,2},{4,5},{5,4},{6,7},{7,6},{8,9},{9,8},{10,11... | collective-permute-start | bytes 393224 | tf_op jit(solution)/shard_map/ppermute | solution.py:356
  8.1 5.7 %collective-permute-start.2 = (f32[64,512]{1,0:T(8,128)S(1)}, f32[64,512]{1,0:T(8,128)S(1)}, u32[]{:S(2)}, u32[]{:S(2)}) collective-permute-start(f32[64,512]{1,0:T(8,128)S(1)} %get-tuple-element.43), channel_id=1, source_target_pairs={{1,3},{9,11},{17,19},{25,27}} | collective-permute-start | bytes 393224 | tf_op jit(solution)/shard_map/ppermute | solution.py:397
  8.8 5.0 %collective-permute-start.1 = (f32[64,512]{1,0:T(8,128)S(1)}, f32[64,512]{1,0:T(8,128)S(1)}, u32[]{:S(2)}, u32[]{:S(2)}) collective-permute-start(f32[64,512]{1,0:T(8,128)S(1)} %get-tuple-element.42), channel_id=1, source_target_pairs={{1,2},{9,10},{17,18},{25,26}} | collective-permute-start | bytes 393224 | tf_op jit(solution)/shard_map/ppermute | solution.py:396
  11.4 6.9 %collective-permute-start.8 = (f32[2,512,512]{2,1,0:T(8,128)S(1)}, f32[2,512,512]{2,1,0:T(8,128)S(1)}, u32[]{:S(2)}, u32[]{:S(2)}) collective-permute-start(f32[2,512,512]{2,1,0:T(8,128)S(1)} %bitcast.11), channel_id=1, source_target_pairs={{0,1},{1,0},{2,3},{3,2},{4,5},{5,4},{6,7},{7,6},{8,9},{9,8},{10,11... | collective-permute-start | bytes 6291464 | tf_op jit(solution)/shard_map/ppermute | solution.py:356
  15.7 5.1 %collective-permute-start.9 = (f32[2,512,512]{2,1,0:T(8,128)S(1)}, f32[2,512,512]{2,1,0:T(8,128)S(1)}, u32[]{:S(2)}, u32[]{:S(2)}) collective-permute-start(f32[2,512,512]{2,1,0:T(8,128)S(1)} %shard_map.57.refs_0_), channel_id=1, source_target_pairs={{0,1},{1,0},{2,3},{3,2},{4,5},{5,4},{6,7},{7,6},{8,9},{9,8},{10,11... | collective-permute-start | bytes 6291464 | tf_op jit(solution)/shard_map/ppermute | solution.py:356
  17.0 0.7 collective-permute-start.6
  17.7 3.8 %collective-permute-start.7 = (f32[64,512]{1,0:T(8,128)S(1)}, f32[64,512]{1,0:T(8,128)S(1)}, u32[]{:S(2)}, u32[]{:S(2)}) collective-permute-start(f32[64,512]{1,0:T(8,128)S(1)} %shard_map.55), channel_id=1, source_target_pairs={{4,6},{5,7},{12,14},{13,15},{20,22},{21,23},{28,30},{29,31}} | collective-permute-start | bytes 393224 | tf_op jit(solution)/shard_map/ppermute | solution.py:359
  23.2 0.7 collective-permute-start.10
  24.0 0.7 collective-permute-start.11
  24.7 27.6 %collective-permute-start.12 = (f32[64,512]{1,0:T(8,128)S(1)}, f32[64,512]{1,0:T(8,128)S(1)}, u32[]{:S(2)}, u32[]{:S(2)}) collective-permute-start(f32[64,512]{1,0:T(8,128)S(1)} %shard_map.61), channel_id=1, source_target_pairs={{2,0},{3,1},{10,8},{11,9},{18,16},{19,17},{26,24},{27,25}} | collective-permute-start | bytes 393224 | tf_op jit(solution)/shard_map/ppermute | solution.py:359
  53.2 4.3 %collective-permute-start.13 = (f32[128,128]{1,0:T(8,128)S(1)}, f32[128,128]{1,0:T(8,128)S(1)}, u32[]{:S(2)}, u32[]{:S(2)}) collective-permute-start(f32[128,128]{1,0:T(8,128)S(1)} %get-tuple-element.59), channel_id=1, source_target_pairs={{0,8},{8,0},{16,24},{24,16},{1,9},{9,1},{17,25},{25,17},{2,10},{10... | collective-permute-start | bytes 196616 | tf_op jit(solution)/shard_map/ppermute | solution.py:362
  54.8 4.3 %collective-permute-start.14 = (f32[128,128]{1,0:T(8,128)S(1)}, f32[128,128]{1,0:T(8,128)S(1)}, u32[]{:S(2)}, u32[]{:S(2)}) collective-permute-start(f32[128,128]{1,0:T(8,128)S(1)} %get-tuple-element.60), channel_id=1, source_target_pairs={{0,16},{8,24},{16,0},{24,8},{1,17},{9,25},{17,1},{25,9},{2,18},{10... | collective-permute-start | bytes 196616 | tf_op jit(solution)/shard_map/ppermute | solution.py:362
  56.3 5.2 %collective-permute-start.15 = (f32[128,128]{1,0:T(8,128)S(1)}, f32[128,128]{1,0:T(8,128)S(1)}, u32[]{:S(2)}, u32[]{:S(2)}) collective-permute-start(f32[128,128]{1,0:T(8,128)S(1)} %get-tuple-element.61), channel_id=1, source_target_pairs={{0,24},{8,16},{16,8},{24,0},{1,25},{9,17},{17,9},{25,1},{2,26},{10... | collective-permute-start | bytes 196616 | tf_op jit(solution)/shard_map/ppermute | solution.py:362
  61.5 1.4 %collective-permute-start.16 = (f32[256,128]{1,0:T(8,128)S(1)}, f32[256,128]{1,0:T(8,128)S(1)}, u32[]{:S(2)}, u32[]{:S(2)}) collective-permute-start(f32[256,128]{1,0:T(8,128)S(1)} %shard_map.63.mine), channel_id=1, source_target_pairs={{0,1},{1,0},{2,3},{3,2},{4,5},{5,4},{6,7},{7,6},{8,9},{9,8},{10,11... | collective-permute-start | bytes 393224 | tf_op jit(solution)/shard_map/ppermute | solution.py:356
  63.3 4.0 %collective-permute-start.17 = (f32[32,256]{1,0:T(8,128)S(1)}, f32[32,256]{1,0:T(8,128)S(1)}, u32[]{:S(2)}, u32[]{:S(2)}) collective-permute-start(f32[32,256]{1,0:T(8,128)S(1)} %get-tuple-element.65), channel_id=1, source_target_pairs={{0,8},{8,0},{16,24},{24,16},{1,9},{9,1},{17,25},{25,17},{2,10},{10... | collective-permute-start | bytes 98312 | tf_op jit(solution)/shard_map/ppermute | solution.py:362
  63.8 4.3 %collective-permute-start.18 = (f32[32,256]{1,0:T(8,128)S(1)}, f32[32,256]{1,0:T(8,128)S(1)}, u32[]{:S(2)}, u32[]{:S(2)}) collective-permute-start(f32[32,256]{1,0:T(8,128)S(1)} %get-tuple-element.66), channel_id=1, source_target_pairs={{0,16},{8,24},{16,0},{24,8},{1,17},{9,25},{17,1},{25,9},{2,18},{10... | collective-permute-start | bytes 98312 | tf_op jit(solution)/shard_map/ppermute | solution.py:362
  64.3 4.8 %collective-permute-start.19 = (f32[32,256]{1,0:T(8,128)S(1)}, f32[32,256]{1,0:T(8,128)S(1)}, u32[]{:S(2)}, u32[]{:S(2)}) collective-permute-start(f32[32,256]{1,0:T(8,128)S(1)} %get-tuple-element.67), channel_id=1, source_target_pairs={{0,24},{8,16},{16,8},{24,0},{1,25},{9,17},{17,9},{25,1},{2,26},{10... | collective-permute-start | bytes 98312 | tf_op jit(solution)/shard_map/ppermute | solution.py:362
  69.2 5.8 %collective-permute-start.22 = (f32[32,256]{1,0:T(8,128)S(1)}, f32[32,256]{1,0:T(8,128)S(1)}, u32[]{:S(2)}, u32[]{:S(2)}) collective-permute-start(f32[32,256]{1,0:T(8,128)S(1)} %add_add_fusion), channel_id=1, source_target_pairs={{0,6},{1,7},{2,4},{3,5},{4,2},{5,3},{6,0},{7,1},{8,14},{9,15},{10,... | collective-permute-start | bytes 98312 | tf_op jit(solution)/shard_map/ppermute | solution.py:365
  69.2 5.7 %collective-permute-start.21 = (f32[32,256]{1,0:T(8,128)S(1)}, f32[32,256]{1,0:T(8,128)S(1)}, u32[]{:S(2)}, u32[]{:S(2)}) collective-permute-start(f32[32,256]{1,0:T(8,128)S(1)} %add_add_fusion), channel_id=1, source_target_pairs={{0,4},{1,5},{2,6},{3,7},{4,0},{5,1},{6,2},{7,3},{8,12},{9,13},{10,... | collective-permute-start | bytes 98312 | tf_op jit(solution)/shard_map/ppermute | solution.py:365
  70.3 5.2 %collective-permute-start.20 = (f32[32,256]{1,0:T(8,128)S(1)}, f32[32,256]{1,0:T(8,128)S(1)}, u32[]{:S(2)}, u32[]{:S(2)}) collective-permute-start(f32[32,256]{1,0:T(8,128)S(1)} %add_add_fusion), channel_id=1, source_target_pairs={{0,2},{1,3},{2,0},{3,1},{4,6},{5,7},{6,4},{7,5},{8,10},{9,11},{10,... | collective-permute-start | bytes 98312 | tf_op jit(solution)/shard_map/ppermute | solution.py:365
  75.5 4.9 %collective-permute-start.25 = (f32[32,256]{1,0:T(8,128)S(1)}, f32[32,256]{1,0:T(8,128)S(1)}, u32[]{:S(2)}, u32[]{:S(2)}) collective-permute-start(f32[32,256]{1,0:T(8,128)S(1)} %add_multiply_fusion.refs_0_), channel_id=1, source_target_pairs={{0,24},{8,16},{16,8},{24,0},{1,25},{9,17},{17,9},{25,1},{2,26},{10... | collective-permute-start | bytes 98312 | tf_op jit(solution)/shard_map/ppermute | solution.py:362
  78.1 3.9 %collective-permute-start.24 = (f32[32,256]{1,0:T(8,128)S(1)}, f32[32,256]{1,0:T(8,128)S(1)}, u32[]{:S(2)}, u32[]{:S(2)}) collective-permute-start(f32[32,256]{1,0:T(8,128)S(1)} %add_multiply_fusion.refs_0_), channel_id=1, source_target_pairs={{0,16},{8,24},{16,0},{24,8},{1,17},{9,25},{17,1},{25,9},{2,18},{10... | collective-permute-start | bytes 98312 | tf_op jit(solution)/shard_map/ppermute | solution.py:362
  78.6 3.9 %collective-permute-start.23 = (f32[32,256]{1,0:T(8,128)S(1)}, f32[32,256]{1,0:T(8,128)S(1)}, u32[]{:S(2)}, u32[]{:S(2)}) collective-permute-start(f32[32,256]{1,0:T(8,128)S(1)} %add_multiply_fusion.refs_0_), channel_id=1, source_target_pairs={{0,8},{8,0},{16,24},{24,16},{1,9},{9,1},{17,25},{25,17},{2,10},{10... | collective-permute-start | bytes 98312 | tf_op jit(solution)/shard_map/ppermute | solution.py:362
  82.5 1.4 %collective-permute-start.26 = (f32[128,256]{1,0:T(8,128)S(1)}, f32[128,256]{1,0:T(8,128)S(1)}, u32[]{:S(2)}, u32[]{:S(2)}) collective-permute-start(f32[128,256]{1,0:T(8,128)S(1)} %shard_map.65.mine), channel_id=1, source_target_pairs={{0,1},{1,0},{2,3},{3,2},{4,5},{5,4},{6,7},{7,6},{8,9},{9,8},{10,11... | collective-permute-start | bytes 393224 | tf_op jit(solution)/shard_map/ppermute | solution.py:356
